TPU v7x, 256 devices: a whole 4x4x8 slice. The times are simulated.
256 devices in a mesh: root: 8 (over z), virt: 16 (over x, y), occ: 2 (over core).
Axes of the slice: x: 4, y: 4, z: 8, core: 2. Of those that a mesh axis runs over, the one named last changes fastest.
Arguments:
- trial_singles: bfloat16 [16, 96], P('root'), may hold values from -6 to 6
- trial_doubles: bfloat16 [16, 480, 9216], P('root', 'virt', 'occ'), may hold values from -6 to 6
- occ_fock: bfloat16 [96, 96], replicated, may hold values from -0.625 to 0.625
- virt_fock: bfloat16 [480, 480], replicated, may hold values from -0.25 to 0.25
- w_ovoo: bfloat16 [96, 480, 9216], P('occ', 'virt', 'root'), may hold values from -0.625 to 0.625
- w_ooov: bfloat16 [96, 480, 9216], P('occ', 'virt', 'root'), may hold values from -0.0029296875 to 0.0029296875
- converged: int32 [16], replicated, may hold values from 0 to 1, as said below
Outputs:
- sigma_doubles: bfloat16 [16, 480, 9216], P('root', 'virt', 'occ')
- sigma_singles: float32 [16, 96], P('root')
- subspace: float32 [16, 16], P('root')
Inputs may be any that keep to these rules, and one draw needn't show every extreme that they name: `converged`: exactly 8 roots are active (0). In every draw at least one aligned block of 2 roots has all its roots active; other blocks may have none.
All inputs are finite; a program needn't handle non-finite values.
Results may differ from a plain program's by a relative error of at most 0.0044.
Values may be sent and summed in bfloat16 or wider, within the bound.
No kernel may reach another device: no remote copies, remote signals or barrier semaphores. Data moves between devices by JAX's collectives and lax.ppermute only.
A program may use at most 256 MiB of HBM per device.

v0:
```python
import math

import jax
import jax.numpy as jnp
from jax import lax
from jax.experimental import pallas as pl
from jax.experimental.pallas import tpu as pltpu
from jax.sharding import Mesh
from jax.sharding import PartitionSpec as P


VIRT = ("virt_0", "virt_1")
ROOT_OCC = ("root", "occ")
BF = jnp.bfloat16
F32 = jnp.float32
HI = lax.Precision.HIGHEST

Z = 8
NV = 16
OC = 96
VL = 30
VP = 32
BLK = 1152
HALF = 4608
COLS = 640
KH = 48
SPARE = 30
GRP = 384

VMEM = pltpu.VMEM
SMEM = pltpu.SMEM


def iota(shape, dim):
    return lax.broadcasted_iota(jnp.int32, shape, dim)


def dot(a, b, precision=None):
    return jnp.dot(a, b, preferred_element_type=F32, precision=precision)


def dot_nt(a, b, precision=None):
    return lax.dot_general(
        a, b, (((1,), (1,)), ((), ())), preferred_element_type=F32, precision=precision
    )


def call(kernel, outs, places, scratch=(), limit=12, flops=1 << 24):
    return pl.pallas_call(
        kernel,
        out_shape=outs,
        in_specs=[pl.BlockSpec(memory_space=p) for p in places],
        out_specs=jax.tree.map(lambda _: pl.BlockSpec(memory_space=VMEM), outs),
        scratch_shapes=scratch,
        compiler_params=pltpu.CompilerParams(vmem_limit_bytes=limit << 20),
        cost_estimate=pl.CostEstimate(flops=flops, bytes_accessed=1 << 20, transcendentals=0),
    )


def exchange(x, axes):
    return lax.all_to_all(x, axes, split_axis=0, concat_axis=0, tiled=True)


def shape(dims, dtype):
    return jax.ShapeDtypeStruct(dims, dtype)


def other_core(x):
    return lax.ppermute(x, "occ", [(0, 1), (1, 0)])


def z_pairs(t):
    return [
        (2 * r + o, 2 * (4 * o + (r + t) % 4) + r // 4) for r in range(Z) for o in range(2)
    ]


def z_steps(x, back=False):
    out = []
    for t in range(4):
        pairs = [(b, a) if back else (a, b) for a, b in z_pairs(t)]
        out.append(lax.ppermute(x[t], ROOT_OCC, pairs))
    return out


def slot_of(q, me):
    return lax.rem(q - me + Z, 4)


def tiles_of(first, count):
    tile, out = 0, []
    while tile < count:
        g, off = divmod(first + tile, 5)
        n = min(5 - off, count - tile)
        out.append((g, 128 * off, 128 * (off + n), 128 * tile, 128 * (tile + n)))
        tile += n
    return out


def prep_kernel(ids, doubles, t1, zb, xb):
    me = ids[0]
    place = (iota((OC, 128), 0) == iota((OC, 128), 1)).astype(F32)
    wide = dot(t1[...].astype(F32), place, HI)
    first = iota((2, 128), 0) == 0
    xb[:, VL:VP, :] = jnp.zeros((NV, VP - VL, COLS), BF)
    xb[14, 0:VL, 256:COLS] = jnp.zeros((VL, COLS - 256), BF)
    xb[15, 0:VL, :] = jnp.zeros((VL, COLS), BF)
    for p in range(2):
        tail = jnp.where(first, jnp.broadcast_to(wide[p : p + 1, :], (2, 128)), 0.0).astype(BF)
        for q in range(4):
            slot = slot_of(q, me)
            zb[slot, p, 0:VL, :] = doubles[p, :, BLK * q : BLK * (q + 1)]
            zb[slot, p, VL:VP, 0:128] = tail
            zb[slot, p, VL:VP, 128:BLK] = jnp.zeros((VP - VL, BLK - 128), BF)
        for g, a, b, lo, hi in tiles_of(36 * p, 36):
            xb[g, 0:VL, a:b] = doubles[p, :, lo:hi]


def oo_kernel(ids, zb, zo, fock, oo, left, own, stack, rolled):
    me, core = ids[0], ids[1]
    f = fock[...]
    rows, depth, half = 96, 768, 192
    e3 = (lax.rem(iota((GRP, OC), 0), OC) == iota((GRP, OC), 1)).astype(BF)
    same = iota((GRP, GRP), 0) // OC == iota((GRP, GRP), 1) // OC
    bd = dot_nt(dot(e3, f).astype(BF), e3)
    bd = jnp.where(same, bd, 0.0).astype(BF)
    col = iota((OC, depth), 1)
    shift = col // half
    group = lax.rem(col, half) // 8
    group = jnp.where(group < 12, group + 12 * core, group - 12 * core)
    diag = lax.rem(iota((rows, depth), 0), 8) == lax.rem(iota((rows, depth), 1), 8)
    for i in range(4):
        mine = 4 * (12 * core + iota((rows, OC), 0) // 8) + i
        ef = dot_nt((iota((rows, OC), 1) == mine).astype(BF), f).astype(BF)
        e2 = (iota((OC, depth), 0) == 4 * group + ((i - shift) & 3)).astype(BF)
        left[rows * i : rows * (i + 1), :] = jnp.where(diag, dot(ef, e2), 0.0).astype(BF)
    lane = iota((rows, 256), 1) & 127
    for p in range(2):
        for b in range(2):
            for h, ref in enumerate((zb, zo)):
                for q in range(4):
                    slot = slot_of(q, me)
                    for u in range(3):
                        at = 12 * h + 3 * q + u
                        piece = ref[
                            slot, p, 16 * b : 16 * (b + 1), GRP * u : GRP * (u + 1)
                        ].astype(F32)
                        stack[0, 8 * at : 8 * (at + 1), :] = piece[0:8, :]
                        stack[1, 8 * at : 8 * (at + 1), :] = piece[8:16, :]
            for c in range(2):
                wide = stack[c]
                rolled[c, 0:half, :] = wide.astype(BF)
                own[rows * c : rows * (c + 1), :] = wide[0:rows, :].astype(BF)
                for s in range(1, 4):
                    rolled[c, half * s : half * (s + 1), :] = pltpu.roll(wide, OC * s, 1).astype(BF)
            second = dot(own[...], bd)
            for tile in range(3):
                lo, hi = 128 * tile, 128 * (tile + 1)
                rhs = jnp.concatenate([rolled[0, :, lo:hi], rolled[1, :, lo:hi]], axis=1)
                y = dot(left[rows * tile : rows * (tile + 2), :], rhs)
                v = jnp.where(lane < 96 - 32 * tile, y[0:rows, :], y[rows:, :])
                for c in range(2):
                    w = v[:, 128 * c : 128 * (c + 1)] + second[rows * c : rows * (c + 1), lo:hi]
                    for g in range(12):
                        q, u = divmod(g, 3)
                        oo[
                            q,
                            p,
                            16 * b + 8 * c : 16 * b + 8 * (c + 1),
                            GRP * u + lo : GRP * u + hi,
                        ] = w[8 * g : 8 * (g + 1), :]


def mm_kernel(fock, x, out):
    n = NV * VP
    count = NV * VL
    row = iota((n, count), 0)
    pick = (VL * (row // VP) + lax.rem(row, VP) == iota((n, count), 1)) & (lax.rem(row, VP) < VL)
    pick = pick.astype(BF)
    padded = dot_nt(dot(pick, fock[...]).astype(BF), pick).astype(BF)
    y = dot(padded, x[...].reshape(n, COLS)).astype(BF)
    out[...] = y.reshape(NV, VP, COLS)


def gather_kernel(ids, after, *refs):
    me, out = ids[0], refs[4]
    del after
    for t in range(4):
        at = 2 * lax.rem(me - t + Z, 4)
        for p in range(2):
            out[at + p] = refs[t][p]


def singles_of(ref):
    mask = iota((16, 128), 0) == SPARE - 16
    rows = []
    for r in range(Z):
        x = ref[r, 16:32, 0:128].astype(F32)
        rows.append(jnp.sum(jnp.where(mask, x, 0.0), axis=0, keepdims=True))
    return jnp.concatenate(rows, axis=0)


def outer_kernel(ids, mine, theirs, w, out_mine, out_theirs):
    core, k = ids[1], 16 * KH
    t1 = jnp.concatenate([singles_of(mine), singles_of(theirs)], axis=0).astype(BF)
    e1 = (iota((256, 16), 0) // 16 == iota((256, 16), 1)).astype(BF)
    e2 = (iota((128, k), 0) == KH * core + lax.rem(iota((128, k), 1), KH)).astype(BF)
    spread = dot(dot(e1, t1).astype(BF), e2)
    diag = lax.rem(iota((256, k), 0), 16) == iota((256, k), 1) // KH
    spread = jnp.where(diag, -spread, 0.0).astype(BF)
    for b, (first, last) in enumerate(((0, 16), (16, VL))):
        depth = (last - first) * KH
        y = dot(spread[:, 0:depth], w[first:last].reshape(depth, BLK)).astype(BF)
        for n in range(Z):
            out_mine[n, 16 * b : 16 * (b + 1), :] = y[16 * n : 16 * (n + 1), :]
            out_theirs[n, 16 * b : 16 * (b + 1), :] = y[128 + 16 * n : 128 + 16 * (n + 1), :]


def add_kernel(ids, a, b, out):
    me = ids[0]
    for t in range(4):
        at = 2 * lax.rem(me - t + Z, 4)
        for p in range(2):
            out[t, p] = (a[at + p].astype(F32) + b[at + p].astype(F32)).astype(BF)


def coupling_kernel(mine, theirs, w, out, t):
    for b in range(2):
        for j, ref in enumerate((mine, theirs)):
            t[b, 128 * j : 128 * (j + 1), :] = ref[:, 16 * b : 16 * (b + 1), :].reshape(128, BLK)
    total = jnp.zeros((KH, 256), F32)
    for b, (first, last) in enumerate(((0, 16), (16, VL))):
        depth = (last - first) * KH
        g = dot_nt(w[first:last].reshape(depth, BLK), t[b])
        g = jnp.where(iota(g.shape, 0) // KH == lax.rem(iota(g.shape, 1), 16), g, 0.0)
        total += jnp.sum(g.reshape(last - first, KH, 256), axis=0)
    right = (iota((256, 16), 0) // 16 == iota((256, 16), 1)).astype(F32)
    out[...] = dot(total, right, HI)


def x_kernel(ids, after, vv, oo, x, xb):
    me = ids[0]
    del after
    for p in range(2):
        for q in range(4):
            slot = slot_of(q, me)
            for g, a, b, lo, hi in tiles_of(36 * p + 9 * q, 9):
                v = vv[g, :, a:b].astype(F32) - oo[q, p, :, lo:hi]
                x[q, p, :, lo:hi] = v
                xb[slot, p, :, lo:hi] = v.astype(BF)


def base_kernel(ids, mine, theirs, coupling, rows, t1_out):
    core = ids[1]
    half = (iota((128, KH), 0) == KH * core + iota((128, KH), 1)).astype(F32)
    place_c = (iota((KH, 128), 1) == KH * core + iota((KH, 128), 0)).astype(F32)
    near, far = 8 * core, 8 - 8 * core
    n16 = iota((16, 128), 0)
    place = (iota((16, 128), 1) == OC + jnp.where(n16 < 8, n16 + near, n16 - near)).astype(F32)
    c = coupling[...]
    t1 = [singles_of(mine), singles_of(theirs)]
    row = lax.dot_general(
        c, place_c, (((0,), (0,)), ((), ())), preferred_element_type=F32, precision=HI
    )
    both = jnp.concatenate(t1, axis=0)
    row += dot(dot(dot(both, half, HI), c, HI) * (-0.5 / math.sqrt(OC)), place, HI)
    rows[...] = row
    for j, start in enumerate((near, far)):
        t1_out[pl.ds(pl.multiple_of(start, 8), 8), :] = t1[j]


def s_kernel(ids, mine, theirs, ov, rows, *refs):
    me, core = ids[0], ids[1]
    out, y = refs[4], refs[5]
    for t in range(4):
        at = 2 * lax.rem(me - t + Z, 4)
        for p in range(2):
            y[at + p] = (refs[t][p].astype(F32) + ov[t, p].astype(F32)).astype(BF)
    y[:, VL:VP, :] = jnp.zeros((Z, VP - VL, BLK), BF)
    near, far = 8 * core, 8 - 8 * core
    n8 = iota((128, 128), 0) // 16
    place = (iota((128, 128), 1) == OC + near + n8).astype(F32)
    place = place * (1.0 / math.sqrt(OC * OC * NV * VL))
    same = lax.rem(iota((128, 128), 0), 16) == lax.rem(iota((128, 128), 1), 16)
    left = (iota((Z, 128), 1) // 16 == iota((Z, 128), 0)).astype(F32)
    for j, ref in enumerate((mine, theirs)):
        g = jnp.zeros((128, 128), F32)
        for b in range(2):
            lhs = ref[:, 16 * b : 16 * (b + 1), :].reshape(128, BLK)
            g += dot_nt(lhs, y[:, 16 * b : 16 * (b + 1), :].reshape(128, BLK))
        row = rows[8 * j : 8 * (j + 1), :] + dot(dot(left, jnp.where(same, g, 0.0), HI), place, HI)
        start = (near if j == 0 else far) // 2
        for i in range(4):
            pair = jnp.concatenate([row[2 * i : 2 * i + 1, :], row[2 * i + 1 : 2 * i + 2, :]], axis=1)
            out[start + i] = jnp.broadcast_to(pair[None], (2, 1, 256))


def sum_kernel(x, out):
    out[...] = jnp.broadcast_to(jnp.sum(x[...], axis=0, keepdims=True), out.shape)


def final_kernel(ids, conv, active, x, t1, fock, singles, subspace):
    me = ids[0]
    summed = jnp.sum(x[...], axis=0)
    total = jnp.concatenate([summed[:, 0:128], summed[:, 128:256]], axis=0)
    mine = jnp.concatenate([t1[pl.ds(2 * me, 1), :], t1[pl.ds(2 * me + 1, 1), :]], axis=0)[:, 0:OC]
    all_fock = dot(t1[:, 0:OC].astype(BF), fock[...])
    own_fock = dot(mine.astype(BF), fock[...])
    a0 = (1 - conv[2 * me]).astype(F32)
    a1 = (1 - conv[2 * me + 1]).astype(F32)
    own_active = jnp.where(iota((2, OC), 0) == 0, a0, a1)
    singles[...] = own_active * (-own_fock - 0.5 * total[:, 0:OC])
    part = total[:, OC : OC + 2 * Z] - dot_nt(mine, all_fock, HI) * (1.0 / math.sqrt(OC))
    subspace[...] = part * active[...]


def out_kernel(ids, conv, x, *refs):
    me = ids[0]
    out, ov = refs[4], refs[5]
    for t in range(4):
        ov[lax.rem(me + t, 4)] = refs[t][...]
    for p in range(2):
        a = (1 - conv[2 * me + p]).astype(F32)
        for q in range(4):
            v = a * (x[q, p, 0:VL, :] + ov[q, p, 0:VL, :].astype(F32))
            out[p, :, BLK * q : BLK * (q + 1)] = v.astype(BF)


def local(trial_singles, trial_doubles, occ_fock, virt_fock, w_ovoo, w_ooov, converged):
    ids = jnp.stack([lax.axis_index("root"), lax.axis_index("occ")]).astype(jnp.int32)
    active = (1 - converged).astype(F32)[None, :]
    chunks = (4, 2, VP, BLK)
    roots = (Z, VP, BLK)
    w_ovoo = jnp.transpose(w_ovoo, (1, 0, 2))
    w_ooov = jnp.transpose(w_ooov, (1, 0, 2))

    zb, xb = call(
        prep_kernel, (shape(chunks, BF), shape((NV, VP, COLS), BF)), [SMEM, VMEM, VMEM]
    )(ids, trial_doubles, trial_singles)

    gathered = exchange(xb, VIRT)
    blocks = z_steps(zb)
    oo = call(
        oo_kernel,
        shape(chunks, F32),
        [SMEM, VMEM, VMEM, VMEM],
        [
            VMEM((384, 768), BF),
            VMEM((192, GRP), BF),
            VMEM((2, 192, GRP), F32),
            VMEM((2, 768, GRP), BF),
        ],
        flops=2 << 30,
    )(ids, zb, other_core(zb), occ_fock)
    product = call(
        mm_kernel, shape((NV, VP, COLS), BF), [VMEM, VMEM], flops=1 << 29
    )(virt_fock, gathered)
    vv = exchange(product, VIRT)

    mine = call(gather_kernel, shape(roots, BF), [SMEM, pl.ANY] + [VMEM] * 4)(ids, product, *blocks)
    theirs = other_core(mine)
    outer_mine, outer_theirs = call(
        outer_kernel, (shape(roots, BF), shape(roots, BF)), [SMEM, VMEM, VMEM, VMEM], flops=1 << 30
    )(ids, mine, theirs, w_ovoo)
    ov = call(add_kernel, shape(chunks, BF), [SMEM, VMEM, VMEM])(
        ids, outer_mine, other_core(outer_theirs)
    )
    ov_owned = z_steps(ov, back=True)
    coupling = call(
        coupling_kernel,
        shape((KH, 16), F32),
        [VMEM, VMEM, VMEM],
        [VMEM((2, 256, BLK), BF)],
        flops=1 << 30,
    )(mine, theirs, w_ooov)

    x, xr = call(
        x_kernel, (shape(chunks, F32), shape(chunks, BF)), [SMEM, pl.ANY, VMEM, VMEM]
    )(ids, coupling, vv, oo)
    x_blocks = z_steps(xr)
    rows, t1 = call(
        base_kernel, (shape((16, 128), F32), shape((16, 128), F32)), [SMEM, VMEM, VMEM, VMEM]
    )(ids, mine, theirs, coupling)
    message = call(
        s_kernel, shape((Z, 2, 1, 256), F32), [SMEM] + [VMEM] * 8, [VMEM(roots, BF)]
    )(ids, mine, theirs, ov, rows, *x_blocks)
    arrived = exchange(message.reshape(16, 1, 256), ROOT_OCC)
    copies = call(sum_kernel, shape((NV, 1, 256), F32), [VMEM])(arrived)
    arrived = exchange(copies, VIRT)
    sigma_singles, subspace = call(
        final_kernel,
        (shape((2, OC), F32), shape((2, 2 * Z), F32)),
        [SMEM, SMEM, VMEM, VMEM, VMEM, VMEM],
    )(ids, converged, active, arrived, t1, occ_fock)

    sigma_doubles = call(
        out_kernel, shape((2, VL, HALF), BF), [SMEM, SMEM] + [VMEM] * 5, [VMEM(chunks, BF)]
    )(ids, converged, x, *ov_owned)
    return (sigma_doubles, sigma_singles, subspace)


def solution(mesh):
    torus = Mesh(
        mesh.devices.reshape(mesh.shape["root"], 4, 4, mesh.shape["occ"]),
        ("root", "virt_0", "virt_1", "occ"),
    )
    return jax.shard_map(
        local,
        mesh=torus,
        in_specs=(
            P("root", None),
            P("root", VIRT, "occ"),
            P(),
            P(),
            P("occ", VIRT, "root"),
            P("occ", VIRT, "root"),
            P(),
        ),
        out_specs=(P("root", VIRT, "occ"), P("root", None), P("root", None)),
        check_vma=False,
    )
```

profile of v0, /device:TPU:1, one launch (start us, length us, event | category | flops | bytes accessed | tf_op | source)
XLA Modules:
  0.0 116.2 jit_solution(7566639026054165373)
XLA Ops:
  0.6 1.2 %copy.10.doubles = bf16[2,30,4608]{2,1,0:T(8,128)(2,1)S(1)} copy(bf16[2,30,4608]{2,0,1:T(2,128)(2,1)} %param.8) | data formatting | bytes 1105920 | tf_op args[1]
  2.5 1.5 %shard_map.94 = (bf16[4,2,32,1152]{3,2,1,0:T(8,128)(2,1)S(1)}, bf16[16,32,640]{2,1,0:T(8,128)(2,1)}) custom-call(s32[2]{0:T(128)S(1)} %pad_add_fusion.ids, bf16[2,30,4608]{2,1,0:T(8,128)(2,1)S(1)} %copy.10.doubles, bf16[2,96]{1,0:T(2,128)(2,1)S(1)} %copy-done.6), custom_call_target="tpu_custom_call" | custom-call | flops 16777216 | bytes 1048576 | tf_op jit(solution)/shard_map/pallas_call | solution.py:337
  4.1 7.6 %all-to-all-start = ((bf16[16,32,640]{2,1,0:T(8,128)(2,1)}), bf16[16,32,640]{2,1,0:T(8,128)(2,1)S(1)}, u32[]{:S(2)}, u32[]{:S(2)}) async-start(bf16[16,32,640]{2,1,0:T(8,128)(2,1)} %get-tuple-element.13), calls=%async_computation | async-start | bytes 1310720 | tf_op jit(solution)/shard_map/all_to_all | solution.py:61
  11.7 1.0 collective-permute-start.5
  13.4 8.7 %collective-permute-start = (bf16[2,32,1152]{2,1,0:T(8,128)(2,1)}, bf16[2,32,1152]{2,1,0:T(8,128)(2,1)S(1)}, u32[]{:S(2)}, u32[]{:S(2)}) collective-permute-start(bf16[2,32,1152]{2,1,0:T(8,128)(2,1)} %get-tuple-element.37), channel_id=1, source_target_pairs={{0,0},{1,128},{32,32},{33,160},{64,64},{65,192},{96,96},{97,224},{... | collective-permute-start | bytes 442376 | tf_op jit(solution)/shard_map/ppermute | solution.py:82
  22.2 4.3 %collective-permute-start.2 = (bf16[2,32,1152]{2,1,0:T(8,128)(2,1)S(1)}, bf16[2,32,1152]{2,1,0:T(8,128)(2,1)S(1)}, u32[]{:S(2)}, u32[]{:S(2)}) collective-permute-start(bf16[2,32,1152]{2,1,0:T(8,128)(2,1)S(1)} %get-tuple-element.35), channel_id=1, source_target_pairs={{0,64},{1,192},{32,96},{33,224},{64,0},{65,128},{96,32},{97,160},{... | collective-permute-start | bytes 442376 | tf_op jit(solution)/shard_map/ppermute | solution.py:82
  26.5 2.1 %shard_map.95.after = bf16[16,32,640]{2,1,0:T(8,128)(2,1)} custom-call(bf16[480,480]{1,0:T(8,128)(2,1)S(1)} %copy-done.8, bf16[16,32,640]{2,1,0:T(8,128)(2,1)S(1)} %all-to-all-done.x), custom_call_target="tpu_custom_call" | custom-call | flops 536870912 | bytes 1048576 | tf_op jit(solution)/shard_map/pallas_call | solution.py:355
  28.7 2.1 %collective-permute-done.1.refs_1_ = bf16[2,32,1152]{2,1,0:T(8,128)(2,1)S(1)} collective-permute-done((bf16[2,32,1152]{2,1,0:T(8,128)(2,1)S(1)}, bf16[2,32,1152]{2,1,0:T(8,128)(2,1)S(1)}, u32[]{:S(2)}, u32[]{:S(2)}) %collective-permute-start.1) | collective-permute-done | bytes 147488 | tf_op jit(solution)/shard_map/ppermute | solution.py:82
  30.8 3.5 %collective-permute-done.2.refs_2_ = bf16[2,32,1152]{2,1,0:T(8,128)(2,1)S(1)} collective-permute-done((bf16[2,32,1152]{2,1,0:T(8,128)(2,1)S(1)}, bf16[2,32,1152]{2,1,0:T(8,128)(2,1)S(1)}, u32[]{:S(2)}, u32[]{:S(2)}) %collective-permute-start.2) | collective-permute-done | bytes 147488 | tf_op jit(solution)/shard_map/ppermute | solution.py:82
  34.3 1.6 %collective-permute-done.3.refs_3_ = bf16[2,32,1152]{2,1,0:T(8,128)(2,1)S(1)} collective-permute-done((bf16[2,32,1152]{2,1,0:T(8,128)(2,1)S(1)}, bf16[2,32,1152]{2,1,0:T(8,128)(2,1)S(1)}, u32[]{:S(2)}, u32[]{:S(2)}) %collective-permute-start.3) | collective-permute-done | bytes 147488 | tf_op jit(solution)/shard_map/ppermute | solution.py:82
  36.5 6.9 %all-to-all-start.1 = ((bf16[16,32,640]{2,1,0:T(8,128)(2,1)}), bf16[16,32,640]{2,1,0:T(8,128)(2,1)S(1)}, u32[]{:S(2)}, u32[]{:S(2)}) async-start(bf16[16,32,640]{2,1,0:T(8,128)(2,1)} %shard_map.95.after), calls=%async_computation.1 | async-start | bytes 1310720 | tf_op jit(solution)/shard_map/all_to_all | solution.py:61
  43.5 3.2 %shard_map.98.oo = f32[4,2,32,1152]{3,2,1,0:T(8,128)S(1)} custom-call(s32[2]{0:T(128)S(1)} %pad_add_fusion.ids, bf16[4,2,32,1152]{3,2,1,0:T(8,128)(2,1)S(1)} %get-tuple-element.14.zb, bf16[4,2,32,1152]{3,2,1,0:T(8,128)(2,1)S(1)} %collective-permute-done.5.zo, bf16[96,96]{1,0:T(8,128)(2,1)S(1)} %copy-done.9), custom_call_target="tpu_custom_call" | custom-call | flops 2147483648 | bytes 1048576 | tf_op jit(solution)/shard_map/pallas_call | solution.py:343
  47.8 2.8 %shard_map.100 = (bf16[8,32,1152]{2,1,0:T(8,128)(2,1)S(1)}, bf16[8,32,1152]{2,1,0:T(8,128)(2,1)}) custom-call(s32[2]{0:T(128)S(1)} %pad_add_fusion.ids, bf16[8,32,1152]{2,1,0:T(8,128)(2,1)S(1)} %shard_map.96.mine, bf16[8,32,1152]{2,1,0:T(8,128)(2,1)S(1)} %collective-permute-done.4.theirs, bf16[30,48,1152]{2,1,0:T(8,128)(2,1)S(1)} %bitcast.31), custom_call_target="tpu_custom_call" | custom-call | flops 1073741824 | bytes 1048576 | tf_op jit(solution)/shard_map/pallas_call | solution.py:362
  52.2 1.5 %shard_map.97.after.coupling = f32[48,16]{1,0:T(8,128)S(1)} custom-call(bf16[8,32,1152]{2,1,0:T(8,128)(2,1)S(1)} %shard_map.96.mine, bf16[8,32,1152]{2,1,0:T(8,128)(2,1)S(1)} %collective-permute-done.4.theirs, bf16[30,48,1152]{2,1,0:T(8,128)(2,1)S(1)} %bitcast.32), custom_call_target="tpu_custom_call" | custom-call | flops 1073741824 | bytes 1048576 | tf_op jit(solution)/shard_map/pallas_call | solution.py:369
  53.6 1.3 %all-to-all-done.1.vv = bf16[16,32,640]{2,1,0:T(8,128)(2,1)S(1)} async-done(((bf16[16,32,640]{2,1,0:T(8,128)(2,1)}), bf16[16,32,640]{2,1,0:T(8,128)(2,1)S(1)}, u32[]{:S(2)}, u32[]{:S(2)}) %all-to-all-start.1) | async-done | bytes 655392 | tf_op jit(solution)/shard_map/all_to_all | solution.py:61
  55.0 1.3 %copy-done.3 = f32[4,2,32,1152]{3,2,1,0:T(8,128)S(1)} copy-done((f32[4,2,32,1152]{3,2,1,0:T(8,128)S(1)}, f32[4,2,32,1152]{3,2,1,0:T(8,128)}, u32[]{:S(2)}) %copy-start.3) | copy-done | bytes 1179672
  57.0 7.2 %collective-permute-start.11 = (bf16[2,32,1152]{2,1,0:T(8,128)(2,1)S(1)}, bf16[2,32,1152]{2,1,0:T(8,128)(2,1)S(1)}, u32[]{:S(2)}, u32[]{:S(2)}) collective-permute-start(bf16[2,32,1152]{2,1,0:T(8,128)(2,1)S(1)} %get-tuple-element.29), channel_id=1, source_target_pairs={{0,0},{1,128},{32,32},{33,160},{64,64},{65,192},{96,96},{97,224},{... | collective-permute-start | bytes 442376 | tf_op jit(solution)/shard_map/ppermute | solution.py:82
  64.8 6.1 %collective-permute-start.13 = (bf16[2,32,1152]{2,1,0:T(8,128)(2,1)S(1)}, bf16[2,32,1152]{2,1,0:T(8,128)(2,1)S(1)}, u32[]{:S(2)}, u32[]{:S(2)}) collective-permute-start(bf16[2,32,1152]{2,1,0:T(8,128)(2,1)S(1)} %get-tuple-element.27), channel_id=1, source_target_pairs={{0,64},{1,192},{32,96},{33,224},{64,0},{65,128},{96,32},{97,160},{... | collective-permute-start | bytes 442376 | tf_op jit(solution)/shard_map/ppermute | solution.py:82
  70.8 1.1 shard_map.103
  71.9 1.1 copy-done.5
  73.0 1.2 %shard_map.101.ov = bf16[4,2,32,1152]{3,2,1,0:T(8,128)(2,1)S(1)} custom-call(s32[2]{0:T(128)S(1)} %pad_add_fusion.ids, bf16[8,32,1152]{2,1,0:T(8,128)(2,1)S(1)} %copy-done.5, bf16[8,32,1152]{2,1,0:T(8,128)(2,1)} %collective-permute-done.6.b), custom_call_target="tpu_custom_call" | custom-call | flops 16777216 | bytes 1048576 | tf_op jit(solution)/shard_map/pallas_call | solution.py:365
  74.3 3.6 %collective-permute-done.13.refs_2_ = bf16[2,32,1152]{2,1,0:T(8,128)(2,1)S(1)} collective-permute-done((bf16[2,32,1152]{2,1,0:T(8,128)(2,1)S(1)}, bf16[2,32,1152]{2,1,0:T(8,128)(2,1)S(1)}, u32[]{:S(2)}, u32[]{:S(2)}) %collective-permute-start.13) | collective-permute-done | bytes 147488 | tf_op jit(solution)/shard_map/ppermute | solution.py:82
  77.9 1.6 %collective-permute-done.14.refs_3_ = bf16[2,32,1152]{2,1,0:T(8,128)(2,1)S(1)} collective-permute-done((bf16[2,32,1152]{2,1,0:T(8,128)(2,1)S(1)}, bf16[2,32,1152]{2,1,0:T(8,128)(2,1)S(1)}, u32[]{:S(2)}, u32[]{:S(2)}) %collective-permute-start.14) | collective-permute-done | bytes 147488 | tf_op jit(solution)/shard_map/ppermute | solution.py:82
  79.5 2.7 %shard_map.104 = f32[8,2,1,256]{3,2,1,0:T(1,128)} custom-call(s32[2]{0:T(128)S(1)} %pad_add_fusion.ids, bf16[8,32,1152]{2,1,0:T(8,128)(2,1)S(1)} %shard_map.96.mine, bf16[8,32,1152]{2,1,0:T(8,128)(2,1)S(1)} %collective-permute-done.4.theirs, bf16[4,2,32,1152]{3,2,1,0:T(8,128)(2,1)S(1)} %shard_map.101.ov, f32[16,128]{1,0:T(8,128)S(1)} %get-tuple-element.18.rows, ...), custom_call_target="tpu_custom_call" | custom-call | flops 16777216 | bytes 1048576 | tf_op jit(solution)/shard_map/pallas_call | solution.py:384
  82.2 6.9 %all-to-all-start.2 = ((f32[16,1,256]{2,1,0:T(1,128)}), f32[16,1,256]{2,1,0:T(1,128)S(1)}, u32[]{:S(2)}, u32[]{:S(2)}) async-start(f32[16,1,256]{2,1,0:T(1,128)} %bitcast.17), calls=%async_computation.2 | async-start | bytes 32768 | tf_op jit(solution)/shard_map/all_to_all | solution.py:61
  89.1 7.5 %collective-permute-start.7 = (bf16[2,32,1152]{2,1,0:T(8,128)(2,1)S(1)}, bf16[2,32,1152]{2,1,0:T(8,128)(2,1)S(1)}, u32[]{:S(2)}, u32[]{:S(2)}) collective-permute-start(bf16[2,32,1152]{2,1,0:T(8,128)(2,1)S(1)} %get-tuple-element.33), channel_id=1, source_target_pairs={{0,0},{128,1},{32,32},{160,33},{64,64},{192,65},{96,96},{224,97},{... | collective-permute-start | bytes 442376 | tf_op jit(solution)/shard_map/ppermute | solution.py:82
  96.9 3.6 %collective-permute-start.9 = (bf16[2,32,1152]{2,1,0:T(8,128)(2,1)S(1)}, bf16[2,32,1152]{2,1,0:T(8,128)(2,1)S(1)}, u32[]{:S(2)}, u32[]{:S(2)}) collective-permute-start(bf16[2,32,1152]{2,1,0:T(8,128)(2,1)S(1)} %get-tuple-element.31), channel_id=1, source_target_pairs={{64,0},{192,1},{96,32},{224,33},{0,64},{128,65},{32,96},{160,97},{... | collective-permute-start | bytes 442376 | tf_op jit(solution)/shard_map/ppermute | solution.py:82
  100.5 1.2 %collective-permute-start.10 = (bf16[2,32,1152]{2,1,0:T(8,128)(2,1)S(1)}, bf16[2,32,1152]{2,1,0:T(8,128)(2,1)S(1)}, u32[]{:S(2)}, u32[]{:S(2)}) collective-permute-start(bf16[2,32,1152]{2,1,0:T(8,128)(2,1)S(1)} %get-tuple-element.30), channel_id=1, source_target_pairs={{96,0},{224,1},{0,32},{128,33},{32,64},{160,65},{64,96},{192,97},{... | collective-permute-start | bytes 442376 | tf_op jit(solution)/shard_map/ppermute | solution.py:82
  102.3 3.8 %all-to-all-start.3 = ((f32[16,1,256]{2,1,0:T(1,128)}), f32[16,1,256]{2,1,0:T(1,128)S(1)}, u32[]{:S(2)}, u32[]{:S(2)}) async-start(f32[16,1,256]{2,1,0:T(1,128)} %shard_map.105), calls=%async_computation.3 | async-start | bytes 32768 | tf_op jit(solution)/shard_map/all_to_all | solution.py:61
  106.1 6.4 %all-to-all-done.3.x = f32[16,1,256]{2,1,0:T(1,128)S(1)} async-done(((f32[16,1,256]{2,1,0:T(1,128)}), f32[16,1,256]{2,1,0:T(1,128)S(1)}, u32[]{:S(2)}, u32[]{:S(2)}) %all-to-all-start.3) | async-done | bytes 16416 | tf_op jit(solution)/shard_map/all_to_all | solution.py:61
  112.6 1.5 %shard_map.106 = (f32[2,96]{1,0:T(2,128)}, f32[2,16]{1,0:T(2,128)}) custom-call(s32[2]{0:T(128)S(1)} %pad_add_fusion.ids, s32[16]{0:T(128)S(1)} %copy-done.7, f32[1,16]{1,0:T(1,128)S(1)} %convert_bitcast_fusion.active, f32[16,1,256]{2,1,0:T(1,128)S(1)} %all-to-all-done.3.x, f32[16,128]{1,0:T(8,128)S(1)} %get-tuple-element.20.t1, bf16[96,96]{1,0:T(8,128)(2,1)S(1)} %copy-done.9), custom_call_target="tpu_custom_call" | custom-call | flops 16777216 | bytes 1048576 | tf_op jit(solution)/shard_map/pallas_call | solution.py:390
  114.8 1.4 %copy.11 = bf16[2,30,4608]{2,0,1:T(2,128)(2,1)} copy(bf16[2,30,4608]{2,1,0:T(8,128)(2,1)S(1)} %shard_map.102) | data formatting | bytes 1105920
  (46 shorter events, 8.0 us)
Async XLA Ops:
  0.6 25.9 %copy-start.8 = (bf16[480,480]{1,0:T(8,128)(2,1)S(1)}, bf16[480,480]{1,0:T(8,128)(2,1)}, u32[]{:S(2)}) copy-start(bf16[480,480]{1,0:T(8,128)(2,1)} %fock.3) | copy-start | bytes 1382404
  1.9 0.7 copy-start.6
  4.1 22.5 %all-to-all-start = ((bf16[16,32,640]{2,1,0:T(8,128)(2,1)}), bf16[16,32,640]{2,1,0:T(8,128)(2,1)S(1)}, u32[]{:S(2)}, u32[]{:S(2)}) async-start(bf16[16,32,640]{2,1,0:T(8,128)(2,1)} %get-tuple-element.13), calls=%async_computation | async-start | bytes 1310720 | tf_op jit(solution)/shard_map/all_to_all | solution.py:61
  11.7 31.9 %copy-start.9 = (bf16[96,96]{1,0:T(8,128)(2,1)S(1)}, bf16[96,96]{1,0:T(8,128)(2,1)}, u32[]{:S(2)}) copy-start(bf16[96,96]{1,0:T(8,128)(2,1)} %fock.5) | copy-start | bytes 55300
  11.7 31.8 %collective-permute-start.5 = (bf16[4,2,32,1152]{3,2,1,0:T(8,128)(2,1)S(1)}, bf16[4,2,32,1152]{3,2,1,0:T(8,128)(2,1)S(1)}, u32[]{:S(2)}, u32[]{:S(2)}) collective-permute-start(bf16[4,2,32,1152]{3,2,1,0:T(8,128)(2,1)S(1)} %get-tuple-element.14.zb), channel_id=1, source_target_pairs={{0,1},{1,0},{2,3},{3,2},{4,5},{5,4},{6,7},{7,6},{8,9},{9,8},{10,11... | collective-permute-start | bytes 1769480 | tf_op jit(solution)/shard_map/ppermute | solution.py:69
  13.4 15.2 %collective-permute-start = (bf16[2,32,1152]{2,1,0:T(8,128)(2,1)}, bf16[2,32,1152]{2,1,0:T(8,128)(2,1)S(1)}, u32[]{:S(2)}, u32[]{:S(2)}) collective-permute-start(bf16[2,32,1152]{2,1,0:T(8,128)(2,1)} %get-tuple-element.37), channel_id=1, source_target_pairs={{0,0},{1,128},{32,32},{33,160},{64,64},{65,192},{96,96},{97,224},{... | collective-permute-start | bytes 442376 | tf_op jit(solution)/shard_map/ppermute | solution.py:82
  22.1 8.6 %collective-permute-start.1 = (bf16[2,32,1152]{2,1,0:T(8,128)(2,1)S(1)}, bf16[2,32,1152]{2,1,0:T(8,128)(2,1)S(1)}, u32[]{:S(2)}, u32[]{:S(2)}) collective-permute-start(bf16[2,32,1152]{2,1,0:T(8,128)(2,1)S(1)} %get-tuple-element.36), channel_id=1, source_target_pairs={{0,32},{1,160},{32,64},{33,192},{64,96},{65,224},{96,0},{97,128},{... | collective-permute-start | bytes 442376 | tf_op jit(solution)/shard_map/ppermute | solution.py:82
  22.2 12.0 %collective-permute-start.2 = (bf16[2,32,1152]{2,1,0:T(8,128)(2,1)S(1)}, bf16[2,32,1152]{2,1,0:T(8,128)(2,1)S(1)}, u32[]{:S(2)}, u32[]{:S(2)}) collective-permute-start(bf16[2,32,1152]{2,1,0:T(8,128)(2,1)S(1)} %get-tuple-element.35), channel_id=1, source_target_pairs={{0,64},{1,192},{32,96},{33,224},{64,0},{65,128},{96,32},{97,160},{... | collective-permute-start | bytes 442376 | tf_op jit(solution)/shard_map/ppermute | solution.py:82
  26.5 9.3 %collective-permute-start.3 = (bf16[2,32,1152]{2,1,0:T(8,128)(2,1)S(1)}, bf16[2,32,1152]{2,1,0:T(8,128)(2,1)S(1)}, u32[]{:S(2)}, u32[]{:S(2)}) collective-permute-start(bf16[2,32,1152]{2,1,0:T(8,128)(2,1)S(1)} %get-tuple-element.34), channel_id=1, source_target_pairs={{0,96},{1,224},{32,0},{33,128},{64,32},{65,160},{96,64},{97,192},{... | collective-permute-start | bytes 442376 | tf_op jit(solution)/shard_map/ppermute | solution.py:82
  36.4 11.3 %collective-permute-start.4 = (bf16[8,32,1152]{2,1,0:T(8,128)(2,1)S(1)}, bf16[8,32,1152]{2,1,0:T(8,128)(2,1)S(1)}, u32[]{:S(2)}, u32[]{:S(2)}) collective-permute-start(bf16[8,32,1152]{2,1,0:T(8,128)(2,1)S(1)} %shard_map.96.mine), channel_id=1, source_target_pairs={{0,1},{1,0},{2,3},{3,2},{4,5},{5,4},{6,7},{7,6},{8,9},{9,8},{10,11... | collective-permute-start | bytes 1769480 | tf_op jit(solution)/shard_map/ppermute | solution.py:69
  36.5 18.4 %all-to-all-start.1 = ((bf16[16,32,640]{2,1,0:T(8,128)(2,1)}), bf16[16,32,640]{2,1,0:T(8,128)(2,1)S(1)}, u32[]{:S(2)}, u32[]{:S(2)}) async-start(bf16[16,32,640]{2,1,0:T(8,128)(2,1)} %shard_map.95.after), calls=%async_computation.1 | async-start | bytes 1310720 | tf_op jit(solution)/shard_map/all_to_all | solution.py:61
  43.5 4.3 %copy-start = (bf16[48,30,1152]{2,0,1:T(8,128)(2,1)S(1)}, bf16[48,30,1152]{2,0,1:T(8,128)(2,1)}, u32[]{:S(2)}) copy-start(bf16[48,30,1152]{2,0,1:T(8,128)(2,1)} %param.11) | copy-start | bytes 9953284
  46.7 1.0 copy-start.2
  47.8 4.4 %copy-start.1 = (bf16[48,30,1152]{2,0,1:T(8,128)(2,1)S(1)}, bf16[48,30,1152]{2,0,1:T(8,128)(2,1)}, u32[]{:S(2)}) copy-start(bf16[48,30,1152]{2,0,1:T(8,128)(2,1)} %param.12) | copy-start | bytes 9953284
  50.6 0.8 copy-start.4
  51.4 20.5 %collective-permute-start.6 = (bf16[8,32,1152]{2,1,0:T(8,128)(2,1)}, bf16[8,32,1152]{2,1,0:T(8,128)(2,1)}, u32[]{:S(2)}, u32[]{:S(2)}) collective-permute-start(bf16[8,32,1152]{2,1,0:T(8,128)(2,1)} %get-tuple-element.17), channel_id=1, source_target_pairs={{0,1},{1,0},{2,3},{3,2},{4,5},{5,4},{6,7},{7,6},{8,9},{9,8},{10,11... | collective-permute-start | bytes 1769480 | tf_op jit(solution)/shard_map/ppermute | solution.py:69
  55.0 1.3 %copy-start.3 = (f32[4,2,32,1152]{3,2,1,0:T(8,128)S(1)}, f32[4,2,32,1152]{3,2,1,0:T(8,128)}, u32[]{:S(2)}) copy-start(f32[4,2,32,1152]{3,2,1,0:T(8,128)} %copy-done.2) | copy-start | bytes 3538948
  57.0 17.2 %collective-permute-start.11 = (bf16[2,32,1152]{2,1,0:T(8,128)(2,1)S(1)}, bf16[2,32,1152]{2,1,0:T(8,128)(2,1)S(1)}, u32[]{:S(2)}, u32[]{:S(2)}) collective-permute-start(bf16[2,32,1152]{2,1,0:T(8,128)(2,1)S(1)} %get-tuple-element.29), channel_id=1, source_target_pairs={{0,0},{1,128},{32,32},{33,160},{64,64},{65,192},{96,96},{97,224},{... | collective-permute-start | bytes 442376 | tf_op jit(solution)/shard_map/ppermute | solution.py:82
  64.2 10.0 %collective-permute-start.12 = (bf16[2,32,1152]{2,1,0:T(8,128)(2,1)S(1)}, bf16[2,32,1152]{2,1,0:T(8,128)(2,1)S(1)}, u32[]{:S(2)}, u32[]{:S(2)}) collective-permute-start(bf16[2,32,1152]{2,1,0:T(8,128)(2,1)S(1)} %get-tuple-element.28), channel_id=1, source_target_pairs={{0,32},{1,160},{32,64},{33,192},{64,96},{65,224},{96,0},{97,128},{... | collective-permute-start | bytes 442376 | tf_op jit(solution)/shard_map/ppermute | solution.py:82
  64.8 13.1 %collective-permute-start.13 = (bf16[2,32,1152]{2,1,0:T(8,128)(2,1)S(1)}, bf16[2,32,1152]{2,1,0:T(8,128)(2,1)S(1)}, u32[]{:S(2)}, u32[]{:S(2)}) collective-permute-start(bf16[2,32,1152]{2,1,0:T(8,128)(2,1)S(1)} %get-tuple-element.27), channel_id=1, source_target_pairs={{0,64},{1,192},{32,96},{33,224},{64,0},{65,128},{96,32},{97,160},{... | collective-permute-start | bytes 442376 | tf_op jit(solution)/shard_map/ppermute | solution.py:82
  70.8 35.3 %copy-start.7 = (s32[16]{0:T(128)S(1)}, s32[16]{0:T(128)}, u32[]{:S(2)}) copy-start(s32[16]{0:T(128)} %conv.3) | copy-start | bytes 196
  70.8 8.7 %collective-permute-start.14 = (bf16[2,32,1152]{2,1,0:T(8,128)(2,1)S(1)}, bf16[2,32,1152]{2,1,0:T(8,128)(2,1)S(1)}, u32[]{:S(2)}, u32[]{:S(2)}) collective-permute-start(bf16[2,32,1152]{2,1,0:T(8,128)(2,1)S(1)} %get-tuple-element.26), channel_id=1, source_target_pairs={{0,96},{1,224},{32,0},{33,128},{64,32},{65,160},{96,64},{97,192},{... | collective-permute-start | bytes 442376 | tf_op jit(solution)/shard_map/ppermute | solution.py:82
  71.9 1.1 copy-start.5
  82.2 19.5 %all-to-all-start.2 = ((f32[16,1,256]{2,1,0:T(1,128)}), f32[16,1,256]{2,1,0:T(1,128)S(1)}, u32[]{:S(2)}, u32[]{:S(2)}) async-start(f32[16,1,256]{2,1,0:T(1,128)} %bitcast.17), calls=%async_computation.2 | async-start | bytes 32768 | tf_op jit(solution)/shard_map/all_to_all | solution.py:61
  89.1 25.0 %collective-permute-start.7 = (bf16[2,32,1152]{2,1,0:T(8,128)(2,1)S(1)}, bf16[2,32,1152]{2,1,0:T(8,128)(2,1)S(1)}, u32[]{:S(2)}, u32[]{:S(2)}) collective-permute-start(bf16[2,32,1152]{2,1,0:T(8,128)(2,1)S(1)} %get-tuple-element.33), channel_id=1, source_target_pairs={{0,0},{128,1},{32,32},{160,33},{64,64},{192,65},{96,96},{224,97},{... | collective-permute-start | bytes 442376 | tf_op jit(solution)/shard_map/ppermute | solution.py:82
  96.6 17.5 %collective-permute-start.8 = (bf16[2,32,1152]{2,1,0:T(8,128)(2,1)S(1)}, bf16[2,32,1152]{2,1,0:T(8,128)(2,1)S(1)}, u32[]{:S(2)}, u32[]{:S(2)}) collective-permute-start(bf16[2,32,1152]{2,1,0:T(8,128)(2,1)S(1)} %get-tuple-element.32), channel_id=1, source_target_pairs={{32,0},{160,1},{64,32},{192,33},{96,64},{224,65},{0,96},{128,97},{... | collective-permute-start | bytes 442376 | tf_op jit(solution)/shard_map/ppermute | solution.py:82
  96.9 17.2 %collective-permute-start.9 = (bf16[2,32,1152]{2,1,0:T(8,128)(2,1)S(1)}, bf16[2,32,1152]{2,1,0:T(8,128)(2,1)S(1)}, u32[]{:S(2)}, u32[]{:S(2)}) collective-permute-start(bf16[2,32,1152]{2,1,0:T(8,128)(2,1)S(1)} %get-tuple-element.31), channel_id=1, source_target_pairs={{64,0},{192,1},{96,32},{224,33},{0,64},{128,65},{32,96},{160,97},{... | collective-permute-start | bytes 442376 | tf_op jit(solution)/shard_map/ppermute | solution.py:82
  100.5 13.6 %collective-permute-start.10 = (bf16[2,32,1152]{2,1,0:T(8,128)(2,1)S(1)}, bf16[2,32,1152]{2,1,0:T(8,128)(2,1)S(1)}, u32[]{:S(2)}, u32[]{:S(2)}) collective-permute-start(bf16[2,32,1152]{2,1,0:T(8,128)(2,1)S(1)} %get-tuple-element.30), channel_id=1, source_target_pairs={{96,0},{224,1},{0,32},{128,33},{32,64},{160,65},{64,96},{192,97},{... | collective-permute-start | bytes 442376 | tf_op jit(solution)/shard_map/ppermute | solution.py:82
  102.3 10.3 %all-to-all-start.3 = ((f32[16,1,256]{2,1,0:T(1,128)}), f32[16,1,256]{2,1,0:T(1,128)S(1)}, u32[]{:S(2)}, u32[]{:S(2)}) async-start(f32[16,1,256]{2,1,0:T(1,128)} %shard_map.105), calls=%async_computation.3 | async-start | bytes 32768 | tf_op jit(solution)/shard_map/all_to_all | solution.py:61
where the time goes:
time: 117 us; the launch traced here: 116 us
  starting transfers between devices  66.6 us (57%)
  Pallas kernels  20.2 us (17%)
  waiting for transfers between devices  20.2 us (17%)
  local copies, waits for them, and re-layouts  8.23 us (7%)
    ppermute x12, starting transfers between devices, z_steps(): out.append(lax.ppermute(x[t], ROOT_OCC, pairs))  39.5 us
    all_to_all x4, starting transfers between devices, exchange(): return lax.all_to_all(x, axes, split_axis=0, concat_axis=0, tiled=True)  25.2 us
    ppermute x12, waiting for transfers between devices, z_steps(): out.append(lax.ppermute(x[t], ROOT_OCC, pairs))  12.4 us
    all_to_all x4, waiting for transfers between devices, exchange(): return lax.all_to_all(x, axes, split_axis=0, concat_axis=0, tiled=True)  7.78 us
    unnamed x22, local copies, waits for them, and re-layouts  7.43 us
    pallas_call x1, Pallas kernels, local(): call(oo_kernel, shape(chunks, F32), [SMEM, VMEM, VMEM, VMEM], [VMEM((384,...  3.17 us
    pallas_call x1, Pallas kernels, local(): call(outer_kernel, (shape(roots, BF), shape(roots, BF)), [SMEM, VMEM, VME...  2.83 us
    pallas_call x1, Pallas kernels, local(): call(s_kernel, shape((Z, 2, 1, 256), F32), [SMEM] + [VMEM] * 8, [VMEM(roo...  2.67 us
  transfers between devices with their start and end apart: 19, of which 7 were waited for; matrix products, arithmetic and copies ran while one was open for 1% of the time, Pallas kernels for 13%

commit v1 on v0

--- a/solution.py
+++ b/solution.py
@@ -25,10 +25,9 @@
 COLS = 640
 KH = 48
 SPARE = 30
-GRP = 384
-
 VMEM = pltpu.VMEM
 SMEM = pltpu.SMEM
+GRP = 384
 
 
 def iota(shape, dim):
@@ -45,12 +44,12 @@
     )
 
 
-def call(kernel, outs, places, scratch=(), limit=12, flops=1 << 24):
+def call(kernel, outs, places, scratch=(), limit=12, flops=1 << 24, out_place=VMEM):
     return pl.pallas_call(
         kernel,
         out_shape=outs,
         in_specs=[pl.BlockSpec(memory_space=p) for p in places],
-        out_specs=jax.tree.map(lambda _: pl.BlockSpec(memory_space=VMEM), outs),
+        out_specs=jax.tree.map(lambda _: pl.BlockSpec(memory_space=out_place), outs),
         scratch_shapes=scratch,
         compiler_params=pltpu.CompilerParams(vmem_limit_bytes=limit << 20),
         cost_estimate=pl.CostEstimate(flops=flops, bytes_accessed=1 << 20, transcendentals=0),
@@ -99,8 +98,7 @@
 
 def prep_kernel(ids, doubles, t1, zb, xb):
     me = ids[0]
-    place = (iota((OC, 128), 0) == iota((OC, 128), 1)).astype(F32)
-    wide = dot(t1[...].astype(F32), place, HI)
+    wide = t1[...].astype(F32)
     first = iota((2, 128), 0) == 0
     xb[:, VL:VP, :] = jnp.zeros((NV, VP - VL, COLS), BF)
     xb[14, 0:VL, 256:COLS] = jnp.zeros((VL, COLS - 256), BF)
@@ -116,59 +114,68 @@
             xb[g, 0:VL, a:b] = doubles[p, :, lo:hi]
 
 
-def oo_kernel(ids, zb, zo, fock, oo, left, own, stack, rolled):
+def oo_kernel(ids, zb, zo, fock, out_own, out_other, left, stack, rolled):
     me, core = ids[0], ids[1]
-    f = fock[...]
     rows, depth, half = 96, 768, 192
-    e3 = (lax.rem(iota((GRP, OC), 0), OC) == iota((GRP, OC), 1)).astype(BF)
-    same = iota((GRP, GRP), 0) // OC == iota((GRP, GRP), 1) // OC
-    bd = dot_nt(dot(e3, f).astype(BF), e3)
-    bd = jnp.where(same, bd, 0.0).astype(BF)
-    col = iota((OC, depth), 1)
-    shift = col // half
-    group = lax.rem(col, half) // 8
-    group = jnp.where(group < 12, group + 12 * core, group - 12 * core)
-    diag = lax.rem(iota((rows, depth), 0), 8) == lax.rem(iota((rows, depth), 1), 8)
-    for i in range(4):
-        mine = 4 * (12 * core + iota((rows, OC), 0) // 8) + i
-        ef = dot_nt((iota((rows, OC), 1) == mine).astype(BF), f).astype(BF)
-        e2 = (iota((OC, depth), 0) == 4 * group + ((i - shift) & 3)).astype(BF)
-        left[rows * i : rows * (i + 1), :] = jnp.where(diag, dot(ef, e2), 0.0).astype(BF)
-    lane = iota((rows, 256), 1) & 127
-    for p in range(2):
-        for b in range(2):
-            for h, ref in enumerate((zb, zo)):
-                for q in range(4):
-                    slot = slot_of(q, me)
-                    for u in range(3):
-                        at = 12 * h + 3 * q + u
-                        piece = ref[
-                            slot, p, 16 * b : 16 * (b + 1), GRP * u : GRP * (u + 1)
-                        ].astype(F32)
-                        stack[0, 8 * at : 8 * (at + 1), :] = piece[0:8, :]
-                        stack[1, 8 * at : 8 * (at + 1), :] = piece[8:16, :]
-            for c in range(2):
-                wide = stack[c]
-                rolled[c, 0:half, :] = wide.astype(BF)
-                own[rows * c : rows * (c + 1), :] = wide[0:rows, :].astype(BF)
-                for s in range(1, 4):
-                    rolled[c, half * s : half * (s + 1), :] = pltpu.roll(wide, OC * s, 1).astype(BF)
-            second = dot(own[...], bd)
-            for tile in range(3):
-                lo, hi = 128 * tile, 128 * (tile + 1)
-                rhs = jnp.concatenate([rolled[0, :, lo:hi], rolled[1, :, lo:hi]], axis=1)
-                y = dot(left[rows * tile : rows * (tile + 2), :], rhs)
-                v = jnp.where(lane < 96 - 32 * tile, y[0:rows, :], y[rows:, :])
+
+    def work():
+        f = fock[...]
+        e3 = (lax.rem(iota((GRP, OC), 0), OC) == iota((GRP, OC), 1)).astype(BF)
+        same = iota((GRP, GRP), 0) // OC == iota((GRP, GRP), 1) // OC
+        bd = dot_nt(dot(e3, f).astype(BF), e3)
+        bd = jnp.where(same, bd, 0.0).astype(BF)
+        col = iota((OC, depth), 1)
+        shift = col // half
+        group = lax.rem(col, half) // 8
+        group = jnp.where(group < 12, group + 12 * core, group - 12 * core)
+        diag = lax.rem(iota((rows, depth), 0), 8) == lax.rem(iota((rows, depth), 1), 8)
+        for i in range(4):
+            e2 = (iota((OC, depth), 0) == 4 * group + ((i - shift) & 3)).astype(BF)
+            for h in range(2):
+                first = 12 * core if h == 0 else 12 - 12 * core
+                at = 4 * (first + iota((rows, OC), 0) // 8) + i
+                ef = dot_nt((iota((rows, OC), 1) == at).astype(BF), f).astype(BF)
+                m = jnp.where(diag, dot(ef, e2), 0.0).astype(BF)
+                left[h, rows * i : rows * (i + 1), :] = m
+        lane = iota((rows, 256), 1) & 127
+        for p in range(2):
+            for b in range(2):
+                for h, ref in enumerate((zb, zo)):
+                    for q in range(4):
+                        slot = slot_of(q, me)
+                        for u in range(3):
+                            at = 8 * (12 * h + 3 * q + u)
+                            piece = ref[
+                                slot, p, 16 * b : 16 * (b + 1), GRP * u : GRP * (u + 1)
+                            ].astype(F32)
+                            stack[0, at : at + 8, :] = piece[0:8, :]
+                            stack[1, at : at + 8, :] = piece[8:16, :]
                 for c in range(2):
-                    w = v[:, 128 * c : 128 * (c + 1)] + second[rows * c : rows * (c + 1), lo:hi]
-                    for g in range(12):
-                        q, u = divmod(g, 3)
-                        oo[
-                            q,
-                            p,
-                            16 * b + 8 * c : 16 * b + 8 * (c + 1),
-                            GRP * u + lo : GRP * u + hi,
-                        ] = w[8 * g : 8 * (g + 1), :]
+                    wide = stack[c]
+                    rolled[c, 0:half, :] = wide.astype(BF)
+                    for s in range(1, 4):
+                        moved = pltpu.roll(wide, OC * s, 1)
+                        rolled[c, half * s : half * (s + 1), :] = moved.astype(BF)
+                second = [dot(rolled[c, 0:half, :], bd) for c in range(2)]
+                for tile in range(3):
+                    lo, hi = 128 * tile, 128 * (tile + 1)
+                    rhs = jnp.concatenate([rolled[0, :, lo:hi], rolled[1, :, lo:hi]], axis=1)
+                    for h, out in enumerate((out_own, out_other)):
+                        y = dot(left[h, rows * tile : rows * (tile + 2), :], rhs)
+                        v = jnp.where(lane < 96 - 32 * tile, y[0:rows, :], y[rows:, :])
+                        w = [
+                            v[:, 128 * c : 128 * (c + 1)]
+                            + second[c][rows * h : rows * (h + 1), lo:hi]
+                            for c in range(2)
+                        ]
+                        for g in range(12):
+                            q, u = divmod(g, 3)
+                            part = [x[8 * g : 8 * (g + 1), :] for x in w]
+                            out[q, p, 16 * b : 16 * (b + 1), GRP * u + lo : GRP * u + hi] = (
+                                jnp.concatenate(part, axis=0).astype(BF)
+                            )
+
+    pl.when(me // 4 == core)(work)
 
 
 def mm_kernel(fock, x, out):
@@ -238,15 +245,25 @@
     out[...] = dot(total, right, HI)
 
 
-def x_kernel(ids, after, vv, oo, x, xb):
+def pick_kernel(ids, oo_own, oo_far, out):
+    near = ids[0] // 4 == ids[1]
+
+    @pl.when(near)
+    def _():
+        out[...] = oo_own[...]
+
+    @pl.when(jnp.logical_not(near))
+    def _():
+        out[...] = oo_far[...]
+
+
+def x_kernel(ids, vv, oo, xb):
     me = ids[0]
-    del after
     for p in range(2):
         for q in range(4):
             slot = slot_of(q, me)
             for g, a, b, lo, hi in tiles_of(36 * p + 9 * q, 9):
-                v = vv[g, :, a:b].astype(F32) - oo[q, p, :, lo:hi]
-                x[q, p, :, lo:hi] = v
+                v = vv[g, :, a:b].astype(F32) - oo[q, p, :, lo:hi].astype(F32)
                 xb[slot, p, :, lo:hi] = v.astype(BF)
 
 
@@ -316,14 +333,13 @@
 
 def out_kernel(ids, conv, x, *refs):
     me = ids[0]
-    out, ov = refs[4], refs[5]
+    out, total = refs[4], refs[5]
     for t in range(4):
-        ov[lax.rem(me + t, 4)] = refs[t][...]
+        total[lax.rem(me + t, 4)] = x[t].astype(F32) + refs[t][...].astype(F32)
     for p in range(2):
         a = (1 - conv[2 * me + p]).astype(F32)
         for q in range(4):
-            v = a * (x[q, p, 0:VL, :] + ov[q, p, 0:VL, :].astype(F32))
-            out[p, :, BLK * q : BLK * (q + 1)] = v.astype(BF)
+            out[p, :, BLK * q : BLK * (q + 1)] = (a * total[q, p, 0:VL, :]).astype(BF)
 
 
 def local(trial_singles, trial_doubles, occ_fock, virt_fock, w_ovoo, w_ooov, converged):
@@ -336,22 +352,26 @@
 
     zb, xb = call(
         prep_kernel, (shape(chunks, BF), shape((NV, VP, COLS), BF)), [SMEM, VMEM, VMEM]
-    )(ids, trial_doubles, trial_singles)
+    )(ids, trial_doubles, jnp.pad(trial_singles, ((0, 0), (0, 128 - OC))))
 
     gathered = exchange(xb, VIRT)
     blocks = z_steps(zb)
-    oo = call(
+    zo = other_core(zb)
+    oo_own, oo_other = call(
         oo_kernel,
-        shape(chunks, F32),
+        (shape(chunks, BF), shape(chunks, BF)),
         [SMEM, VMEM, VMEM, VMEM],
         [
-            VMEM((384, 768), BF),
-            VMEM((192, GRP), BF),
+            VMEM((2, 384, 768), BF),
             VMEM((2, 192, GRP), F32),
             VMEM((2, 768, GRP), BF),
         ],
         flops=2 << 30,
-    )(ids, zb, other_core(zb), occ_fock)
+    )(ids, zb, zo, occ_fock)
+    oo_far = other_core(oo_other)
+    oo = call(pick_kernel, shape(chunks, BF), [SMEM, VMEM, VMEM])(
+        ids, oo_own, oo_far
+    )
     product = call(
         mm_kernel, shape((NV, VP, COLS), BF), [VMEM, VMEM], flops=1 << 29
     )(virt_fock, gathered)
@@ -374,10 +394,8 @@
         flops=1 << 30,
     )(mine, theirs, w_ooov)
 
-    x, xr = call(
-        x_kernel, (shape(chunks, F32), shape(chunks, BF)), [SMEM, pl.ANY, VMEM, VMEM]
-    )(ids, coupling, vv, oo)
-    x_blocks = z_steps(xr)
+    x = call(x_kernel, shape(chunks, BF), [SMEM, VMEM, VMEM])(ids, vv, oo)
+    x_blocks = z_steps(x)
     rows, t1 = call(
         base_kernel, (shape((16, 128), F32), shape((16, 128), F32)), [SMEM, VMEM, VMEM, VMEM]
     )(ids, mine, theirs, coupling)
@@ -394,7 +412,7 @@
     )(ids, converged, active, arrived, t1, occ_fock)
 
     sigma_doubles = call(
-        out_kernel, shape((2, VL, HALF), BF), [SMEM, SMEM] + [VMEM] * 5, [VMEM(chunks, BF)]
+        out_kernel, shape((2, VL, HALF), BF), [SMEM, SMEM] + [VMEM] * 5, [VMEM(chunks, F32)]
     )(ids, converged, x, *ov_owned)
     return (sigma_doubles, sigma_singles, subspace)
 

time: 117 us -> 115 us (0.983)
  waiting for transfers between devices: 20.2 us -> 16.9 us
  local copies, waits for them, and re-layouts: 8.23 us -> 11.5 us
    ppermute x12, waiting for transfers between devices: 12.4 us -> 7.93 us  [z_steps(): out.append(lax.ppermute(x[t], ROOT_OCC, pairs))]
    all_to_all x4, starting transfers between devices: 25.2 us -> 22.3 us  [exchange(): return lax.all_to_all(x, axes, split_axis=0, concat_axis=0, tiled=True)]
    unnamed x22 -> x24, local copies, waits for them, and re-layouts: 7.43 us -> 9.89 us
    ppermute x3 -> x4, starting transfers between devices: 1.9 us -> 4.06 us  [other_core(): return lax.ppermute(x, 'occ', [(0, 1), (1, 0)])]
    pallas_call x2 -> x3, Pallas kernels: 3.87 us -> 2.65 us  [the longest x1 1.37 us: local(): call(oo_kernel, (shape(chunks, BF), shape(chunks, BF)), [SMEM, VMEM, VMEM...]
    all_to_all x4, waiting for transfers between devices: 7.78 us -> 9 us  [exchange(): return lax.all_to_all(x, axes, split_axis=0, concat_axis=0, tiled=True)]
  transfers between devices with their start and end apart: 19 -> 20, of which waited for: 7 -> 6; matrix products, arithmetic and copies ran while one was open for 1% -> 1% of each run, Pallas kernels for 13% -> 12%
where the time goes in v1:
time: 115 us
  starting transfers between devices  66.3 us (58%)
  Pallas kernels  19.1 us (17%)
  waiting for transfers between devices  16.9 us (15%)
  local copies, waits for them, and re-layouts  11.5 us (10%)
    ppermute x12, starting transfers between devices, z_steps(): out.append(lax.ppermute(x[t], ROOT_OCC, pairs))  39.9 us
    all_to_all x4, starting transfers between devices, exchange(): return lax.all_to_all(x, axes, split_axis=0, concat_axis=0, tiled=True)  22.3 us
    unnamed x24, local copies, waits for them, and re-layouts  9.89 us
    all_to_all x4, waiting for transfers between devices, exchange(): return lax.all_to_all(x, axes, split_axis=0, concat_axis=0, tiled=True)  9 us
    ppermute x12, waiting for transfers between devices, z_steps(): out.append(lax.ppermute(x[t], ROOT_OCC, pairs))  7.93 us
    ppermute x4, starting transfers between devices, other_core(): return lax.ppermute(x, 'occ', [(0, 1), (1, 0)])  4.06 us
    pallas_call x1, Pallas kernels, local(): call(outer_kernel, (shape(roots, BF), shape(roots, BF)), [SMEM, VMEM, VME...  2.84 us
    pallas_call x1, Pallas kernels, local(): call(s_kernel, shape((Z, 2, 1, 256), F32), [SMEM] + [VMEM] * 8, [VMEM(roo...  2.68 us
  transfers between devices with their start and end apart: 20, of which 6 were waited for; matrix products, arithmetic and copies ran while one was open for 1% of the time, Pallas kernels for 12%

profile of v1, /device:TPU:1, one launch (start us, length us, event | category | flops | bytes accessed | tf_op | source)
XLA Modules:
  0.0 114.7 jit_solution(1691556366859236309)
XLA Ops:
  0.6 1.1 copy.10.doubles
  2.5 1.5 %shard_map.94 = (bf16[4,2,32,1152]{3,2,1,0:T(8,128)(2,1)S(1)}, bf16[16,32,640]{2,1,0:T(8,128)(2,1)}) custom-call(s32[2]{0:T(128)S(1)} %pad_add_fusion.ids, bf16[2,30,4608]{2,1,0:T(8,128)(2,1)S(1)} %copy.10.doubles, bf16[2,128]{1,0:T(2,128)(2,1)S(1)} %pad.4.t1), custom_call_target="tpu_custom_call" | custom-call | flops 16777216 | bytes 1048576 | tf_op jit(solution)/shard_map/pallas_call | solution.py:353
  4.0 3.2 %collective-permute-start = (bf16[4,2,32,1152]{3,2,1,0:T(8,128)(2,1)S(1)}, bf16[4,2,32,1152]{3,2,1,0:T(8,128)(2,1)S(1)}, u32[]{:S(2)}, u32[]{:S(2)}) collective-permute-start(bf16[4,2,32,1152]{3,2,1,0:T(8,128)(2,1)S(1)} %get-tuple-element.14.zb), channel_id=1, source_target_pairs={{0,1},{1,0},{2,3},{3,2},{4,5},{5,4},{6,7},{7,6},{8,9},{9,8},{10,11... | collective-permute-start | bytes 1769480 | tf_op jit(solution)/shard_map/ppermute | solution.py:68
  7.2 5.0 %all-to-all-start = ((bf16[16,32,640]{2,1,0:T(8,128)(2,1)}), bf16[16,32,640]{2,1,0:T(8,128)(2,1)S(1)}, u32[]{:S(2)}, u32[]{:S(2)}) async-start(bf16[16,32,640]{2,1,0:T(8,128)(2,1)} %get-tuple-element.13), calls=%async_computation | async-start | bytes 1310720 | tf_op jit(solution)/shard_map/all_to_all | solution.py:60
  13.1 9.0 %collective-permute-start.2 = (bf16[2,32,1152]{2,1,0:T(8,128)(2,1)}, bf16[2,32,1152]{2,1,0:T(8,128)(2,1)S(1)}, u32[]{:S(2)}, u32[]{:S(2)}) collective-permute-start(bf16[2,32,1152]{2,1,0:T(8,128)(2,1)} %get-tuple-element.37), channel_id=1, source_target_pairs={{0,0},{1,128},{32,32},{33,160},{64,64},{65,192},{96,96},{97,224},{... | collective-permute-start | bytes 442376 | tf_op jit(solution)/shard_map/ppermute | solution.py:81
  22.2 4.3 %collective-permute-start.4 = (bf16[2,32,1152]{2,1,0:T(8,128)(2,1)}, bf16[2,32,1152]{2,1,0:T(8,128)(2,1)S(1)}, u32[]{:S(2)}, u32[]{:S(2)}) collective-permute-start(bf16[2,32,1152]{2,1,0:T(8,128)(2,1)} %get-tuple-element.35), channel_id=1, source_target_pairs={{0,64},{1,192},{32,96},{33,224},{64,0},{65,128},{96,32},{97,160},{... | collective-permute-start | bytes 442376 | tf_op jit(solution)/shard_map/ppermute | solution.py:81
  26.5 1.4 %shard_map.96 = (bf16[4,2,32,1152]{3,2,1,0:T(8,128)(2,1)S(1)}, bf16[4,2,32,1152]{3,2,1,0:T(8,128)(2,1)}) custom-call(s32[2]{0:T(128)S(1)} %pad_add_fusion.ids, bf16[4,2,32,1152]{3,2,1,0:T(8,128)(2,1)S(1)} %get-tuple-element.14.zb, bf16[4,2,32,1152]{3,2,1,0:T(8,128)(2,1)S(1)} %collective-permute-done.zo, bf16[96,96]{1,0:T(8,128)(2,1)S(1)} %copy-done.10), custom_call_target="tpu_custom_call" | custom-call | flops 2147483648 | bytes 1048576 | tf_op jit(solution)/shard_map/pallas_call | solution.py:360
  28.7 2.1 %shard_map.95.after = bf16[16,32,640]{2,1,0:T(8,128)(2,1)} custom-call(bf16[480,480]{1,0:T(8,128)(2,1)S(1)} %copy-done.9, bf16[16,32,640]{2,1,0:T(8,128)(2,1)S(1)} %all-to-all-done.x), custom_call_target="tpu_custom_call" | custom-call | flops 536870912 | bytes 1048576 | tf_op jit(solution)/shard_map/pallas_call | solution.py:375
  30.8 3.5 %collective-permute-done.4.refs_2_ = bf16[2,32,1152]{2,1,0:T(8,128)(2,1)S(1)} collective-permute-done((bf16[2,32,1152]{2,1,0:T(8,128)(2,1)}, bf16[2,32,1152]{2,1,0:T(8,128)(2,1)S(1)}, u32[]{:S(2)}, u32[]{:S(2)}) %collective-permute-start.4) | collective-permute-done | bytes 147488 | tf_op jit(solution)/shard_map/ppermute | solution.py:81
  34.4 1.5 %collective-permute-done.5.refs_3_ = bf16[2,32,1152]{2,1,0:T(8,128)(2,1)S(1)} collective-permute-done((bf16[2,32,1152]{2,1,0:T(8,128)(2,1)}, bf16[2,32,1152]{2,1,0:T(8,128)(2,1)S(1)}, u32[]{:S(2)}, u32[]{:S(2)}) %collective-permute-start.5) | collective-permute-done | bytes 147488 | tf_op jit(solution)/shard_map/ppermute | solution.py:81
  36.6 6.9 %all-to-all-start.1 = ((bf16[16,32,640]{2,1,0:T(8,128)(2,1)}), bf16[16,32,640]{2,1,0:T(8,128)(2,1)S(1)}, u32[]{:S(2)}, u32[]{:S(2)}) async-start(bf16[16,32,640]{2,1,0:T(8,128)(2,1)} %shard_map.95.after), calls=%async_computation.1 | async-start | bytes 1310720 | tf_op jit(solution)/shard_map/all_to_all | solution.py:60
  44.3 1.1 copy-done.7
  46.0 1.9 %copy-done = bf16[48,30,1152]{2,0,1:T(8,128)(2,1)S(1)} copy-done((bf16[48,30,1152]{2,0,1:T(8,128)(2,1)S(1)}, bf16[48,30,1152]{2,0,1:T(8,128)(2,1)}, u32[]{:S(2)}) %copy-start) | copy-done | bytes 3317784
  48.0 2.8 %shard_map.100 = (bf16[8,32,1152]{2,1,0:T(8,128)(2,1)S(1)}, bf16[8,32,1152]{2,1,0:T(8,128)(2,1)}) custom-call(s32[2]{0:T(128)S(1)} %pad_add_fusion.ids, bf16[8,32,1152]{2,1,0:T(8,128)(2,1)S(1)} %shard_map.99.mine, bf16[8,32,1152]{2,1,0:T(8,128)(2,1)S(1)} %collective-permute-done.6.theirs, bf16[30,48,1152]{2,1,0:T(8,128)(2,1)S(1)} %bitcast.31), custom_call_target="tpu_custom_call" | custom-call | flops 1073741824 | bytes 1048576 | tf_op jit(solution)/shard_map/pallas_call | solution.py:382
  52.4 2.6 %all-to-all-done.1.vv = bf16[16,32,640]{2,1,0:T(8,128)(2,1)S(1)} async-done(((bf16[16,32,640]{2,1,0:T(8,128)(2,1)}), bf16[16,32,640]{2,1,0:T(8,128)(2,1)S(1)}, u32[]{:S(2)}, u32[]{:S(2)}) %all-to-all-start.1) | async-done | bytes 655392 | tf_op jit(solution)/shard_map/all_to_all | solution.py:60
  55.8 7.2 %collective-permute-start.12 = (bf16[2,32,1152]{2,1,0:T(8,128)(2,1)S(1)}, bf16[2,32,1152]{2,1,0:T(8,128)(2,1)S(1)}, u32[]{:S(2)}, u32[]{:S(2)}) collective-permute-start(bf16[2,32,1152]{2,1,0:T(8,128)(2,1)S(1)} %get-tuple-element.29), channel_id=1, source_target_pairs={{0,0},{1,128},{32,32},{33,160},{64,64},{65,192},{96,96},{97,224},{... | collective-permute-start | bytes 442376 | tf_op jit(solution)/shard_map/ppermute | solution.py:81
  63.7 6.1 %collective-permute-start.14 = (bf16[2,32,1152]{2,1,0:T(8,128)(2,1)S(1)}, bf16[2,32,1152]{2,1,0:T(8,128)(2,1)S(1)}, u32[]{:S(2)}, u32[]{:S(2)}) collective-permute-start(bf16[2,32,1152]{2,1,0:T(8,128)(2,1)S(1)} %get-tuple-element.27), channel_id=1, source_target_pairs={{0,64},{1,192},{32,96},{33,224},{64,0},{65,128},{96,32},{97,160},{... | collective-permute-start | bytes 442376 | tf_op jit(solution)/shard_map/ppermute | solution.py:81
  69.8 1.9 %copy-done.1 = bf16[48,30,1152]{2,0,1:T(8,128)(2,1)S(1)} copy-done((bf16[48,30,1152]{2,0,1:T(8,128)(2,1)S(1)}, bf16[48,30,1152]{2,0,1:T(8,128)(2,1)}, u32[]{:S(2)}) %copy-start.1) | copy-done | bytes 3317784
  71.7 1.4 %shard_map.103.coupling = f32[48,16]{1,0:T(8,128)S(1)} custom-call(bf16[8,32,1152]{2,1,0:T(8,128)(2,1)S(1)} %shard_map.99.mine, bf16[8,32,1152]{2,1,0:T(8,128)(2,1)S(1)} %collective-permute-done.6.theirs, bf16[30,48,1152]{2,1,0:T(8,128)(2,1)S(1)} %bitcast.32), custom_call_target="tpu_custom_call" | custom-call | flops 1073741824 | bytes 1048576 | tf_op jit(solution)/shard_map/pallas_call | solution.py:389
  73.2 1.1 shard_map.104
  74.3 1.2 %shard_map.101.ov = bf16[4,2,32,1152]{3,2,1,0:T(8,128)(2,1)S(1)} custom-call(s32[2]{0:T(128)S(1)} %pad_add_fusion.ids, bf16[8,32,1152]{2,1,0:T(8,128)(2,1)S(1)} %copy-done.5, bf16[8,32,1152]{2,1,0:T(8,128)(2,1)} %collective-permute-done.7.b), custom_call_target="tpu_custom_call" | custom-call | flops 16777216 | bytes 1048576 | tf_op jit(solution)/shard_map/pallas_call | solution.py:385
  75.6 1.2 %collective-permute-done.14.refs_2_ = bf16[2,32,1152]{2,1,0:T(8,128)(2,1)S(1)} collective-permute-done((bf16[2,32,1152]{2,1,0:T(8,128)(2,1)S(1)}, bf16[2,32,1152]{2,1,0:T(8,128)(2,1)S(1)}, u32[]{:S(2)}, u32[]{:S(2)}) %collective-permute-start.14) | collective-permute-done | bytes 147488 | tf_op jit(solution)/shard_map/ppermute | solution.py:81
  76.8 1.6 %collective-permute-done.15.refs_3_ = bf16[2,32,1152]{2,1,0:T(8,128)(2,1)S(1)} collective-permute-done((bf16[2,32,1152]{2,1,0:T(8,128)(2,1)S(1)}, bf16[2,32,1152]{2,1,0:T(8,128)(2,1)S(1)}, u32[]{:S(2)}, u32[]{:S(2)}) %collective-permute-start.15) | collective-permute-done | bytes 147488 | tf_op jit(solution)/shard_map/ppermute | solution.py:81
  78.4 2.7 %shard_map.105 = f32[8,2,1,256]{3,2,1,0:T(1,128)} custom-call(s32[2]{0:T(128)S(1)} %pad_add_fusion.ids, bf16[8,32,1152]{2,1,0:T(8,128)(2,1)S(1)} %shard_map.99.mine, bf16[8,32,1152]{2,1,0:T(8,128)(2,1)S(1)} %collective-permute-done.6.theirs, bf16[4,2,32,1152]{3,2,1,0:T(8,128)(2,1)S(1)} %shard_map.101.ov, f32[16,128]{1,0:T(8,128)S(1)} %get-tuple-element.19.rows, ...), custom_call_target="tpu_custom_call" | custom-call | flops 16777216 | bytes 1048576 | tf_op jit(solution)/shard_map/pallas_call | solution.py:402
  81.1 6.8 %all-to-all-start.2 = ((f32[16,1,256]{2,1,0:T(1,128)}), f32[16,1,256]{2,1,0:T(1,128)S(1)}, u32[]{:S(2)}, u32[]{:S(2)}) async-start(f32[16,1,256]{2,1,0:T(1,128)} %bitcast.17), calls=%async_computation.2 | async-start | bytes 32768 | tf_op jit(solution)/shard_map/all_to_all | solution.py:60
  87.9 7.5 %collective-permute-start.8 = (bf16[2,32,1152]{2,1,0:T(8,128)(2,1)S(1)}, bf16[2,32,1152]{2,1,0:T(8,128)(2,1)S(1)}, u32[]{:S(2)}, u32[]{:S(2)}) collective-permute-start(bf16[2,32,1152]{2,1,0:T(8,128)(2,1)S(1)} %get-tuple-element.33), channel_id=1, source_target_pairs={{0,0},{128,1},{32,32},{160,33},{64,64},{192,65},{96,96},{224,97},{... | collective-permute-start | bytes 442376 | tf_op jit(solution)/shard_map/ppermute | solution.py:81
  95.8 3.6 %collective-permute-start.10 = (bf16[2,32,1152]{2,1,0:T(8,128)(2,1)S(1)}, bf16[2,32,1152]{2,1,0:T(8,128)(2,1)S(1)}, u32[]{:S(2)}, u32[]{:S(2)}) collective-permute-start(bf16[2,32,1152]{2,1,0:T(8,128)(2,1)S(1)} %get-tuple-element.31), channel_id=1, source_target_pairs={{64,0},{192,1},{96,32},{224,33},{0,64},{128,65},{32,96},{160,97},{... | collective-permute-start | bytes 442376 | tf_op jit(solution)/shard_map/ppermute | solution.py:81
  99.3 1.2 %collective-permute-start.11 = (bf16[2,32,1152]{2,1,0:T(8,128)(2,1)S(1)}, bf16[2,32,1152]{2,1,0:T(8,128)(2,1)S(1)}, u32[]{:S(2)}, u32[]{:S(2)}) collective-permute-start(bf16[2,32,1152]{2,1,0:T(8,128)(2,1)S(1)} %get-tuple-element.30), channel_id=1, source_target_pairs={{96,0},{224,1},{0,32},{128,33},{32,64},{160,65},{64,96},{192,97},{... | collective-permute-start | bytes 442376 | tf_op jit(solution)/shard_map/ppermute | solution.py:81
  101.1 3.5 %all-to-all-start.3 = ((f32[16,1,256]{2,1,0:T(1,128)}), f32[16,1,256]{2,1,0:T(1,128)S(1)}, u32[]{:S(2)}, u32[]{:S(2)}) async-start(f32[16,1,256]{2,1,0:T(1,128)} %shard_map.106), calls=%async_computation.3 | async-start | bytes 32768 | tf_op jit(solution)/shard_map/all_to_all | solution.py:60
  104.7 6.4 %all-to-all-done.3.x = f32[16,1,256]{2,1,0:T(1,128)S(1)} async-done(((f32[16,1,256]{2,1,0:T(1,128)}), f32[16,1,256]{2,1,0:T(1,128)S(1)}, u32[]{:S(2)}, u32[]{:S(2)}) %all-to-all-start.3) | async-done | bytes 16416 | tf_op jit(solution)/shard_map/all_to_all | solution.py:60
  111.0 1.5 %shard_map.107 = (f32[2,96]{1,0:T(2,128)}, f32[2,16]{1,0:T(2,128)}) custom-call(s32[2]{0:T(128)S(1)} %pad_add_fusion.ids, s32[16]{0:T(128)S(1)} %copy-done.8, f32[1,16]{1,0:T(1,128)S(1)} %convert_bitcast_fusion.active, f32[16,1,256]{2,1,0:T(1,128)S(1)} %all-to-all-done.3.x, f32[16,128]{1,0:T(8,128)S(1)} %get-tuple-element.20.t1, bf16[96,96]{1,0:T(8,128)(2,1)S(1)} %copy-done.10), custom_call_target="tpu_custom_call" | custom-call | flops 16777216 | bytes 1048576 | tf_op jit(solution)/shard_map/pallas_call | solution.py:408
  113.3 1.4 %copy.11 = bf16[2,30,4608]{2,0,1:T(2,128)(2,1)} copy(bf16[2,30,4608]{2,1,0:T(8,128)(2,1)S(1)} %shard_map.102) | data formatting | bytes 1105920
  (52 shorter events, 9.4 us)
Async XLA Ops:
  0.6 25.8 %copy-start.10 = (bf16[96,96]{1,0:T(8,128)(2,1)S(1)}, bf16[96,96]{1,0:T(8,128)(2,1)}, u32[]{:S(2)}) copy-start(bf16[96,96]{1,0:T(8,128)(2,1)} %fock.5) | copy-start | bytes 55300
  4.0 22.5 %collective-permute-start = (bf16[4,2,32,1152]{3,2,1,0:T(8,128)(2,1)S(1)}, bf16[4,2,32,1152]{3,2,1,0:T(8,128)(2,1)S(1)}, u32[]{:S(2)}, u32[]{:S(2)}) collective-permute-start(bf16[4,2,32,1152]{3,2,1,0:T(8,128)(2,1)S(1)} %get-tuple-element.14.zb), channel_id=1, source_target_pairs={{0,1},{1,0},{2,3},{3,2},{4,5},{5,4},{6,7},{7,6},{8,9},{9,8},{10,11... | collective-permute-start | bytes 1769480 | tf_op jit(solution)/shard_map/ppermute | solution.py:68
  7.2 21.5 %all-to-all-start = ((bf16[16,32,640]{2,1,0:T(8,128)(2,1)}), bf16[16,32,640]{2,1,0:T(8,128)(2,1)S(1)}, u32[]{:S(2)}, u32[]{:S(2)}) async-start(bf16[16,32,640]{2,1,0:T(8,128)(2,1)} %get-tuple-element.13), calls=%async_computation | async-start | bytes 1310720 | tf_op jit(solution)/shard_map/all_to_all | solution.py:60
  13.1 17.7 %collective-permute-start.2 = (bf16[2,32,1152]{2,1,0:T(8,128)(2,1)}, bf16[2,32,1152]{2,1,0:T(8,128)(2,1)S(1)}, u32[]{:S(2)}, u32[]{:S(2)}) collective-permute-start(bf16[2,32,1152]{2,1,0:T(8,128)(2,1)} %get-tuple-element.37), channel_id=1, source_target_pairs={{0,0},{1,128},{32,32},{33,160},{64,64},{65,192},{96,96},{97,224},{... | collective-permute-start | bytes 442376 | tf_op jit(solution)/shard_map/ppermute | solution.py:81
  22.1 8.8 %collective-permute-start.3 = (bf16[2,32,1152]{2,1,0:T(8,128)(2,1)}, bf16[2,32,1152]{2,1,0:T(8,128)(2,1)S(1)}, u32[]{:S(2)}, u32[]{:S(2)}) collective-permute-start(bf16[2,32,1152]{2,1,0:T(8,128)(2,1)} %get-tuple-element.36), channel_id=1, source_target_pairs={{0,32},{1,160},{32,64},{33,192},{64,96},{65,224},{96,0},{97,128},{... | collective-permute-start | bytes 442376 | tf_op jit(solution)/shard_map/ppermute | solution.py:81
  22.2 12.2 %collective-permute-start.4 = (bf16[2,32,1152]{2,1,0:T(8,128)(2,1)}, bf16[2,32,1152]{2,1,0:T(8,128)(2,1)S(1)}, u32[]{:S(2)}, u32[]{:S(2)}) collective-permute-start(bf16[2,32,1152]{2,1,0:T(8,128)(2,1)} %get-tuple-element.35), channel_id=1, source_target_pairs={{0,64},{1,192},{32,96},{33,224},{64,0},{65,128},{96,32},{97,160},{... | collective-permute-start | bytes 442376 | tf_op jit(solution)/shard_map/ppermute | solution.py:81
  26.5 2.2 %copy-start.9 = (bf16[480,480]{1,0:T(8,128)(2,1)S(1)}, bf16[480,480]{1,0:T(8,128)(2,1)}, u32[]{:S(2)}) copy-start(bf16[480,480]{1,0:T(8,128)(2,1)} %fock.3) | copy-start | bytes 1382404
  26.5 9.4 %collective-permute-start.5 = (bf16[2,32,1152]{2,1,0:T(8,128)(2,1)}, bf16[2,32,1152]{2,1,0:T(8,128)(2,1)S(1)}, u32[]{:S(2)}, u32[]{:S(2)}) collective-permute-start(bf16[2,32,1152]{2,1,0:T(8,128)(2,1)} %get-tuple-element.34), channel_id=1, source_target_pairs={{0,96},{1,224},{32,0},{33,128},{64,32},{65,160},{96,64},{97,192},{... | collective-permute-start | bytes 442376 | tf_op jit(solution)/shard_map/ppermute | solution.py:81
  27.8 0.8 copy-start.2
  28.7 15.7 %copy-start.3 = (bf16[4,2,32,1152]{3,2,1,0:T(8,128)(2,1)S(1)}, bf16[4,2,32,1152]{3,2,1,0:T(8,128)(2,1)}, u32[]{:S(2)}) copy-start(bf16[4,2,32,1152]{3,2,1,0:T(8,128)(2,1)} %copy-done.2) | copy-start | bytes 1769476
  28.7 14.8 %collective-permute-start.1 = (bf16[4,2,32,1152]{3,2,1,0:T(8,128)(2,1)}, bf16[4,2,32,1152]{3,2,1,0:T(8,128)(2,1)S(1)}, u32[]{:S(2)}, u32[]{:S(2)}) collective-permute-start(bf16[4,2,32,1152]{3,2,1,0:T(8,128)(2,1)} %get-tuple-element.16), channel_id=1, source_target_pairs={{0,1},{1,0},{2,3},{3,2},{4,5},{5,4},{6,7},{7,6},{8,9},{9,8},{10,11... | collective-permute-start | bytes 1769480 | tf_op jit(solution)/shard_map/ppermute | solution.py:68
  36.5 9.5 %collective-permute-start.6 = (bf16[8,32,1152]{2,1,0:T(8,128)(2,1)S(1)}, bf16[8,32,1152]{2,1,0:T(8,128)(2,1)S(1)}, u32[]{:S(2)}, u32[]{:S(2)}) collective-permute-start(bf16[8,32,1152]{2,1,0:T(8,128)(2,1)S(1)} %shard_map.99.mine), channel_id=1, source_target_pairs={{0,1},{1,0},{2,3},{3,2},{4,5},{5,4},{6,7},{7,6},{8,9},{9,8},{10,11... | collective-permute-start | bytes 1769480 | tf_op jit(solution)/shard_map/ppermute | solution.py:68
  36.6 18.4 %all-to-all-start.1 = ((bf16[16,32,640]{2,1,0:T(8,128)(2,1)}), bf16[16,32,640]{2,1,0:T(8,128)(2,1)S(1)}, u32[]{:S(2)}, u32[]{:S(2)}) async-start(bf16[16,32,640]{2,1,0:T(8,128)(2,1)} %shard_map.95.after), calls=%async_computation.1 | async-start | bytes 1310720 | tf_op jit(solution)/shard_map/all_to_all | solution.py:60
  43.5 0.8 copy-start.6
  44.3 1.1 copy-start.7
  46.0 1.9 %copy-start = (bf16[48,30,1152]{2,0,1:T(8,128)(2,1)S(1)}, bf16[48,30,1152]{2,0,1:T(8,128)(2,1)}, u32[]{:S(2)}) copy-start(bf16[48,30,1152]{2,0,1:T(8,128)(2,1)} %param.11) | copy-start | bytes 9953284
  50.8 0.8 copy-start.4
  51.6 22.7 %collective-permute-start.7 = (bf16[8,32,1152]{2,1,0:T(8,128)(2,1)}, bf16[8,32,1152]{2,1,0:T(8,128)(2,1)}, u32[]{:S(2)}, u32[]{:S(2)}) collective-permute-start(bf16[8,32,1152]{2,1,0:T(8,128)(2,1)} %get-tuple-element.18), channel_id=1, source_target_pairs={{0,1},{1,0},{2,3},{3,2},{4,5},{5,4},{6,7},{7,6},{8,9},{9,8},{10,11... | collective-permute-start | bytes 1769480 | tf_op jit(solution)/shard_map/ppermute | solution.py:68
  55.7 18.6 %copy-start.5 = (bf16[8,32,1152]{2,1,0:T(8,128)(2,1)S(1)}, bf16[8,32,1152]{2,1,0:T(8,128)(2,1)}, u32[]{:S(2)}) copy-start(bf16[8,32,1152]{2,1,0:T(8,128)(2,1)} %copy-done.4) | copy-start | bytes 1769476
  55.8 19.8 %collective-permute-start.12 = (bf16[2,32,1152]{2,1,0:T(8,128)(2,1)S(1)}, bf16[2,32,1152]{2,1,0:T(8,128)(2,1)S(1)}, u32[]{:S(2)}, u32[]{:S(2)}) collective-permute-start(bf16[2,32,1152]{2,1,0:T(8,128)(2,1)S(1)} %get-tuple-element.29), channel_id=1, source_target_pairs={{0,0},{1,128},{32,32},{33,160},{64,64},{65,192},{96,96},{97,224},{... | collective-permute-start | bytes 442376 | tf_op jit(solution)/shard_map/ppermute | solution.py:81
  63.0 12.6 %collective-permute-start.13 = (bf16[2,32,1152]{2,1,0:T(8,128)(2,1)S(1)}, bf16[2,32,1152]{2,1,0:T(8,128)(2,1)S(1)}, u32[]{:S(2)}, u32[]{:S(2)}) collective-permute-start(bf16[2,32,1152]{2,1,0:T(8,128)(2,1)S(1)} %get-tuple-element.28), channel_id=1, source_target_pairs={{0,32},{1,160},{32,64},{33,192},{64,96},{65,224},{96,0},{97,128},{... | collective-permute-start | bytes 442376 | tf_op jit(solution)/shard_map/ppermute | solution.py:81
  63.7 13.1 %collective-permute-start.14 = (bf16[2,32,1152]{2,1,0:T(8,128)(2,1)S(1)}, bf16[2,32,1152]{2,1,0:T(8,128)(2,1)S(1)}, u32[]{:S(2)}, u32[]{:S(2)}) collective-permute-start(bf16[2,32,1152]{2,1,0:T(8,128)(2,1)S(1)} %get-tuple-element.27), channel_id=1, source_target_pairs={{0,64},{1,192},{32,96},{33,224},{64,0},{65,128},{96,32},{97,160},{... | collective-permute-start | bytes 442376 | tf_op jit(solution)/shard_map/ppermute | solution.py:81
  69.8 8.6 %collective-permute-start.15 = (bf16[2,32,1152]{2,1,0:T(8,128)(2,1)S(1)}, bf16[2,32,1152]{2,1,0:T(8,128)(2,1)S(1)}, u32[]{:S(2)}, u32[]{:S(2)}) collective-permute-start(bf16[2,32,1152]{2,1,0:T(8,128)(2,1)S(1)} %get-tuple-element.26), channel_id=1, source_target_pairs={{0,96},{1,224},{32,0},{33,128},{64,32},{65,160},{96,64},{97,192},{... | collective-permute-start | bytes 442376 | tf_op jit(solution)/shard_map/ppermute | solution.py:81
  69.8 1.9 %copy-start.1 = (bf16[48,30,1152]{2,0,1:T(8,128)(2,1)S(1)}, bf16[48,30,1152]{2,0,1:T(8,128)(2,1)}, u32[]{:S(2)}) copy-start(bf16[48,30,1152]{2,0,1:T(8,128)(2,1)} %param.12) | copy-start | bytes 9953284
  73.2 31.5 %copy-start.8 = (s32[16]{0:T(128)S(1)}, s32[16]{0:T(128)}, u32[]{:S(2)}) copy-start(s32[16]{0:T(128)} %conv.3) | copy-start | bytes 196
  81.1 19.4 %all-to-all-start.2 = ((f32[16,1,256]{2,1,0:T(1,128)}), f32[16,1,256]{2,1,0:T(1,128)S(1)}, u32[]{:S(2)}, u32[]{:S(2)}) async-start(f32[16,1,256]{2,1,0:T(1,128)} %bitcast.17), calls=%async_computation.2 | async-start | bytes 32768 | tf_op jit(solution)/shard_map/all_to_all | solution.py:60
  87.9 24.6 %collective-permute-start.8 = (bf16[2,32,1152]{2,1,0:T(8,128)(2,1)S(1)}, bf16[2,32,1152]{2,1,0:T(8,128)(2,1)S(1)}, u32[]{:S(2)}, u32[]{:S(2)}) collective-permute-start(bf16[2,32,1152]{2,1,0:T(8,128)(2,1)S(1)} %get-tuple-element.33), channel_id=1, source_target_pairs={{0,0},{128,1},{32,32},{160,33},{64,64},{192,65},{96,96},{224,97},{... | collective-permute-start | bytes 442376 | tf_op jit(solution)/shard_map/ppermute | solution.py:81
  95.4 17.2 %collective-permute-start.9 = (bf16[2,32,1152]{2,1,0:T(8,128)(2,1)S(1)}, bf16[2,32,1152]{2,1,0:T(8,128)(2,1)S(1)}, u32[]{:S(2)}, u32[]{:S(2)}) collective-permute-start(bf16[2,32,1152]{2,1,0:T(8,128)(2,1)S(1)} %get-tuple-element.32), channel_id=1, source_target_pairs={{32,0},{160,1},{64,32},{192,33},{96,64},{224,65},{0,96},{128,97},{... | collective-permute-start | bytes 442376 | tf_op jit(solution)/shard_map/ppermute | solution.py:81
  95.8 16.8 %collective-permute-start.10 = (bf16[2,32,1152]{2,1,0:T(8,128)(2,1)S(1)}, bf16[2,32,1152]{2,1,0:T(8,128)(2,1)S(1)}, u32[]{:S(2)}, u32[]{:S(2)}) collective-permute-start(bf16[2,32,1152]{2,1,0:T(8,128)(2,1)S(1)} %get-tuple-element.31), channel_id=1, source_target_pairs={{64,0},{192,1},{96,32},{224,33},{0,64},{128,65},{32,96},{160,97},{... | collective-permute-start | bytes 442376 | tf_op jit(solution)/shard_map/ppermute | solution.py:81
  99.3 13.2 %collective-permute-start.11 = (bf16[2,32,1152]{2,1,0:T(8,128)(2,1)S(1)}, bf16[2,32,1152]{2,1,0:T(8,128)(2,1)S(1)}, u32[]{:S(2)}, u32[]{:S(2)}) collective-permute-start(bf16[2,32,1152]{2,1,0:T(8,128)(2,1)S(1)} %get-tuple-element.30), channel_id=1, source_target_pairs={{96,0},{224,1},{0,32},{128,33},{32,64},{160,65},{64,96},{192,97},{... | collective-permute-start | bytes 442376 | tf_op jit(solution)/shard_map/ppermute | solution.py:81
  101.1 9.9 %all-to-all-start.3 = ((f32[16,1,256]{2,1,0:T(1,128)}), f32[16,1,256]{2,1,0:T(1,128)S(1)}, u32[]{:S(2)}, u32[]{:S(2)}) async-start(f32[16,1,256]{2,1,0:T(1,128)} %shard_map.106), calls=%async_computation.3 | async-start | bytes 32768 | tf_op jit(solution)/shard_map/all_to_all | solution.py:60

commit v2 on v0

--- a/solution.py
+++ b/solution.py
@@ -238,20 +238,46 @@
     out[...] = dot(total, right, HI)
 
 
-def x_kernel(ids, after, vv, oo, x, xb):
-    me = ids[0]
+def x_kernel(ids, after, vv, oo, x, keep, send):
+    core = ids[1]
     del after
-    for p in range(2):
-        for q in range(4):
-            slot = slot_of(q, me)
-            for g, a, b, lo, hi in tiles_of(36 * p + 9 * q, 9):
-                v = vv[g, :, a:b].astype(F32) - oo[q, p, :, lo:hi]
-                x[q, p, :, lo:hi] = v
-                xb[slot, p, :, lo:hi] = v.astype(BF)
-
-
-def base_kernel(ids, mine, theirs, coupling, rows, t1_out):
+
+    def work(own):
+        for p in range(2):
+            out = keep if p == own else send
+            for q in range(4):
+                for g, a, b, lo, hi in tiles_of(36 * p + 9 * q, 9):
+                    v = vv[g, :, a:b].astype(F32) - oo[q, p, :, lo:hi]
+                    x[q, p, :, lo:hi] = v
+                    out[q, :, lo:hi] = v.astype(BF)
+                out[q, VL:VP, :] = jnp.zeros((VP - VL, BLK), BF)
+
+    pl.when(core == 0)(lambda: work(0))
+    pl.when(core == 1)(lambda: work(1))
+
+
+def merge_kernel(ids, keep, recv, out):
     core = ids[1]
+    out[pl.ds(4 * core, 4)] = keep[...]
+    out[pl.ds(4 - 4 * core, 4)] = recv[...]
+
+
+def products(mine, theirs, y, place):
+    scale = 1.0 / math.sqrt(OC * OC * NV * VL)
+    same = lax.rem(iota((128, 128), 0), 16) == lax.rem(iota((128, 128), 1), 16)
+    left = (iota((Z, 128), 1) // 16 == iota((Z, 128), 0)).astype(F32)
+    rows = []
+    for ref in (mine, theirs):
+        g = jnp.zeros((128, 128), F32)
+        for b in range(2):
+            lhs = ref[:, 16 * b : 16 * (b + 1), :].reshape(128, BLK)
+            g += dot_nt(lhs, y[:, 16 * b : 16 * (b + 1), :].reshape(128, BLK))
+        rows.append(dot(dot(left, jnp.where(same, g, 0.0), HI), place * scale, HI))
+    return rows
+
+
+def base_kernel(ids, mine, theirs, ov, coupling, rows, t1_out, y):
+    me, core = ids[0], ids[1]
     half = (iota((128, KH), 0) == KH * core + iota((128, KH), 1)).astype(F32)
     place_c = (iota((KH, 128), 1) == KH * core + iota((KH, 128), 0)).astype(F32)
     near, far = 8 * core, 8 - 8 * core
@@ -264,31 +290,24 @@
     )
     both = jnp.concatenate(t1, axis=0)
     row += dot(dot(dot(both, half, HI), c, HI) * (-0.5 / math.sqrt(OC)), place, HI)
-    rows[...] = row
-    for j, start in enumerate((near, far)):
-        t1_out[pl.ds(pl.multiple_of(start, 8), 8), :] = t1[j]
-
-
-def s_kernel(ids, mine, theirs, ov, rows, *refs):
-    me, core = ids[0], ids[1]
-    out, y = refs[4], refs[5]
     for t in range(4):
         at = 2 * lax.rem(me - t + Z, 4)
         for p in range(2):
-            y[at + p] = (refs[t][p].astype(F32) + ov[t, p].astype(F32)).astype(BF)
-    y[:, VL:VP, :] = jnp.zeros((Z, VP - VL, BLK), BF)
+            y[at + p] = ov[t, p]
+    spot = iota((128, 128), 1) == OC + near + iota((128, 128), 0) // 16
+    parts = products(mine, theirs, y, spot.astype(F32))
+    rows[...] = row + jnp.concatenate(parts, axis=0)
+    for j, start in enumerate((near, far)):
+        t1_out[pl.ds(pl.multiple_of(start, 8), 8), :] = t1[j]
+
+
+def s_kernel(ids, mine, theirs, x, rows, out):
+    core = ids[1]
     near, far = 8 * core, 8 - 8 * core
-    n8 = iota((128, 128), 0) // 16
-    place = (iota((128, 128), 1) == OC + near + n8).astype(F32)
-    place = place * (1.0 / math.sqrt(OC * OC * NV * VL))
-    same = lax.rem(iota((128, 128), 0), 16) == lax.rem(iota((128, 128), 1), 16)
-    left = (iota((Z, 128), 1) // 16 == iota((Z, 128), 0)).astype(F32)
-    for j, ref in enumerate((mine, theirs)):
-        g = jnp.zeros((128, 128), F32)
-        for b in range(2):
-            lhs = ref[:, 16 * b : 16 * (b + 1), :].reshape(128, BLK)
-            g += dot_nt(lhs, y[:, 16 * b : 16 * (b + 1), :].reshape(128, BLK))
-        row = rows[8 * j : 8 * (j + 1), :] + dot(dot(left, jnp.where(same, g, 0.0), HI), place, HI)
+    spot = iota((128, 128), 1) == OC + core + 2 * (iota((128, 128), 0) // 16)
+    parts = products(mine, theirs, x, spot.astype(F32))
+    for j in range(2):
+        row = rows[8 * j : 8 * (j + 1), :] + parts[j]
         start = (near if j == 0 else far) // 2
         for i in range(4):
             pair = jnp.concatenate([row[2 * i : 2 * i + 1, :], row[2 * i + 1 : 2 * i + 2, :]], axis=1)
@@ -362,9 +381,8 @@
     outer_mine, outer_theirs = call(
         outer_kernel, (shape(roots, BF), shape(roots, BF)), [SMEM, VMEM, VMEM, VMEM], flops=1 << 30
     )(ids, mine, theirs, w_ovoo)
-    ov = call(add_kernel, shape(chunks, BF), [SMEM, VMEM, VMEM])(
-        ids, outer_mine, other_core(outer_theirs)
-    )
+    outer_recv = other_core(outer_theirs)
+    ov = call(add_kernel, shape(chunks, BF), [SMEM, VMEM, VMEM])(ids, outer_mine, outer_recv)
     ov_owned = z_steps(ov, back=True)
     coupling = call(
         coupling_kernel,
@@ -374,16 +392,24 @@
         flops=1 << 30,
     )(mine, theirs, w_ooov)
 
-    x, xr = call(
-        x_kernel, (shape(chunks, F32), shape(chunks, BF)), [SMEM, pl.ANY, VMEM, VMEM]
+    half = (4, VP, BLK)
+    x, keep, send = call(
+        x_kernel, (shape(chunks, F32), shape(half, BF), shape(half, BF)), [SMEM, pl.ANY, VMEM, VMEM]
     )(ids, coupling, vv, oo)
-    x_blocks = z_steps(xr)
+    recv = other_core(send)
+    x_root = call(merge_kernel, shape(roots, BF), [SMEM, VMEM, VMEM])(
+        ids, keep, recv
+    )
+    x_blocks = exchange(x_root, "root")
     rows, t1 = call(
-        base_kernel, (shape((16, 128), F32), shape((16, 128), F32)), [SMEM, VMEM, VMEM, VMEM]
-    )(ids, mine, theirs, coupling)
+        base_kernel,
+        (shape((16, 128), F32), shape((16, 128), F32)),
+        [SMEM, VMEM, VMEM, VMEM, VMEM],
+        [VMEM(roots, BF)],
+    )(ids, mine, theirs, ov, coupling)
     message = call(
-        s_kernel, shape((Z, 2, 1, 256), F32), [SMEM] + [VMEM] * 8, [VMEM(roots, BF)]
-    )(ids, mine, theirs, ov, rows, *x_blocks)
+        s_kernel, shape((Z, 2, 1, 256), F32), [SMEM, VMEM, VMEM, VMEM, VMEM]
+    )(ids, mine, theirs, x_blocks, rows)
     arrived = exchange(message.reshape(16, 1, 256), ROOT_OCC)
     copies = call(sum_kernel, shape((NV, 1, 256), F32), [VMEM])(arrived)
     arrived = exchange(copies, VIRT)

time: 117 us -> 120 us (1.026)
  waiting for transfers between devices: 20.2 us -> 30.3 us
  starting transfers between devices: 66.6 us -> 58.9 us
    ppermute x12 -> x8, starting transfers between devices: 39.5 us -> 25.7 us  [z_steps(): out.append(lax.ppermute(x[t], ROOT_OCC, pairs))]
    all_to_all x4 -> x5, waiting for transfers between devices: 7.78 us -> 15 us  [exchange(): return lax.all_to_all(x, axes, split_axis=0, concat_axis=0, tiled=True)]
    all_to_all x4 -> x5, starting transfers between devices: 25.2 us -> 28.7 us  [exchange(): return lax.all_to_all(x, axes, split_axis=0, concat_axis=0, tiled=True)]
    ppermute x3 -> x4, waiting for transfers between devices: 0.01 us -> 2.84 us  [other_core(): return lax.ppermute(x, 'occ', [(0, 1), (1, 0)])]
    ppermute x3 -> x4, starting transfers between devices: 1.9 us -> 4.5 us  [other_core(): return lax.ppermute(x, 'occ', [(0, 1), (1, 0)])]
    pallas_call x1, Pallas kernels: 1.1 us -> 2.32 us  [local(): call(base_kernel, (shape((16, 128), F32), shape((16, 128), F32)), [SMEM,...]
    pallas_call x2 -> x3, Pallas kernels: 3.36 us -> 4.56 us  [the longest x1 2.46 us: local(): call(s_kernel, shape((Z, 2, 1, 256), F32), [SMEM, VMEM, VMEM, VMEM, VMEM])]
    unnamed x22 -> x28, local copies, waits for them, and re-layouts: 7.43 us -> 8.07 us
  transfers between devices with their start and end apart: 19 -> 17, of which waited for: 7 -> 10; matrix products, arithmetic and copies ran while one was open for 1% -> 1% of each run, Pallas kernels for 13% -> 11%
where the time goes in v2:
time: 120 us
  starting transfers between devices  58.9 us (49%)
  waiting for transfers between devices  30.3 us (25%)
  Pallas kernels  21.3 us (18%)
  local copies, waits for them, and re-layouts  8.17 us (7%)
    all_to_all x5, starting transfers between devices, exchange(): return lax.all_to_all(x, axes, split_axis=0, concat_axis=0, tiled=True)  28.7 us
    ppermute x8, starting transfers between devices, z_steps(): out.append(lax.ppermute(x[t], ROOT_OCC, pairs))  25.7 us
    all_to_all x5, waiting for transfers between devices, exchange(): return lax.all_to_all(x, axes, split_axis=0, concat_axis=0, tiled=True)  15 us
    ppermute x8, waiting for transfers between devices, z_steps(): out.append(lax.ppermute(x[t], ROOT_OCC, pairs))  12.5 us
    unnamed x28, local copies, waits for them, and re-layouts  8.07 us
    ppermute x4, starting transfers between devices, other_core(): return lax.ppermute(x, 'occ', [(0, 1), (1, 0)])  4.5 us
    pallas_call x1, Pallas kernels, local(): call(oo_kernel, shape(chunks, F32), [SMEM, VMEM, VMEM, VMEM], [VMEM((384,...  3.16 us
    ppermute x4, waiting for transfers between devices, other_core(): return lax.ppermute(x, 'occ', [(0, 1), (1, 0)])  2.84 us
  transfers between devices with their start and end apart: 17, of which 10 were waited for; matrix products, arithmetic and copies ran while one was open for 1% of the time, Pallas kernels for 11%

profile of v2, /device:TPU:1, one launch (start us, length us, event | category | flops | bytes accessed | tf_op | source)
XLA Modules:
  0.0 119.6 jit_solution(15809897144109028623)
XLA Ops:
  0.6 1.2 copy.10.doubles
  2.5 1.5 %shard_map.94 = (bf16[4,2,32,1152]{3,2,1,0:T(8,128)(2,1)S(1)}, bf16[16,32,640]{2,1,0:T(8,128)(2,1)}) custom-call(s32[2]{0:T(128)S(1)} %pad_add_fusion.ids, bf16[2,30,4608]{2,1,0:T(8,128)(2,1)S(1)} %copy.10.doubles, bf16[2,96]{1,0:T(2,128)(2,1)S(1)} %copy-done.6), custom_call_target="tpu_custom_call" | custom-call | flops 16777216 | bytes 1048576 | tf_op jit(solution)/shard_map/pallas_call | solution.py:356
  4.1 7.6 %all-to-all-start = ((bf16[16,32,640]{2,1,0:T(8,128)(2,1)}), bf16[16,32,640]{2,1,0:T(8,128)(2,1)S(1)}, u32[]{:S(2)}, u32[]{:S(2)}) async-start(bf16[16,32,640]{2,1,0:T(8,128)(2,1)} %get-tuple-element.14), calls=%async_computation | async-start | bytes 1310720 | tf_op jit(solution)/shard_map/all_to_all | solution.py:61
  12.8 8.7 %collective-permute-start = (bf16[2,32,1152]{2,1,0:T(8,128)(2,1)S(1)}, bf16[2,32,1152]{2,1,0:T(8,128)(2,1)S(1)}, u32[]{:S(2)}, u32[]{:S(2)}) collective-permute-start(bf16[2,32,1152]{2,1,0:T(8,128)(2,1)S(1)} %get-tuple-element.35), channel_id=1, source_target_pairs={{0,0},{1,128},{32,32},{33,160},{64,64},{65,192},{96,96},{97,224},{... | collective-permute-start | bytes 442376 | tf_op jit(solution)/shard_map/ppermute | solution.py:82
  21.6 4.3 %collective-permute-start.2 = (bf16[2,32,1152]{2,1,0:T(8,128)(2,1)S(1)}, bf16[2,32,1152]{2,1,0:T(8,128)(2,1)S(1)}, u32[]{:S(2)}, u32[]{:S(2)}) collective-permute-start(bf16[2,32,1152]{2,1,0:T(8,128)(2,1)S(1)} %get-tuple-element.33), channel_id=1, source_target_pairs={{0,64},{1,192},{32,96},{33,224},{64,0},{65,128},{96,32},{97,160},{... | collective-permute-start | bytes 442376 | tf_op jit(solution)/shard_map/ppermute | solution.py:82
  25.9 2.1 %shard_map.95.after = bf16[16,32,640]{2,1,0:T(8,128)(2,1)} custom-call(bf16[480,480]{1,0:T(8,128)(2,1)S(1)} %copy-done.8, bf16[16,32,640]{2,1,0:T(8,128)(2,1)S(1)} %all-to-all-done.x), custom_call_target="tpu_custom_call" | custom-call | flops 536870912 | bytes 1048576 | tf_op jit(solution)/shard_map/pallas_call | solution.py:374
  28.3 5.0 %collective-permute-done.2.refs_2_ = bf16[2,32,1152]{2,1,0:T(8,128)(2,1)S(1)} collective-permute-done((bf16[2,32,1152]{2,1,0:T(8,128)(2,1)S(1)}, bf16[2,32,1152]{2,1,0:T(8,128)(2,1)S(1)}, u32[]{:S(2)}, u32[]{:S(2)}) %collective-permute-start.2) | collective-permute-done | bytes 147488 | tf_op jit(solution)/shard_map/ppermute | solution.py:82
  33.3 1.6 %collective-permute-done.3.refs_3_ = bf16[2,32,1152]{2,1,0:T(8,128)(2,1)S(1)} collective-permute-done((bf16[2,32,1152]{2,1,0:T(8,128)(2,1)S(1)}, bf16[2,32,1152]{2,1,0:T(8,128)(2,1)S(1)}, u32[]{:S(2)}, u32[]{:S(2)}) %collective-permute-start.3) | collective-permute-done | bytes 147488 | tf_op jit(solution)/shard_map/ppermute | solution.py:82
  35.5 6.9 %all-to-all-start.1 = ((bf16[16,32,640]{2,1,0:T(8,128)(2,1)}), bf16[16,32,640]{2,1,0:T(8,128)(2,1)S(1)}, u32[]{:S(2)}, u32[]{:S(2)}) async-start(bf16[16,32,640]{2,1,0:T(8,128)(2,1)} %shard_map.95.after), calls=%async_computation.1 | async-start | bytes 1310720 | tf_op jit(solution)/shard_map/all_to_all | solution.py:61
  42.5 3.2 %shard_map.98.oo = f32[4,2,32,1152]{3,2,1,0:T(8,128)S(1)} custom-call(s32[2]{0:T(128)S(1)} %pad_add_fusion.ids, bf16[4,2,32,1152]{3,2,1,0:T(8,128)(2,1)S(1)} %get-tuple-element.15.zb, bf16[4,2,32,1152]{3,2,1,0:T(8,128)(2,1)S(1)} %collective-permute-done.5.zo, bf16[96,96]{1,0:T(8,128)(2,1)S(1)} %copy-done.9), custom_call_target="tpu_custom_call" | custom-call | flops 2147483648 | bytes 1048576 | tf_op jit(solution)/shard_map/pallas_call | solution.py:362
  46.7 1.5 %shard_map.97.after.coupling = f32[48,16]{1,0:T(8,128)S(1)} custom-call(bf16[8,32,1152]{2,1,0:T(8,128)(2,1)S(1)} %shard_map.96.mine, bf16[8,32,1152]{2,1,0:T(8,128)(2,1)S(1)} %collective-permute-done.4.theirs, bf16[30,48,1152]{2,1,0:T(8,128)(2,1)S(1)} %bitcast.24), custom_call_target="tpu_custom_call" | custom-call | flops 1073741824 | bytes 1048576 | tf_op jit(solution)/shard_map/pallas_call | solution.py:387
  48.2 5.8 %all-to-all-done.1.vv = bf16[16,32,640]{2,1,0:T(8,128)(2,1)S(1)} async-done(((bf16[16,32,640]{2,1,0:T(8,128)(2,1)}), bf16[16,32,640]{2,1,0:T(8,128)(2,1)S(1)}, u32[]{:S(2)}, u32[]{:S(2)}) %all-to-all-start.1) | async-done | bytes 655392 | tf_op jit(solution)/shard_map/all_to_all | solution.py:61
  54.0 1.3 %copy-done.3 = f32[4,2,32,1152]{3,2,1,0:T(8,128)S(1)} copy-done((f32[4,2,32,1152]{3,2,1,0:T(8,128)S(1)}, f32[4,2,32,1152]{3,2,1,0:T(8,128)}, u32[]{:S(2)}) %copy-start.3) | copy-done | bytes 1179672
  56.0 2.4 %collective-permute-start.11 = (bf16[4,32,1152]{2,1,0:T(8,128)(2,1)S(1)}, bf16[4,32,1152]{2,1,0:T(8,128)(2,1)S(1)}, u32[]{:S(2)}, u32[]{:S(2)}) collective-permute-start(bf16[4,32,1152]{2,1,0:T(8,128)(2,1)S(1)} %get-tuple-element.20), channel_id=1, source_target_pairs={{0,1},{1,0},{2,3},{3,2},{4,5},{5,4},{6,7},{7,6},{8,9},{9,8},{10,11... | collective-permute-start | bytes 884744 | tf_op jit(solution)/shard_map/ppermute | solution.py:69
  58.4 1.2 %collective-permute-done.11.recv = bf16[4,32,1152]{2,1,0:T(8,128)(2,1)S(1)} collective-permute-done((bf16[4,32,1152]{2,1,0:T(8,128)(2,1)S(1)}, bf16[4,32,1152]{2,1,0:T(8,128)(2,1)S(1)}, u32[]{:S(2)}, u32[]{:S(2)}) %collective-permute-start.11) | collective-permute-done | bytes 294944 | tf_op jit(solution)/shard_map/ppermute | solution.py:69
  59.6 1.4 %shard_map.103 = bf16[8,32,1152]{2,1,0:T(8,128)(2,1)} custom-call(s32[2]{0:T(128)S(1)} %pad_add_fusion.ids, bf16[4,32,1152]{2,1,0:T(8,128)(2,1)S(1)} %get-tuple-element.19.keep, bf16[4,32,1152]{2,1,0:T(8,128)(2,1)S(1)} %collective-permute-done.11.recv), custom_call_target="tpu_custom_call" | custom-call | flops 16777216 | bytes 1048576 | tf_op jit(solution)/shard_map/pallas_call | solution.py:400
  61.0 6.8 %all-to-all-start.2 = ((bf16[8,32,1152]{2,1,0:T(8,128)(2,1)}), bf16[8,32,1152]{2,1,0:T(8,128)(2,1)S(1)}, u32[]{:S(2)}, u32[]{:S(2)}) async-start(bf16[8,32,1152]{2,1,0:T(8,128)(2,1)} %shard_map.103), calls=%async_computation.2 | async-start | bytes 1179648 | tf_op jit(solution)/shard_map/all_to_all | solution.py:61
  67.8 1.9 %copy-done = bf16[48,30,1152]{2,0,1:T(8,128)(2,1)S(1)} copy-done((bf16[48,30,1152]{2,0,1:T(8,128)(2,1)S(1)}, bf16[48,30,1152]{2,0,1:T(8,128)(2,1)}, u32[]{:S(2)}) %copy-start) | copy-done | bytes 3317784
  69.8 2.0 %shard_map.100 = (bf16[8,32,1152]{2,1,0:T(8,128)(2,1)S(1)}, bf16[8,32,1152]{2,1,0:T(8,128)(2,1)S(1)}) custom-call(s32[2]{0:T(128)S(1)} %pad_add_fusion.ids, bf16[8,32,1152]{2,1,0:T(8,128)(2,1)S(1)} %shard_map.96.mine, bf16[8,32,1152]{2,1,0:T(8,128)(2,1)S(1)} %collective-permute-done.4.theirs, bf16[30,48,1152]{2,1,0:T(8,128)(2,1)S(1)} %bitcast.23), custom_call_target="tpu_custom_call" | custom-call | flops 1073741824 | bytes 1048576 | tf_op jit(solution)/shard_map/pallas_call | solution.py:381
  72.7 1.6 %collective-permute-done.6.b = bf16[8,32,1152]{2,1,0:T(8,128)(2,1)S(1)} collective-permute-done((bf16[8,32,1152]{2,1,0:T(8,128)(2,1)S(1)}, bf16[8,32,1152]{2,1,0:T(8,128)(2,1)S(1)}, u32[]{:S(2)}, u32[]{:S(2)}) %collective-permute-start.6) | collective-permute-done | bytes 589856 | tf_op jit(solution)/shard_map/ppermute | solution.py:69
  75.0 2.3 %shard_map.104 = (f32[16,128]{1,0:T(8,128)S(1)}, f32[16,128]{1,0:T(8,128)S(1)}) custom-call(s32[2]{0:T(128)S(1)} %pad_add_fusion.ids, bf16[8,32,1152]{2,1,0:T(8,128)(2,1)S(1)} %shard_map.96.mine, bf16[8,32,1152]{2,1,0:T(8,128)(2,1)S(1)} %collective-permute-done.4.theirs, bf16[4,2,32,1152]{3,2,1,0:T(8,128)(2,1)S(1)} %shard_map.101.ov, f32[48,16]{1,0:T(8,128)S(1)} %copy-done.5), custom_call_target="tpu_custom_call" | custom-call | flops 16777216 | bytes 1048576 | tf_op jit(solution)/shard_map/pallas_call | solution.py:404
  78.0 9.2 %all-to-all-done.2.x = bf16[8,32,1152]{2,1,0:T(8,128)(2,1)S(1)} async-done(((bf16[8,32,1152]{2,1,0:T(8,128)(2,1)}), bf16[8,32,1152]{2,1,0:T(8,128)(2,1)S(1)}, u32[]{:S(2)}, u32[]{:S(2)}) %all-to-all-start.2) | async-done | bytes 589856 | tf_op jit(solution)/shard_map/all_to_all | solution.py:61
  87.2 2.5 %shard_map.105 = f32[8,2,1,256]{3,2,1,0:T(1,128)} custom-call(s32[2]{0:T(128)S(1)} %pad_add_fusion.ids, bf16[8,32,1152]{2,1,0:T(8,128)(2,1)S(1)} %shard_map.96.mine, bf16[8,32,1152]{2,1,0:T(8,128)(2,1)S(1)} %collective-permute-done.4.theirs, bf16[8,32,1152]{2,1,0:T(8,128)(2,1)S(1)} %all-to-all-done.2.x, f32[16,128]{1,0:T(8,128)S(1)} %get-tuple-element.21.rows), custom_call_target="tpu_custom_call" | custom-call | flops 16777216 | bytes 1048576 | tf_op jit(solution)/shard_map/pallas_call | solution.py:410
  89.6 3.9 %all-to-all-start.3 = ((f32[16,1,256]{2,1,0:T(1,128)}), f32[16,1,256]{2,1,0:T(1,128)S(1)}, u32[]{:S(2)}, u32[]{:S(2)}) async-start(f32[16,1,256]{2,1,0:T(1,128)} %bitcast.13), calls=%async_computation.3 | async-start | bytes 32768 | tf_op jit(solution)/shard_map/all_to_all | solution.py:61
  93.6 7.5 %collective-permute-start.7 = (bf16[2,32,1152]{2,1,0:T(8,128)(2,1)S(1)}, bf16[2,32,1152]{2,1,0:T(8,128)(2,1)S(1)}, u32[]{:S(2)}, u32[]{:S(2)}) collective-permute-start(bf16[2,32,1152]{2,1,0:T(8,128)(2,1)S(1)} %get-tuple-element.31), channel_id=1, source_target_pairs={{0,0},{128,1},{32,32},{160,33},{64,64},{192,65},{96,96},{224,97},{... | collective-permute-start | bytes 442376 | tf_op jit(solution)/shard_map/ppermute | solution.py:82
  101.5 3.6 %collective-permute-start.9 = (bf16[2,32,1152]{2,1,0:T(8,128)(2,1)S(1)}, bf16[2,32,1152]{2,1,0:T(8,128)(2,1)S(1)}, u32[]{:S(2)}, u32[]{:S(2)}) collective-permute-start(bf16[2,32,1152]{2,1,0:T(8,128)(2,1)S(1)} %get-tuple-element.29), channel_id=1, source_target_pairs={{64,0},{192,1},{96,32},{224,33},{0,64},{128,65},{32,96},{160,97},{... | collective-permute-start | bytes 442376 | tf_op jit(solution)/shard_map/ppermute | solution.py:82
  105.1 1.1 collective-permute-start.10
  106.8 3.4 %all-to-all-start.4 = ((f32[16,1,256]{2,1,0:T(1,128)}), f32[16,1,256]{2,1,0:T(1,128)S(1)}, u32[]{:S(2)}, u32[]{:S(2)}) async-start(f32[16,1,256]{2,1,0:T(1,128)} %shard_map.106), calls=%async_computation.4 | async-start | bytes 32768 | tf_op jit(solution)/shard_map/all_to_all | solution.py:61
  110.3 2.5 %collective-permute-done.8.refs_1_ = bf16[2,32,1152]{2,1,0:T(8,128)(2,1)S(1)} collective-permute-done((bf16[2,32,1152]{2,1,0:T(8,128)(2,1)S(1)}, bf16[2,32,1152]{2,1,0:T(8,128)(2,1)S(1)}, u32[]{:S(2)}, u32[]{:S(2)}) %collective-permute-start.8) | collective-permute-done | bytes 147488 | tf_op jit(solution)/shard_map/ppermute | solution.py:82
  113.6 2.3 %collective-permute-done.10.refs_3_ = bf16[2,32,1152]{2,1,0:T(8,128)(2,1)S(1)} collective-permute-done((bf16[2,32,1152]{2,1,0:T(8,128)(2,1)S(1)}, bf16[2,32,1152]{2,1,0:T(8,128)(2,1)S(1)}, u32[]{:S(2)}, u32[]{:S(2)}) %collective-permute-start.10) | collective-permute-done | bytes 147488 | tf_op jit(solution)/shard_map/ppermute | solution.py:82
  116.7 1.4 %copy.11 = bf16[2,30,4608]{2,0,1:T(2,128)(2,1)} copy(bf16[2,30,4608]{2,1,0:T(8,128)(2,1)S(1)} %shard_map.102) | data formatting | bytes 1105920
  118.1 1.5 %shard_map.107 = (f32[2,96]{1,0:T(2,128)}, f32[2,16]{1,0:T(2,128)}) custom-call(s32[2]{0:T(128)S(1)} %pad_add_fusion.ids, s32[16]{0:T(128)S(1)} %copy-done.7, f32[1,16]{1,0:T(1,128)S(1)} %convert_bitcast_fusion.active, f32[16,1,256]{2,1,0:T(1,128)S(1)} %all-to-all-done.4.x, f32[16,128]{1,0:T(8,128)S(1)} %copy-done.12, bf16[96,96]{1,0:T(8,128)(2,1)S(1)} %copy-done.10), custom_call_target="tpu_custom_call" | custom-call | flops 16777216 | bytes 1048576 | tf_op jit(solution)/shard_map/pallas_call | solution.py:416
  (48 shorter events, 9.4 us)
Async XLA Ops:
  0.6 25.3 %copy-start.8 = (bf16[480,480]{1,0:T(8,128)(2,1)S(1)}, bf16[480,480]{1,0:T(8,128)(2,1)}, u32[]{:S(2)}) copy-start(bf16[480,480]{1,0:T(8,128)(2,1)} %fock.3) | copy-start | bytes 1382404
  1.9 0.7 copy-start.6
  4.1 21.8 %all-to-all-start = ((bf16[16,32,640]{2,1,0:T(8,128)(2,1)}), bf16[16,32,640]{2,1,0:T(8,128)(2,1)S(1)}, u32[]{:S(2)}, u32[]{:S(2)}) async-start(bf16[16,32,640]{2,1,0:T(8,128)(2,1)} %get-tuple-element.14), calls=%async_computation | async-start | bytes 1310720 | tf_op jit(solution)/shard_map/all_to_all | solution.py:61
  11.7 30.9 %copy-start.9 = (bf16[96,96]{1,0:T(8,128)(2,1)S(1)}, bf16[96,96]{1,0:T(8,128)(2,1)}, u32[]{:S(2)}) copy-start(bf16[96,96]{1,0:T(8,128)(2,1)} %fock.5) | copy-start | bytes 55300
  11.7 30.8 %collective-permute-start.5 = (bf16[4,2,32,1152]{3,2,1,0:T(8,128)(2,1)S(1)}, bf16[4,2,32,1152]{3,2,1,0:T(8,128)(2,1)S(1)}, u32[]{:S(2)}, u32[]{:S(2)}) collective-permute-start(bf16[4,2,32,1152]{3,2,1,0:T(8,128)(2,1)S(1)} %get-tuple-element.15.zb), channel_id=1, source_target_pairs={{0,1},{1,0},{2,3},{3,2},{4,5},{5,4},{6,7},{7,6},{8,9},{9,8},{10,11... | collective-permute-start | bytes 1769480 | tf_op jit(solution)/shard_map/ppermute | solution.py:69
  12.8 15.2 %collective-permute-start = (bf16[2,32,1152]{2,1,0:T(8,128)(2,1)S(1)}, bf16[2,32,1152]{2,1,0:T(8,128)(2,1)S(1)}, u32[]{:S(2)}, u32[]{:S(2)}) collective-permute-start(bf16[2,32,1152]{2,1,0:T(8,128)(2,1)S(1)} %get-tuple-element.35), channel_id=1, source_target_pairs={{0,0},{1,128},{32,32},{33,160},{64,64},{65,192},{96,96},{97,224},{... | collective-permute-start | bytes 442376 | tf_op jit(solution)/shard_map/ppermute | solution.py:82
  21.5 6.8 %collective-permute-start.1 = (bf16[2,32,1152]{2,1,0:T(8,128)(2,1)S(1)}, bf16[2,32,1152]{2,1,0:T(8,128)(2,1)S(1)}, u32[]{:S(2)}, u32[]{:S(2)}) collective-permute-start(bf16[2,32,1152]{2,1,0:T(8,128)(2,1)S(1)} %get-tuple-element.34), channel_id=1, source_target_pairs={{0,32},{1,160},{32,64},{33,192},{64,96},{65,224},{96,0},{97,128},{... | collective-permute-start | bytes 442376 | tf_op jit(solution)/shard_map/ppermute | solution.py:82
  21.6 11.7 %collective-permute-start.2 = (bf16[2,32,1152]{2,1,0:T(8,128)(2,1)S(1)}, bf16[2,32,1152]{2,1,0:T(8,128)(2,1)S(1)}, u32[]{:S(2)}, u32[]{:S(2)}) collective-permute-start(bf16[2,32,1152]{2,1,0:T(8,128)(2,1)S(1)} %get-tuple-element.33), channel_id=1, source_target_pairs={{0,64},{1,192},{32,96},{33,224},{64,0},{65,128},{96,32},{97,160},{... | collective-permute-start | bytes 442376 | tf_op jit(solution)/shard_map/ppermute | solution.py:82
  25.9 9.0 %collective-permute-start.3 = (bf16[2,32,1152]{2,1,0:T(8,128)(2,1)S(1)}, bf16[2,32,1152]{2,1,0:T(8,128)(2,1)S(1)}, u32[]{:S(2)}, u32[]{:S(2)}) collective-permute-start(bf16[2,32,1152]{2,1,0:T(8,128)(2,1)S(1)} %get-tuple-element.32), channel_id=1, source_target_pairs={{0,96},{1,224},{32,0},{33,128},{64,32},{65,160},{96,64},{97,192},{... | collective-permute-start | bytes 442376 | tf_op jit(solution)/shard_map/ppermute | solution.py:82
  35.4 11.3 %collective-permute-start.4 = (bf16[8,32,1152]{2,1,0:T(8,128)(2,1)S(1)}, bf16[8,32,1152]{2,1,0:T(8,128)(2,1)S(1)}, u32[]{:S(2)}, u32[]{:S(2)}) collective-permute-start(bf16[8,32,1152]{2,1,0:T(8,128)(2,1)S(1)} %shard_map.96.mine), channel_id=1, source_target_pairs={{0,1},{1,0},{2,3},{3,2},{4,5},{5,4},{6,7},{7,6},{8,9},{9,8},{10,11... | collective-permute-start | bytes 1769480 | tf_op jit(solution)/shard_map/ppermute | solution.py:69
  35.5 18.4 %all-to-all-start.1 = ((bf16[16,32,640]{2,1,0:T(8,128)(2,1)}), bf16[16,32,640]{2,1,0:T(8,128)(2,1)S(1)}, u32[]{:S(2)}, u32[]{:S(2)}) async-start(bf16[16,32,640]{2,1,0:T(8,128)(2,1)} %shard_map.95.after), calls=%async_computation.1 | async-start | bytes 1310720 | tf_op jit(solution)/shard_map/all_to_all | solution.py:61
  42.5 4.2 %copy-start.1 = (bf16[48,30,1152]{2,0,1:T(8,128)(2,1)S(1)}, bf16[48,30,1152]{2,0,1:T(8,128)(2,1)}, u32[]{:S(2)}) copy-start(bf16[48,30,1152]{2,0,1:T(8,128)(2,1)} %param.12) | copy-start | bytes 9953284
  45.7 1.0 copy-start.2
  48.2 12.8 %copy-start.4 = (f32[48,16]{1,0:T(8,128)}, f32[48,16]{1,0:T(8,128)S(1)}, u32[]{:S(2)}) copy-start(f32[48,16]{1,0:T(8,128)S(1)} %shard_map.97.after.coupling) | copy-start | bytes 9220
  54.0 1.3 %copy-start.3 = (f32[4,2,32,1152]{3,2,1,0:T(8,128)S(1)}, f32[4,2,32,1152]{3,2,1,0:T(8,128)}, u32[]{:S(2)}) copy-start(f32[4,2,32,1152]{3,2,1,0:T(8,128)} %copy-done.2) | copy-start | bytes 3538948
  56.0 3.7 %collective-permute-start.11 = (bf16[4,32,1152]{2,1,0:T(8,128)(2,1)S(1)}, bf16[4,32,1152]{2,1,0:T(8,128)(2,1)S(1)}, u32[]{:S(2)}, u32[]{:S(2)}) collective-permute-start(bf16[4,32,1152]{2,1,0:T(8,128)(2,1)S(1)} %get-tuple-element.20), channel_id=1, source_target_pairs={{0,1},{1,0},{2,3},{3,2},{4,5},{5,4},{6,7},{7,6},{8,9},{9,8},{10,11... | collective-permute-start | bytes 884744 | tf_op jit(solution)/shard_map/ppermute | solution.py:69
  61.0 26.1 %all-to-all-start.2 = ((bf16[8,32,1152]{2,1,0:T(8,128)(2,1)}), bf16[8,32,1152]{2,1,0:T(8,128)(2,1)S(1)}, u32[]{:S(2)}, u32[]{:S(2)}) async-start(bf16[8,32,1152]{2,1,0:T(8,128)(2,1)} %shard_map.103), calls=%async_computation.2 | async-start | bytes 1179648 | tf_op jit(solution)/shard_map/all_to_all | solution.py:61
  67.8 1.9 %copy-start = (bf16[48,30,1152]{2,0,1:T(8,128)(2,1)S(1)}, bf16[48,30,1152]{2,0,1:T(8,128)(2,1)}, u32[]{:S(2)}) copy-start(bf16[48,30,1152]{2,0,1:T(8,128)(2,1)} %param.11) | copy-start | bytes 9953284
  69.8 5.3 %copy-start.5 = (f32[48,16]{1,0:T(8,128)S(1)}, f32[48,16]{1,0:T(8,128)}, u32[]{:S(2)}) copy-start(f32[48,16]{1,0:T(8,128)} %copy-done.4) | copy-start | bytes 9220
  71.8 2.6 %collective-permute-start.6 = (bf16[8,32,1152]{2,1,0:T(8,128)(2,1)S(1)}, bf16[8,32,1152]{2,1,0:T(8,128)(2,1)S(1)}, u32[]{:S(2)}, u32[]{:S(2)}) collective-permute-start(bf16[8,32,1152]{2,1,0:T(8,128)(2,1)S(1)} %get-tuple-element.18), channel_id=1, source_target_pairs={{0,1},{1,0},{2,3},{3,2},{4,5},{5,4},{6,7},{7,6},{8,9},{9,8},{10,11... | collective-permute-start | bytes 1769480 | tf_op jit(solution)/shard_map/ppermute | solution.py:69
  74.3 36.0 %copy-start.7 = (s32[16]{0:T(128)S(1)}, s32[16]{0:T(128)}, u32[]{:S(2)}) copy-start(s32[16]{0:T(128)} %conv.3) | copy-start | bytes 196
  77.3 0.6 copy-start.11
  89.6 28.4 %copy-start.10 = (bf16[96,96]{1,0:T(8,128)(2,1)S(1)}, bf16[96,96]{1,0:T(8,128)(2,1)}, u32[]{:S(2)}) copy-start(bf16[96,96]{1,0:T(8,128)(2,1)} %fock.5) | copy-start | bytes 55300
  89.6 28.4 %copy-start.12 = (f32[16,128]{1,0:T(8,128)S(1)}, f32[16,128]{1,0:T(8,128)}, u32[]{:S(2)}) copy-start(f32[16,128]{1,0:T(8,128)} %copy-done.11) | copy-start | bytes 24580
  89.6 16.6 %all-to-all-start.3 = ((f32[16,1,256]{2,1,0:T(1,128)}), f32[16,1,256]{2,1,0:T(1,128)S(1)}, u32[]{:S(2)}, u32[]{:S(2)}) async-start(f32[16,1,256]{2,1,0:T(1,128)} %bitcast.13), calls=%async_computation.3 | async-start | bytes 32768 | tf_op jit(solution)/shard_map/all_to_all | solution.py:61
  93.6 16.7 %collective-permute-start.7 = (bf16[2,32,1152]{2,1,0:T(8,128)(2,1)S(1)}, bf16[2,32,1152]{2,1,0:T(8,128)(2,1)S(1)}, u32[]{:S(2)}, u32[]{:S(2)}) collective-permute-start(bf16[2,32,1152]{2,1,0:T(8,128)(2,1)S(1)} %get-tuple-element.31), channel_id=1, source_target_pairs={{0,0},{128,1},{32,32},{160,33},{64,64},{192,65},{96,96},{224,97},{... | collective-permute-start | bytes 442376 | tf_op jit(solution)/shard_map/ppermute | solution.py:82
  101.1 11.7 %collective-permute-start.8 = (bf16[2,32,1152]{2,1,0:T(8,128)(2,1)S(1)}, bf16[2,32,1152]{2,1,0:T(8,128)(2,1)S(1)}, u32[]{:S(2)}, u32[]{:S(2)}) collective-permute-start(bf16[2,32,1152]{2,1,0:T(8,128)(2,1)S(1)} %get-tuple-element.30), channel_id=1, source_target_pairs={{32,0},{160,1},{64,32},{192,33},{96,64},{224,65},{0,96},{128,97},{... | collective-permute-start | bytes 442376 | tf_op jit(solution)/shard_map/ppermute | solution.py:82
  101.5 12.1 %collective-permute-start.9 = (bf16[2,32,1152]{2,1,0:T(8,128)(2,1)S(1)}, bf16[2,32,1152]{2,1,0:T(8,128)(2,1)S(1)}, u32[]{:S(2)}, u32[]{:S(2)}) collective-permute-start(bf16[2,32,1152]{2,1,0:T(8,128)(2,1)S(1)} %get-tuple-element.29), channel_id=1, source_target_pairs={{64,0},{192,1},{96,32},{224,33},{0,64},{128,65},{32,96},{160,97},{... | collective-permute-start | bytes 442376 | tf_op jit(solution)/shard_map/ppermute | solution.py:82
  105.1 10.9 %collective-permute-start.10 = (bf16[2,32,1152]{2,1,0:T(8,128)(2,1)S(1)}, bf16[2,32,1152]{2,1,0:T(8,128)(2,1)S(1)}, u32[]{:S(2)}, u32[]{:S(2)}) collective-permute-start(bf16[2,32,1152]{2,1,0:T(8,128)(2,1)S(1)} %get-tuple-element.28), channel_id=1, source_target_pairs={{96,0},{224,1},{0,32},{128,33},{32,64},{160,65},{64,96},{192,97},{... | collective-permute-start | bytes 442376 | tf_op jit(solution)/shard_map/ppermute | solution.py:82
  106.8 11.2 %all-to-all-start.4 = ((f32[16,1,256]{2,1,0:T(1,128)}), f32[16,1,256]{2,1,0:T(1,128)S(1)}, u32[]{:S(2)}, u32[]{:S(2)}) async-start(f32[16,1,256]{2,1,0:T(1,128)} %shard_map.106), calls=%async_computation.4 | async-start | bytes 32768 | tf_op jit(solution)/shard_map/all_to_all | solution.py:61

commit v3 on v2

--- a/solution.py
+++ b/solution.py
@@ -238,28 +238,22 @@
     out[...] = dot(total, right, HI)
 
 
-def x_kernel(ids, after, vv, oo, x, keep, send):
+def x_kernel(ids, after, vv, oo, x, full, send):
     core = ids[1]
     del after
 
     def work(own):
         for p in range(2):
-            out = keep if p == own else send
             for q in range(4):
+                out = full.at[4 * own + q] if p == own else send.at[q]
                 for g, a, b, lo, hi in tiles_of(36 * p + 9 * q, 9):
                     v = vv[g, :, a:b].astype(F32) - oo[q, p, :, lo:hi]
                     x[q, p, :, lo:hi] = v
-                    out[q, :, lo:hi] = v.astype(BF)
-                out[q, VL:VP, :] = jnp.zeros((VP - VL, BLK), BF)
+                    out[:, lo:hi] = v.astype(BF)
+                out[VL:VP, :] = jnp.zeros((VP - VL, BLK), BF)
 
     pl.when(core == 0)(lambda: work(0))
     pl.when(core == 1)(lambda: work(1))
-
-
-def merge_kernel(ids, keep, recv, out):
-    core = ids[1]
-    out[pl.ds(4 * core, 4)] = keep[...]
-    out[pl.ds(4 - 4 * core, 4)] = recv[...]
 
 
 def products(mine, theirs, y, place):
@@ -276,7 +270,7 @@
     return rows
 
 
-def base_kernel(ids, mine, theirs, ov, coupling, rows, t1_out, y):
+def base_kernel(ids, mine, theirs, ov, coupling, fock, rows, singles_out, sub_out, y, t1_all):
     me, core = ids[0], ids[1]
     half = (iota((128, KH), 0) == KH * core + iota((128, KH), 1)).astype(F32)
     place_c = (iota((KH, 128), 1) == KH * core + iota((KH, 128), 0)).astype(F32)
@@ -298,7 +292,12 @@
     parts = products(mine, theirs, y, spot.astype(F32))
     rows[...] = row + jnp.concatenate(parts, axis=0)
     for j, start in enumerate((near, far)):
-        t1_out[pl.ds(pl.multiple_of(start, 8), 8), :] = t1[j]
+        t1_all[pl.ds(pl.multiple_of(start, 8), 8), :] = t1[j]
+    own = [t1_all[pl.ds(2 * me + p, 1), :] for p in range(2)]
+    own = jnp.concatenate(own, axis=0)[:, 0:OC]
+    all_fock = dot(t1_all[:, 0:OC].astype(BF), fock[...])
+    singles_out[...] = -dot(own.astype(BF), fock[...])
+    sub_out[...] = -dot_nt(own, all_fock, HI) * (1.0 / math.sqrt(OC))
 
 
 def s_kernel(ids, mine, theirs, x, rows, out):
@@ -318,19 +317,15 @@
     out[...] = jnp.broadcast_to(jnp.sum(x[...], axis=0, keepdims=True), out.shape)
 
 
-def final_kernel(ids, conv, active, x, t1, fock, singles, subspace):
+def final_kernel(ids, conv, active, x, own_singles, own_sub, singles, subspace):
     me = ids[0]
     summed = jnp.sum(x[...], axis=0)
     total = jnp.concatenate([summed[:, 0:128], summed[:, 128:256]], axis=0)
-    mine = jnp.concatenate([t1[pl.ds(2 * me, 1), :], t1[pl.ds(2 * me + 1, 1), :]], axis=0)[:, 0:OC]
-    all_fock = dot(t1[:, 0:OC].astype(BF), fock[...])
-    own_fock = dot(mine.astype(BF), fock[...])
     a0 = (1 - conv[2 * me]).astype(F32)
     a1 = (1 - conv[2 * me + 1]).astype(F32)
     own_active = jnp.where(iota((2, OC), 0) == 0, a0, a1)
-    singles[...] = own_active * (-own_fock - 0.5 * total[:, 0:OC])
-    part = total[:, OC : OC + 2 * Z] - dot_nt(mine, all_fock, HI) * (1.0 / math.sqrt(OC))
-    subspace[...] = part * active[...]
+    singles[...] = own_active * (own_singles[...] - 0.5 * total[:, 0:OC])
+    subspace[...] = (total[:, OC : OC + 2 * Z] + own_sub[...]) * active[...]
 
 
 def out_kernel(ids, conv, x, *refs):
@@ -392,21 +387,21 @@
         flops=1 << 30,
     )(mine, theirs, w_ooov)
 
-    half = (4, VP, BLK)
-    x, keep, send = call(
-        x_kernel, (shape(chunks, F32), shape(half, BF), shape(half, BF)), [SMEM, pl.ANY, VMEM, VMEM]
+    x, full, send = call(
+        x_kernel,
+        (shape(chunks, F32), shape(roots, BF), shape((4, VP, BLK), BF)),
+        [SMEM, pl.ANY, VMEM, VMEM],
     )(ids, coupling, vv, oo)
     recv = other_core(send)
-    x_root = call(merge_kernel, shape(roots, BF), [SMEM, VMEM, VMEM])(
-        ids, keep, recv
-    )
+    other = 4 * (1 - lax.axis_index("occ"))
+    x_root = lax.dynamic_update_slice_in_dim(full, recv, other, 0)
     x_blocks = exchange(x_root, "root")
-    rows, t1 = call(
+    rows, own_singles, own_sub = call(
         base_kernel,
-        (shape((16, 128), F32), shape((16, 128), F32)),
-        [SMEM, VMEM, VMEM, VMEM, VMEM],
-        [VMEM(roots, BF)],
-    )(ids, mine, theirs, ov, coupling)
+        (shape((16, 128), F32), shape((2, OC), F32), shape((2, 2 * Z), F32)),
+        [SMEM] + [VMEM] * 5,
+        [VMEM(roots, BF), VMEM((16, 128), F32)],
+    )(ids, mine, theirs, ov, coupling, occ_fock)
     message = call(
         s_kernel, shape((Z, 2, 1, 256), F32), [SMEM, VMEM, VMEM, VMEM, VMEM]
     )(ids, mine, theirs, x_blocks, rows)
@@ -417,7 +412,7 @@
         final_kernel,
         (shape((2, OC), F32), shape((2, 2 * Z), F32)),
         [SMEM, SMEM, VMEM, VMEM, VMEM, VMEM],
-    )(ids, converged, active, arrived, t1, occ_fock)
+    )(ids, converged, active, arrived, own_singles, own_sub)
 
     sigma_doubles = call(
         out_kernel, shape((2, VL, HALF), BF), [SMEM, SMEM] + [VMEM] * 5, [VMEM(chunks, BF)]

time: 120 us -> 120 us (level)
  local copies, waits for them, and re-layouts: 8.17 us -> 11 us
  waiting for transfers between devices: 30.3 us -> 28.4 us
    unnamed x28 -> x34, local copies, waits for them, and re-layouts: 8.07 us -> 10.1 us
    all_to_all x5, waiting for transfers between devices: 15 us -> 13.1 us  [exchange(): return lax.all_to_all(x, axes, split_axis=0, concat_axis=0, tiled=True)]
    pallas_call x3 -> x2, Pallas kernels: 4.42 us -> 3.02 us  [the longest x1 2.34 us: local(): call(base_kernel, (shape((16, 128), F32), shape((2, OC), F32), shape((2,...]
  transfers between devices with their start and end apart: 17 -> 17, of which waited for: 10 -> 10; matrix products, arithmetic and copies ran while one was open for 1% -> 1% of each run, Pallas kernels for 11% -> 12%
where the time goes in v3:
time: 120 us; the launch traced here: 119 us
  starting transfers between devices  58.8 us (49%)
  waiting for transfers between devices  28.4 us (24%)
  Pallas kernels  20.2 us (17%)
  local copies, waits for them, and re-layouts  11 us (9%)
    all_to_all x5, starting transfers between devices, exchange(): return lax.all_to_all(x, axes, split_axis=0, concat_axis=0, tiled=True)  28.7 us
    ppermute x8, starting transfers between devices, z_steps(): out.append(lax.ppermute(x[t], ROOT_OCC, pairs))  25.7 us
    all_to_all x5, waiting for transfers between devices, exchange(): return lax.all_to_all(x, axes, split_axis=0, concat_axis=0, tiled=True)  13.1 us
    ppermute x8, waiting for transfers between devices, z_steps(): out.append(lax.ppermute(x[t], ROOT_OCC, pairs))  12.4 us
    unnamed x34, local copies, waits for them, and re-layouts  10.1 us
    ppermute x4, starting transfers between devices, other_core(): return lax.ppermute(x, 'occ', [(0, 1), (1, 0)])  4.4 us
    pallas_call x1, Pallas kernels, local(): call(oo_kernel, shape(chunks, F32), [SMEM, VMEM, VMEM, VMEM], [VMEM((384,...  3.85 us
    ppermute x4, waiting for transfers between devices, other_core(): return lax.ppermute(x, 'occ', [(0, 1), (1, 0)])  2.84 us
  transfers between devices with their start and end apart: 17, of which 10 were waited for; matrix products, arithmetic and copies ran while one was open for 1% of the time, Pallas kernels for 12%

profile of v3, /device:TPU:1, one launch (start us, length us, event | category | flops | bytes accessed | tf_op | source)
XLA Modules:
  0.0 119.4 jit_solution(9969042630140459201)
XLA Ops:
  0.6 1.2 copy.10.doubles
  2.5 1.5 %shard_map.94 = (bf16[4,2,32,1152]{3,2,1,0:T(8,128)(2,1)S(1)}, bf16[16,32,640]{2,1,0:T(8,128)(2,1)}) custom-call(s32[2]{0:T(128)S(1)} %pad_add_fusion.ids, bf16[2,30,4608]{2,1,0:T(8,128)(2,1)S(1)} %copy.10.doubles, bf16[2,96]{1,0:T(2,128)(2,1)S(1)} %copy-done.9), custom_call_target="tpu_custom_call" | custom-call | flops 16777216 | bytes 1048576 | tf_op jit(solution)/shard_map/pallas_call | solution.py:351
  4.1 7.6 %all-to-all-start = ((bf16[16,32,640]{2,1,0:T(8,128)(2,1)}), bf16[16,32,640]{2,1,0:T(8,128)(2,1)S(1)}, u32[]{:S(2)}, u32[]{:S(2)}) async-start(bf16[16,32,640]{2,1,0:T(8,128)(2,1)} %get-tuple-element.15), calls=%async_computation | async-start | bytes 1310720 | tf_op jit(solution)/shard_map/all_to_all | solution.py:61
  11.7 1.0 collective-permute-start.5
  12.8 8.7 %collective-permute-start = (bf16[2,32,1152]{2,1,0:T(8,128)(2,1)S(1)}, bf16[2,32,1152]{2,1,0:T(8,128)(2,1)S(1)}, u32[]{:S(2)}, u32[]{:S(2)}) collective-permute-start(bf16[2,32,1152]{2,1,0:T(8,128)(2,1)S(1)} %get-tuple-element.37), channel_id=1, source_target_pairs={{0,0},{1,128},{32,32},{33,160},{64,64},{65,192},{96,96},{97,224},{... | collective-permute-start | bytes 442376 | tf_op jit(solution)/shard_map/ppermute | solution.py:82
  21.6 4.3 %collective-permute-start.2 = (bf16[2,32,1152]{2,1,0:T(8,128)(2,1)S(1)}, bf16[2,32,1152]{2,1,0:T(8,128)(2,1)S(1)}, u32[]{:S(2)}, u32[]{:S(2)}) collective-permute-start(bf16[2,32,1152]{2,1,0:T(8,128)(2,1)S(1)} %get-tuple-element.35), channel_id=1, source_target_pairs={{0,64},{1,192},{32,96},{33,224},{64,0},{65,128},{96,32},{97,160},{... | collective-permute-start | bytes 442376 | tf_op jit(solution)/shard_map/ppermute | solution.py:82
  25.9 2.1 %shard_map.95.after = bf16[16,32,640]{2,1,0:T(8,128)(2,1)} custom-call(bf16[480,480]{1,0:T(8,128)(2,1)S(1)} %copy-done.11, bf16[16,32,640]{2,1,0:T(8,128)(2,1)S(1)} %all-to-all-done.x), custom_call_target="tpu_custom_call" | custom-call | flops 536870912 | bytes 1048576 | tf_op jit(solution)/shard_map/pallas_call | solution.py:369
  28.3 5.0 %collective-permute-done.2.refs_2_ = bf16[2,32,1152]{2,1,0:T(8,128)(2,1)S(1)} collective-permute-done((bf16[2,32,1152]{2,1,0:T(8,128)(2,1)S(1)}, bf16[2,32,1152]{2,1,0:T(8,128)(2,1)S(1)}, u32[]{:S(2)}, u32[]{:S(2)}) %collective-permute-start.2) | collective-permute-done | bytes 147488 | tf_op jit(solution)/shard_map/ppermute | solution.py:82
  33.3 1.6 %collective-permute-done.3.refs_3_ = bf16[2,32,1152]{2,1,0:T(8,128)(2,1)S(1)} collective-permute-done((bf16[2,32,1152]{2,1,0:T(8,128)(2,1)S(1)}, bf16[2,32,1152]{2,1,0:T(8,128)(2,1)S(1)}, u32[]{:S(2)}, u32[]{:S(2)}) %collective-permute-start.3) | collective-permute-done | bytes 147488 | tf_op jit(solution)/shard_map/ppermute | solution.py:82
  35.5 6.9 %all-to-all-start.1 = ((bf16[16,32,640]{2,1,0:T(8,128)(2,1)}), bf16[16,32,640]{2,1,0:T(8,128)(2,1)S(1)}, u32[]{:S(2)}, u32[]{:S(2)}) async-start(bf16[16,32,640]{2,1,0:T(8,128)(2,1)} %shard_map.95.after), calls=%async_computation.1 | async-start | bytes 1310720 | tf_op jit(solution)/shard_map/all_to_all | solution.py:61
  42.5 3.8 %shard_map.98.oo = f32[4,2,32,1152]{3,2,1,0:T(8,128)S(1)} custom-call(s32[2]{0:T(128)S(1)} %pad_add_fusion.ids, bf16[4,2,32,1152]{3,2,1,0:T(8,128)(2,1)S(1)} %get-tuple-element.16.zb, bf16[4,2,32,1152]{3,2,1,0:T(8,128)(2,1)} %collective-permute-done.5.zo, bf16[96,96]{1,0:T(8,128)(2,1)S(1)} %copy-done.7), custom_call_target="tpu_custom_call" | custom-call | flops 2147483648 | bytes 1048576 | tf_op jit(solution)/shard_map/pallas_call | solution.py:357
  47.4 1.4 %shard_map.97.after.coupling = f32[48,16]{1,0:T(8,128)S(1)} custom-call(bf16[8,32,1152]{2,1,0:T(8,128)(2,1)S(1)} %shard_map.96.mine, bf16[8,32,1152]{2,1,0:T(8,128)(2,1)S(1)} %collective-permute-done.4.theirs, bf16[30,48,1152]{2,1,0:T(8,128)(2,1)S(1)} %bitcast.24), custom_call_target="tpu_custom_call" | custom-call | flops 1073741824 | bytes 1048576 | tf_op jit(solution)/shard_map/pallas_call | solution.py:382
  48.9 5.1 %all-to-all-done.1.vv = bf16[16,32,640]{2,1,0:T(8,128)(2,1)S(1)} async-done(((bf16[16,32,640]{2,1,0:T(8,128)(2,1)}), bf16[16,32,640]{2,1,0:T(8,128)(2,1)S(1)}, u32[]{:S(2)}, u32[]{:S(2)}) %all-to-all-start.1) | async-done | bytes 655392 | tf_op jit(solution)/shard_map/all_to_all | solution.py:61
  54.0 1.3 %copy-done.3 = f32[4,2,32,1152]{3,2,1,0:T(8,128)S(1)} copy-done((f32[4,2,32,1152]{3,2,1,0:T(8,128)S(1)}, f32[4,2,32,1152]{3,2,1,0:T(8,128)}, u32[]{:S(2)}) %copy-start.3) | copy-done | bytes 1179672
  56.8 2.4 %collective-permute-start.11 = (bf16[4,32,1152]{2,1,0:T(8,128)(2,1)S(1)}, bf16[4,32,1152]{2,1,0:T(8,128)(2,1)S(1)}, u32[]{:S(2)}, u32[]{:S(2)}) collective-permute-start(bf16[4,32,1152]{2,1,0:T(8,128)(2,1)S(1)} %get-tuple-element.21), channel_id=1, source_target_pairs={{0,1},{1,0},{2,3},{3,2},{4,5},{5,4},{6,7},{7,6},{8,9},{9,8},{10,11... | collective-permute-start | bytes 884744 | tf_op jit(solution)/shard_map/ppermute | solution.py:69
  59.1 1.2 %collective-permute-done.11 = bf16[4,32,1152]{2,1,0:T(8,128)(2,1)S(1)} collective-permute-done((bf16[4,32,1152]{2,1,0:T(8,128)(2,1)S(1)}, bf16[4,32,1152]{2,1,0:T(8,128)(2,1)S(1)}, u32[]{:S(2)}, u32[]{:S(2)}) %collective-permute-start.11) | collective-permute-done | bytes 294944 | tf_op jit(solution)/shard_map/ppermute | solution.py:69
  61.1 6.8 %all-to-all-start.2 = ((bf16[8,32,1152]{2,1,0:T(8,128)(2,1)}), bf16[8,32,1152]{2,1,0:T(8,128)(2,1)S(1)}, u32[]{:S(2)}, u32[]{:S(2)}) async-start(bf16[8,32,1152]{2,1,0:T(8,128)(2,1)} %constant_dynamic-update-slice_fusion), calls=%async_computation.2 | async-start | bytes 1179648 | tf_op jit(solution)/shard_map/all_to_all | solution.py:61
  67.9 1.9 %copy-done = bf16[48,30,1152]{2,0,1:T(8,128)(2,1)S(1)} copy-done((bf16[48,30,1152]{2,0,1:T(8,128)(2,1)S(1)}, bf16[48,30,1152]{2,0,1:T(8,128)(2,1)}, u32[]{:S(2)}) %copy-start) | copy-done | bytes 3317784
  69.8 2.0 %shard_map.100 = (bf16[8,32,1152]{2,1,0:T(8,128)(2,1)S(1)}, bf16[8,32,1152]{2,1,0:T(8,128)(2,1)S(1)}) custom-call(s32[2]{0:T(128)S(1)} %pad_add_fusion.ids, bf16[8,32,1152]{2,1,0:T(8,128)(2,1)S(1)} %shard_map.96.mine, bf16[8,32,1152]{2,1,0:T(8,128)(2,1)S(1)} %collective-permute-done.4.theirs, bf16[30,48,1152]{2,1,0:T(8,128)(2,1)S(1)} %bitcast.23), custom_call_target="tpu_custom_call" | custom-call | flops 1073741824 | bytes 1048576 | tf_op jit(solution)/shard_map/pallas_call | solution.py:376
  72.7 1.6 %collective-permute-done.6.b = bf16[8,32,1152]{2,1,0:T(8,128)(2,1)S(1)} collective-permute-done((bf16[8,32,1152]{2,1,0:T(8,128)(2,1)S(1)}, bf16[8,32,1152]{2,1,0:T(8,128)(2,1)S(1)}, u32[]{:S(2)}, u32[]{:S(2)}) %collective-permute-start.6) | collective-permute-done | bytes 589856 | tf_op jit(solution)/shard_map/ppermute | solution.py:69
  75.8 2.3 %shard_map.103 = (f32[16,128]{1,0:T(8,128)S(1)}, f32[2,96]{1,0:T(2,128)S(1)}, f32[2,16]{1,0:T(2,128)S(1)}) custom-call(s32[2]{0:T(128)S(1)} %pad_add_fusion.ids, bf16[8,32,1152]{2,1,0:T(8,128)(2,1)S(1)} %shard_map.96.mine, bf16[8,32,1152]{2,1,0:T(8,128)(2,1)S(1)} %collective-permute-done.4.theirs, bf16[4,2,32,1152]{3,2,1,0:T(8,128)(2,1)S(1)} %shard_map.101.ov, ...), custom_call_target="tpu_custom_call" | custom-call | flops 16777216 | bytes 1048576 | tf_op jit(solution)/shard_map/pallas_call | solution.py:399
  79.3 8.0 %all-to-all-done.2.x = bf16[8,32,1152]{2,1,0:T(8,128)(2,1)S(1)} async-done(((bf16[8,32,1152]{2,1,0:T(8,128)(2,1)}), bf16[8,32,1152]{2,1,0:T(8,128)(2,1)S(1)}, u32[]{:S(2)}, u32[]{:S(2)}) %all-to-all-start.2) | async-done | bytes 589856 | tf_op jit(solution)/shard_map/all_to_all | solution.py:61
  87.2 2.5 %shard_map.104 = f32[8,2,1,256]{3,2,1,0:T(1,128)} custom-call(s32[2]{0:T(128)S(1)} %pad_add_fusion.ids, bf16[8,32,1152]{2,1,0:T(8,128)(2,1)S(1)} %shard_map.96.mine, bf16[8,32,1152]{2,1,0:T(8,128)(2,1)S(1)} %collective-permute-done.4.theirs, bf16[8,32,1152]{2,1,0:T(8,128)(2,1)S(1)} %all-to-all-done.2.x, f32[16,128]{1,0:T(8,128)S(1)} %get-tuple-element.22.rows), custom_call_target="tpu_custom_call" | custom-call | flops 16777216 | bytes 1048576 | tf_op jit(solution)/shard_map/pallas_call | solution.py:405
  89.7 3.9 %all-to-all-start.3 = ((f32[16,1,256]{2,1,0:T(1,128)}), f32[16,1,256]{2,1,0:T(1,128)S(1)}, u32[]{:S(2)}, u32[]{:S(2)}) async-start(f32[16,1,256]{2,1,0:T(1,128)} %bitcast.13), calls=%async_computation.3 | async-start | bytes 32768 | tf_op jit(solution)/shard_map/all_to_all | solution.py:61
  93.7 7.5 %collective-permute-start.7 = (bf16[2,32,1152]{2,1,0:T(8,128)(2,1)S(1)}, bf16[2,32,1152]{2,1,0:T(8,128)(2,1)S(1)}, u32[]{:S(2)}, u32[]{:S(2)}) collective-permute-start(bf16[2,32,1152]{2,1,0:T(8,128)(2,1)S(1)} %get-tuple-element.33), channel_id=1, source_target_pairs={{0,0},{128,1},{32,32},{160,33},{64,64},{192,65},{96,96},{224,97},{... | collective-permute-start | bytes 442376 | tf_op jit(solution)/shard_map/ppermute | solution.py:82
  101.5 3.6 %collective-permute-start.9 = (bf16[2,32,1152]{2,1,0:T(8,128)(2,1)S(1)}, bf16[2,32,1152]{2,1,0:T(8,128)(2,1)S(1)}, u32[]{:S(2)}, u32[]{:S(2)}) collective-permute-start(bf16[2,32,1152]{2,1,0:T(8,128)(2,1)S(1)} %get-tuple-element.31), channel_id=1, source_target_pairs={{64,0},{192,1},{96,32},{224,33},{0,64},{128,65},{32,96},{160,97},{... | collective-permute-start | bytes 442376 | tf_op jit(solution)/shard_map/ppermute | solution.py:82
  105.1 1.1 collective-permute-start.10
  106.9 3.5 %all-to-all-start.4 = ((f32[16,1,256]{2,1,0:T(1,128)}), f32[16,1,256]{2,1,0:T(1,128)S(1)}, u32[]{:S(2)}, u32[]{:S(2)}) async-start(f32[16,1,256]{2,1,0:T(1,128)} %shard_map.105), calls=%async_computation.4 | async-start | bytes 32768 | tf_op jit(solution)/shard_map/all_to_all | solution.py:61
  110.4 2.4 %collective-permute-done.8.refs_1_ = bf16[2,32,1152]{2,1,0:T(8,128)(2,1)S(1)} collective-permute-done((bf16[2,32,1152]{2,1,0:T(8,128)(2,1)S(1)}, bf16[2,32,1152]{2,1,0:T(8,128)(2,1)S(1)}, u32[]{:S(2)}, u32[]{:S(2)}) %collective-permute-start.8) | collective-permute-done | bytes 147488 | tf_op jit(solution)/shard_map/ppermute | solution.py:82
  113.6 2.3 %collective-permute-done.10.refs_3_ = bf16[2,32,1152]{2,1,0:T(8,128)(2,1)S(1)} collective-permute-done((bf16[2,32,1152]{2,1,0:T(8,128)(2,1)S(1)}, bf16[2,32,1152]{2,1,0:T(8,128)(2,1)S(1)}, u32[]{:S(2)}, u32[]{:S(2)}) %collective-permute-start.10) | collective-permute-done | bytes 147488 | tf_op jit(solution)/shard_map/ppermute | solution.py:82
  116.7 1.4 %copy.11 = bf16[2,30,4608]{2,0,1:T(2,128)(2,1)} copy(bf16[2,30,4608]{2,1,0:T(8,128)(2,1)S(1)} %shard_map.102) | data formatting | bytes 1105920
  118.1 1.2 %shard_map.106 = (f32[2,96]{1,0:T(2,128)}, f32[2,16]{1,0:T(2,128)}) custom-call(s32[2]{0:T(128)S(1)} %pad_add_fusion.ids, s32[16]{0:T(128)S(1)} %copy-done.10, f32[1,16]{1,0:T(1,128)S(1)} %convert_bitcast_fusion.active, f32[16,1,256]{2,1,0:T(1,128)S(1)} %all-to-all-done.4.x, f32[2,96]{1,0:T(2,128)S(1)} %copy-done.13, f32[2,16]{1,0:T(2,128)S(1)} %copy-done.15), custom_call_target="tpu_custom_call" | custom-call | flops 16777216 | bytes 1048576 | tf_op jit(solution)/shard_map/pallas_call | solution.py:411
  (54 shorter events, 11.2 us)
Async XLA Ops:
  0.6 25.3 %copy-start.11 = (bf16[480,480]{1,0:T(8,128)(2,1)S(1)}, bf16[480,480]{1,0:T(8,128)(2,1)}, u32[]{:S(2)}) copy-start(bf16[480,480]{1,0:T(8,128)(2,1)} %fock.3) | copy-start | bytes 1382404
  1.9 0.7 copy-start.9
  4.1 21.8 %all-to-all-start = ((bf16[16,32,640]{2,1,0:T(8,128)(2,1)}), bf16[16,32,640]{2,1,0:T(8,128)(2,1)S(1)}, u32[]{:S(2)}, u32[]{:S(2)}) async-start(bf16[16,32,640]{2,1,0:T(8,128)(2,1)} %get-tuple-element.15), calls=%async_computation | async-start | bytes 1310720 | tf_op jit(solution)/shard_map/all_to_all | solution.py:61
  11.6 30.9 %copy-start.7 = (bf16[96,96]{1,0:T(8,128)(2,1)S(1)}, bf16[96,96]{1,0:T(8,128)(2,1)}, u32[]{:S(2)}) copy-start(bf16[96,96]{1,0:T(8,128)(2,1)} %fock.5) | copy-start | bytes 55300
  11.7 30.8 %collective-permute-start.5 = (bf16[4,2,32,1152]{3,2,1,0:T(8,128)(2,1)S(1)}, bf16[4,2,32,1152]{3,2,1,0:T(8,128)(2,1)}, u32[]{:S(2)}, u32[]{:S(2)}) collective-permute-start(bf16[4,2,32,1152]{3,2,1,0:T(8,128)(2,1)S(1)} %get-tuple-element.16.zb), channel_id=1, source_target_pairs={{0,1},{1,0},{2,3},{3,2},{4,5},{5,4},{6,7},{7,6},{8,9},{9,8},{10,11... | collective-permute-start | bytes 1769480 | tf_op jit(solution)/shard_map/ppermute | solution.py:69
  12.8 15.2 %collective-permute-start = (bf16[2,32,1152]{2,1,0:T(8,128)(2,1)S(1)}, bf16[2,32,1152]{2,1,0:T(8,128)(2,1)S(1)}, u32[]{:S(2)}, u32[]{:S(2)}) collective-permute-start(bf16[2,32,1152]{2,1,0:T(8,128)(2,1)S(1)} %get-tuple-element.37), channel_id=1, source_target_pairs={{0,0},{1,128},{32,32},{33,160},{64,64},{65,192},{96,96},{97,224},{... | collective-permute-start | bytes 442376 | tf_op jit(solution)/shard_map/ppermute | solution.py:82
  21.5 6.8 %collective-permute-start.1 = (bf16[2,32,1152]{2,1,0:T(8,128)(2,1)S(1)}, bf16[2,32,1152]{2,1,0:T(8,128)(2,1)S(1)}, u32[]{:S(2)}, u32[]{:S(2)}) collective-permute-start(bf16[2,32,1152]{2,1,0:T(8,128)(2,1)S(1)} %get-tuple-element.36), channel_id=1, source_target_pairs={{0,32},{1,160},{32,64},{33,192},{64,96},{65,224},{96,0},{97,128},{... | collective-permute-start | bytes 442376 | tf_op jit(solution)/shard_map/ppermute | solution.py:82
  21.6 11.7 %collective-permute-start.2 = (bf16[2,32,1152]{2,1,0:T(8,128)(2,1)S(1)}, bf16[2,32,1152]{2,1,0:T(8,128)(2,1)S(1)}, u32[]{:S(2)}, u32[]{:S(2)}) collective-permute-start(bf16[2,32,1152]{2,1,0:T(8,128)(2,1)S(1)} %get-tuple-element.35), channel_id=1, source_target_pairs={{0,64},{1,192},{32,96},{33,224},{64,0},{65,128},{96,32},{97,160},{... | collective-permute-start | bytes 442376 | tf_op jit(solution)/shard_map/ppermute | solution.py:82
  25.9 9.0 %collective-permute-start.3 = (bf16[2,32,1152]{2,1,0:T(8,128)(2,1)S(1)}, bf16[2,32,1152]{2,1,0:T(8,128)(2,1)S(1)}, u32[]{:S(2)}, u32[]{:S(2)}) collective-permute-start(bf16[2,32,1152]{2,1,0:T(8,128)(2,1)S(1)} %get-tuple-element.34), channel_id=1, source_target_pairs={{0,96},{1,224},{32,0},{33,128},{64,32},{65,160},{96,64},{97,192},{... | collective-permute-start | bytes 442376 | tf_op jit(solution)/shard_map/ppermute | solution.py:82
  35.4 12.0 %collective-permute-start.4 = (bf16[8,32,1152]{2,1,0:T(8,128)(2,1)S(1)}, bf16[8,32,1152]{2,1,0:T(8,128)(2,1)S(1)}, u32[]{:S(2)}, u32[]{:S(2)}) collective-permute-start(bf16[8,32,1152]{2,1,0:T(8,128)(2,1)S(1)} %shard_map.96.mine), channel_id=1, source_target_pairs={{0,1},{1,0},{2,3},{3,2},{4,5},{5,4},{6,7},{7,6},{8,9},{9,8},{10,11... | collective-permute-start | bytes 1769480 | tf_op jit(solution)/shard_map/ppermute | solution.py:69
  35.5 18.4 %all-to-all-start.1 = ((bf16[16,32,640]{2,1,0:T(8,128)(2,1)}), bf16[16,32,640]{2,1,0:T(8,128)(2,1)S(1)}, u32[]{:S(2)}, u32[]{:S(2)}) async-start(bf16[16,32,640]{2,1,0:T(8,128)(2,1)} %shard_map.95.after), calls=%async_computation.1 | async-start | bytes 1310720 | tf_op jit(solution)/shard_map/all_to_all | solution.py:61
  42.5 4.9 %copy-start.1 = (bf16[48,30,1152]{2,0,1:T(8,128)(2,1)S(1)}, bf16[48,30,1152]{2,0,1:T(8,128)(2,1)}, u32[]{:S(2)}) copy-start(bf16[48,30,1152]{2,0,1:T(8,128)(2,1)} %param.12) | copy-start | bytes 9953284
  46.4 1.0 copy-start.2
  48.9 22.9 %copy-start.5 = (f32[48,16]{1,0:T(8,128)}, f32[48,16]{1,0:T(8,128)S(1)}, u32[]{:S(2)}) copy-start(f32[48,16]{1,0:T(8,128)S(1)} %shard_map.97.after.coupling) | copy-start | bytes 9220
  54.0 1.3 %copy-start.3 = (f32[4,2,32,1152]{3,2,1,0:T(8,128)S(1)}, f32[4,2,32,1152]{3,2,1,0:T(8,128)}, u32[]{:S(2)}) copy-start(f32[4,2,32,1152]{3,2,1,0:T(8,128)} %copy-done.2) | copy-start | bytes 3538948
  55.9 0.8 copy-start.4
  56.8 3.6 %collective-permute-start.11 = (bf16[4,32,1152]{2,1,0:T(8,128)(2,1)S(1)}, bf16[4,32,1152]{2,1,0:T(8,128)(2,1)S(1)}, u32[]{:S(2)}, u32[]{:S(2)}) collective-permute-start(bf16[4,32,1152]{2,1,0:T(8,128)(2,1)S(1)} %get-tuple-element.21), channel_id=1, source_target_pairs={{0,1},{1,0},{2,3},{3,2},{4,5},{5,4},{6,7},{7,6},{8,9},{9,8},{10,11... | collective-permute-start | bytes 884744 | tf_op jit(solution)/shard_map/ppermute | solution.py:69
  61.1 26.1 %all-to-all-start.2 = ((bf16[8,32,1152]{2,1,0:T(8,128)(2,1)}), bf16[8,32,1152]{2,1,0:T(8,128)(2,1)S(1)}, u32[]{:S(2)}, u32[]{:S(2)}) async-start(bf16[8,32,1152]{2,1,0:T(8,128)(2,1)} %constant_dynamic-update-slice_fusion), calls=%async_computation.2 | async-start | bytes 1179648 | tf_op jit(solution)/shard_map/all_to_all | solution.py:61
  67.9 1.9 %copy-start = (bf16[48,30,1152]{2,0,1:T(8,128)(2,1)S(1)}, bf16[48,30,1152]{2,0,1:T(8,128)(2,1)}, u32[]{:S(2)}) copy-start(bf16[48,30,1152]{2,0,1:T(8,128)(2,1)} %param.11) | copy-start | bytes 9953284
  69.8 5.2 %copy-start.8 = (bf16[96,96]{1,0:T(8,128)(2,1)S(1)}, bf16[96,96]{1,0:T(8,128)(2,1)}, u32[]{:S(2)}) copy-start(bf16[96,96]{1,0:T(8,128)(2,1)} %fock.5) | copy-start | bytes 55300
  71.8 2.5 %collective-permute-start.6 = (bf16[8,32,1152]{2,1,0:T(8,128)(2,1)S(1)}, bf16[8,32,1152]{2,1,0:T(8,128)(2,1)S(1)}, u32[]{:S(2)}, u32[]{:S(2)}) collective-permute-start(bf16[8,32,1152]{2,1,0:T(8,128)(2,1)S(1)} %get-tuple-element.19), channel_id=1, source_target_pairs={{0,1},{1,0},{2,3},{3,2},{4,5},{5,4},{6,7},{7,6},{8,9},{9,8},{10,11... | collective-permute-start | bytes 1769480 | tf_op jit(solution)/shard_map/ppermute | solution.py:69
  74.3 36.0 %copy-start.10 = (s32[16]{0:T(128)S(1)}, s32[16]{0:T(128)}, u32[]{:S(2)}) copy-start(s32[16]{0:T(128)} %conv.3) | copy-start | bytes 196
  75.0 0.7 copy-start.6
  78.1 0.6 copy-start.12
  89.7 28.4 %copy-start.13 = (f32[2,96]{1,0:T(2,128)S(1)}, f32[2,96]{1,0:T(2,128)}, u32[]{:S(2)}) copy-start(f32[2,96]{1,0:T(2,128)} %copy-done.12) | copy-start | bytes 2308
  89.7 28.4 %copy-start.15 = (f32[2,16]{1,0:T(2,128)S(1)}, f32[2,16]{1,0:T(2,128)}, u32[]{:S(2)}) copy-start(f32[2,16]{1,0:T(2,128)} %copy-done.14) | copy-start | bytes 388
  89.7 16.6 %all-to-all-start.3 = ((f32[16,1,256]{2,1,0:T(1,128)}), f32[16,1,256]{2,1,0:T(1,128)S(1)}, u32[]{:S(2)}, u32[]{:S(2)}) async-start(f32[16,1,256]{2,1,0:T(1,128)} %bitcast.13), calls=%async_computation.3 | async-start | bytes 32768 | tf_op jit(solution)/shard_map/all_to_all | solution.py:61
  93.7 16.7 %collective-permute-start.7 = (bf16[2,32,1152]{2,1,0:T(8,128)(2,1)S(1)}, bf16[2,32,1152]{2,1,0:T(8,128)(2,1)S(1)}, u32[]{:S(2)}, u32[]{:S(2)}) collective-permute-start(bf16[2,32,1152]{2,1,0:T(8,128)(2,1)S(1)} %get-tuple-element.33), channel_id=1, source_target_pairs={{0,0},{128,1},{32,32},{160,33},{64,64},{192,65},{96,96},{224,97},{... | collective-permute-start | bytes 442376 | tf_op jit(solution)/shard_map/ppermute | solution.py:82
  101.2 11.7 %collective-permute-start.8 = (bf16[2,32,1152]{2,1,0:T(8,128)(2,1)S(1)}, bf16[2,32,1152]{2,1,0:T(8,128)(2,1)S(1)}, u32[]{:S(2)}, u32[]{:S(2)}) collective-permute-start(bf16[2,32,1152]{2,1,0:T(8,128)(2,1)S(1)} %get-tuple-element.32), channel_id=1, source_target_pairs={{32,0},{160,1},{64,32},{192,33},{96,64},{224,65},{0,96},{128,97},{... | collective-permute-start | bytes 442376 | tf_op jit(solution)/shard_map/ppermute | solution.py:82
  101.5 12.1 %collective-permute-start.9 = (bf16[2,32,1152]{2,1,0:T(8,128)(2,1)S(1)}, bf16[2,32,1152]{2,1,0:T(8,128)(2,1)S(1)}, u32[]{:S(2)}, u32[]{:S(2)}) collective-permute-start(bf16[2,32,1152]{2,1,0:T(8,128)(2,1)S(1)} %get-tuple-element.31), channel_id=1, source_target_pairs={{64,0},{192,1},{96,32},{224,33},{0,64},{128,65},{32,96},{160,97},{... | collective-permute-start | bytes 442376 | tf_op jit(solution)/shard_map/ppermute | solution.py:82
  105.1 10.9 %collective-permute-start.10 = (bf16[2,32,1152]{2,1,0:T(8,128)(2,1)S(1)}, bf16[2,32,1152]{2,1,0:T(8,128)(2,1)S(1)}, u32[]{:S(2)}, u32[]{:S(2)}) collective-permute-start(bf16[2,32,1152]{2,1,0:T(8,128)(2,1)S(1)} %get-tuple-element.30), channel_id=1, source_target_pairs={{96,0},{224,1},{0,32},{128,33},{32,64},{160,65},{64,96},{192,97},{... | collective-permute-start | bytes 442376 | tf_op jit(solution)/shard_map/ppermute | solution.py:82
  106.9 11.2 %all-to-all-start.4 = ((f32[16,1,256]{2,1,0:T(1,128)}), f32[16,1,256]{2,1,0:T(1,128)S(1)}, u32[]{:S(2)}, u32[]{:S(2)}) async-start(f32[16,1,256]{2,1,0:T(1,128)} %shard_map.105), calls=%async_computation.4 | async-start | bytes 32768 | tf_op jit(solution)/shard_map/all_to_all | solution.py:61
  (1 other events, 0.6 us)

commit v4 on v2

--- a/solution.py
+++ b/solution.py
@@ -159,16 +159,15 @@
                 rhs = jnp.concatenate([rolled[0, :, lo:hi], rolled[1, :, lo:hi]], axis=1)
                 y = dot(left[rows * tile : rows * (tile + 2), :], rhs)
                 v = jnp.where(lane < 96 - 32 * tile, y[0:rows, :], y[rows:, :])
-                for c in range(2):
-                    w = v[:, 128 * c : 128 * (c + 1)] + second[rows * c : rows * (c + 1), lo:hi]
-                    for g in range(12):
-                        q, u = divmod(g, 3)
-                        oo[
-                            q,
-                            p,
-                            16 * b + 8 * c : 16 * b + 8 * (c + 1),
-                            GRP * u + lo : GRP * u + hi,
-                        ] = w[8 * g : 8 * (g + 1), :]
+                w = [
+                    v[:, 128 * c : 128 * (c + 1)] + second[rows * c : rows * (c + 1), lo:hi]
+                    for c in range(2)
+                ]
+                for g in range(12):
+                    q, u = divmod(g, 3)
+                    part = jnp.concatenate([y[8 * g : 8 * (g + 1), :] for y in w], axis=0)
+                    at = GRP * u + lo
+                    oo[q, p, 16 * b : 16 * (b + 1), at : at + 128] = part.astype(BF)
 
 
 def mm_kernel(fock, x, out):
@@ -238,16 +237,15 @@
     out[...] = dot(total, right, HI)
 
 
-def x_kernel(ids, after, vv, oo, x, keep, send):
+def x_kernel(ids, vv, oo, x, keep, send):
     core = ids[1]
-    del after
 
     def work(own):
         for p in range(2):
             out = keep if p == own else send
             for q in range(4):
                 for g, a, b, lo, hi in tiles_of(36 * p + 9 * q, 9):
-                    v = vv[g, :, a:b].astype(F32) - oo[q, p, :, lo:hi]
+                    v = vv[g, :, a:b].astype(F32) - oo[q, p, :, lo:hi].astype(F32)
                     x[q, p, :, lo:hi] = v
                     out[q, :, lo:hi] = v.astype(BF)
                 out[q, VL:VP, :] = jnp.zeros((VP - VL, BLK), BF)
@@ -361,7 +359,7 @@
     blocks = z_steps(zb)
     oo = call(
         oo_kernel,
-        shape(chunks, F32),
+        shape(chunks, BF),
         [SMEM, VMEM, VMEM, VMEM],
         [
             VMEM((384, 768), BF),
@@ -394,8 +392,8 @@
 
     half = (4, VP, BLK)
     x, keep, send = call(
-        x_kernel, (shape(chunks, F32), shape(half, BF), shape(half, BF)), [SMEM, pl.ANY, VMEM, VMEM]
-    )(ids, coupling, vv, oo)
+        x_kernel, (shape(chunks, F32), shape(half, BF), shape(half, BF)), [SMEM, VMEM, VMEM]
+    )(ids, vv, oo)
     recv = other_core(send)
     x_root = call(merge_kernel, shape(roots, BF), [SMEM, VMEM, VMEM])(
         ids, keep, recv

time: 120 us -> 119 us (level)
    all_to_all x5, waiting for transfers between devices: 15 us -> 21.9 us  [exchange(): return lax.all_to_all(x, axes, split_axis=0, concat_axis=0, tiled=True)]
    ppermute x8, waiting for transfers between devices: 12.5 us -> 7.85 us  [z_steps(): out.append(lax.ppermute(x[t], ROOT_OCC, pairs))]
    ppermute x4, starting transfers between devices: 4.5 us -> 1.79 us  [other_core(): return lax.ppermute(x, 'occ', [(0, 1), (1, 0)])]
    ppermute x4, waiting for transfers between devices: 2.84 us -> 0.25 us  [other_core(): return lax.ppermute(x, 'occ', [(0, 1), (1, 0)])]
    ppermute x8, starting transfers between devices: 25.7 us -> 27.9 us  [z_steps(): out.append(lax.ppermute(x[t], ROOT_OCC, pairs))]
    unnamed x28 -> x20, local copies, waits for them, and re-layouts: 8.07 us -> 6.74 us
  transfers between devices with their start and end apart: 17 -> 17, of which waited for: 10 -> 7; matrix products, arithmetic and copies ran while one was open for 1% -> 2% of each run, Pallas kernels for 11% -> 14%
where the time goes in v4:
time: 119 us; the launch traced here: 118 us
  starting transfers between devices  57.9 us (49%)
  waiting for transfers between devices  30 us (25%)
  Pallas kernels  21.8 us (18%)
  local copies, waits for them, and re-layouts  7.6 us (6%)
    all_to_all x5, starting transfers between devices, exchange(): return lax.all_to_all(x, axes, split_axis=0, concat_axis=0, tiled=True)  28.2 us
    ppermute x8, starting transfers between devices, z_steps(): out.append(lax.ppermute(x[t], ROOT_OCC, pairs))  27.9 us
    all_to_all x5, waiting for transfers between devices, exchange(): return lax.all_to_all(x, axes, split_axis=0, concat_axis=0, tiled=True)  21.9 us
    ppermute x8, waiting for transfers between devices, z_steps(): out.append(lax.ppermute(x[t], ROOT_OCC, pairs))  7.85 us
    unnamed x20, local copies, waits for them, and re-layouts  6.74 us
    pallas_call x1, Pallas kernels, local(): call(oo_kernel, shape(chunks, BF), [SMEM, VMEM, VMEM, VMEM], [VMEM((384,...  3.19 us
    pallas_call x1, Pallas kernels, local(): call(s_kernel, shape((Z, 2, 1, 256), F32), [SMEM, VMEM, VMEM, VMEM, VMEM])  2.46 us
  transfers between devices with their start and end apart: 17, of which 7 were waited for; matrix products, arithmetic and copies ran while one was open for 2% of the time, Pallas kernels for 14%

profile of v4, /device:TPU:1, one launch (start us, length us, event | category | flops | bytes accessed | tf_op | source)
XLA Modules:
  0.0 118.3 jit_solution(4617931890109532397)
XLA Ops:
  0.6 1.1 copy.10.doubles
  2.5 1.5 %shard_map.94 = (bf16[4,2,32,1152]{3,2,1,0:T(8,128)(2,1)S(1)}, bf16[16,32,640]{2,1,0:T(8,128)(2,1)}) custom-call(s32[2]{0:T(128)S(1)} %pad_add_fusion.ids, bf16[2,30,4608]{2,1,0:T(8,128)(2,1)S(1)} %copy.10.doubles, bf16[2,96]{1,0:T(2,128)(2,1)S(1)} %copy-done.2), custom_call_target="tpu_custom_call" | custom-call | flops 16777216 | bytes 1048576 | tf_op jit(solution)/shard_map/pallas_call | solution.py:354
  4.0 7.6 %all-to-all-start = ((bf16[16,32,640]{2,1,0:T(8,128)(2,1)}), bf16[16,32,640]{2,1,0:T(8,128)(2,1)S(1)}, u32[]{:S(2)}, u32[]{:S(2)}) async-start(bf16[16,32,640]{2,1,0:T(8,128)(2,1)} %get-tuple-element.14), calls=%async_computation | async-start | bytes 1310720 | tf_op jit(solution)/shard_map/all_to_all | solution.py:61
  11.6 1.0 collective-permute-start
  12.7 10.5 %all-to-all-done.x = bf16[16,32,640]{2,1,0:T(8,128)(2,1)S(1)} async-done(((bf16[16,32,640]{2,1,0:T(8,128)(2,1)}), bf16[16,32,640]{2,1,0:T(8,128)(2,1)S(1)}, u32[]{:S(2)}, u32[]{:S(2)}) %all-to-all-start) | async-done | bytes 655392 | tf_op jit(solution)/shard_map/all_to_all | solution.py:61
  23.2 1.0 copy-done.4
  24.2 2.1 %shard_map.95.after = bf16[16,32,640]{2,1,0:T(8,128)(2,1)} custom-call(bf16[480,480]{1,0:T(8,128)(2,1)S(1)} %copy-done.4, bf16[16,32,640]{2,1,0:T(8,128)(2,1)S(1)} %all-to-all-done.x), custom_call_target="tpu_custom_call" | custom-call | flops 536870912 | bytes 1048576 | tf_op jit(solution)/shard_map/pallas_call | solution.py:372
  26.3 3.6 %all-to-all-start.1 = ((bf16[16,32,640]{2,1,0:T(8,128)(2,1)}), bf16[16,32,640]{2,1,0:T(8,128)(2,1)S(1)}, u32[]{:S(2)}, u32[]{:S(2)}) async-start(bf16[16,32,640]{2,1,0:T(8,128)(2,1)} %shard_map.95.after), calls=%async_computation.1 | async-start | bytes 1310720 | tf_op jit(solution)/shard_map/all_to_all | solution.py:61
  30.0 0.8 slice_bitcast_fusion.4
  30.8 10.9 %collective-permute-start.1 = (bf16[2,32,1152]{2,1,0:T(8,128)(2,1)}, bf16[2,32,1152]{2,1,0:T(8,128)(2,1)S(1)}, u32[]{:S(2)}, u32[]{:S(2)}) collective-permute-start(bf16[2,32,1152]{2,1,0:T(8,128)(2,1)} %get-tuple-element.35), channel_id=1, source_target_pairs={{0,0},{1,128},{32,32},{33,160},{64,64},{65,192},{96,96},{97,224},{... | collective-permute-start | bytes 442376 | tf_op jit(solution)/shard_map/ppermute | solution.py:82
  41.8 4.3 %collective-permute-start.3 = (bf16[2,32,1152]{2,1,0:T(8,128)(2,1)}, bf16[2,32,1152]{2,1,0:T(8,128)(2,1)}, u32[]{:S(2)}, u32[]{:S(2)}) collective-permute-start(bf16[2,32,1152]{2,1,0:T(8,128)(2,1)} %get-tuple-element.33), channel_id=1, source_target_pairs={{0,64},{1,192},{32,96},{33,224},{64,0},{65,128},{96,32},{97,160},{... | collective-permute-start | bytes 442376 | tf_op jit(solution)/shard_map/ppermute | solution.py:82
  46.1 3.2 %shard_map.96.oo = bf16[4,2,32,1152]{3,2,1,0:T(8,128)(2,1)S(1)} custom-call(s32[2]{0:T(128)S(1)} %pad_add_fusion.ids, bf16[4,2,32,1152]{3,2,1,0:T(8,128)(2,1)S(1)} %get-tuple-element.15.zb, bf16[4,2,32,1152]{3,2,1,0:T(8,128)(2,1)S(1)} %collective-permute-done.zo, bf16[96,96]{1,0:T(8,128)(2,1)S(1)} %copy-done.5), custom_call_target="tpu_custom_call" | custom-call | flops 2147483648 | bytes 1048576 | tf_op jit(solution)/shard_map/pallas_call | solution.py:360
  50.1 3.8 %collective-permute-done.3.refs_2_ = bf16[2,32,1152]{2,1,0:T(8,128)(2,1)} collective-permute-done((bf16[2,32,1152]{2,1,0:T(8,128)(2,1)}, bf16[2,32,1152]{2,1,0:T(8,128)(2,1)}, u32[]{:S(2)}, u32[]{:S(2)}) %collective-permute-start.3) | collective-permute-done | bytes 147488 | tf_op jit(solution)/shard_map/ppermute | solution.py:82
  54.0 1.5 %collective-permute-done.4.refs_3_ = bf16[2,32,1152]{2,1,0:T(8,128)(2,1)} collective-permute-done((bf16[2,32,1152]{2,1,0:T(8,128)(2,1)}, bf16[2,32,1152]{2,1,0:T(8,128)(2,1)}, u32[]{:S(2)}, u32[]{:S(2)}) %collective-permute-start.4) | collective-permute-done | bytes 147488 | tf_op jit(solution)/shard_map/ppermute | solution.py:82
  55.5 1.1 shard_map.98.mine
  56.7 1.4 %shard_map.102 = bf16[8,32,1152]{2,1,0:T(8,128)(2,1)} custom-call(s32[2]{0:T(128)S(1)} %pad_add_fusion.ids, bf16[4,32,1152]{2,1,0:T(8,128)(2,1)S(1)} %get-tuple-element.19.keep, bf16[4,32,1152]{2,1,0:T(8,128)(2,1)S(1)} %collective-permute-done.11.recv), custom_call_target="tpu_custom_call" | custom-call | flops 16777216 | bytes 1048576 | tf_op jit(solution)/shard_map/pallas_call | solution.py:398
  58.1 6.2 %all-to-all-start.2 = ((bf16[8,32,1152]{2,1,0:T(8,128)(2,1)}), bf16[8,32,1152]{2,1,0:T(8,128)(2,1)S(1)}, u32[]{:S(2)}, u32[]{:S(2)}) async-start(bf16[8,32,1152]{2,1,0:T(8,128)(2,1)} %shard_map.102), calls=%async_computation.2 | async-start | bytes 1179648 | tf_op jit(solution)/shard_map/all_to_all | solution.py:61
  64.4 1.9 %copy-done = bf16[48,30,1152]{2,0,1:T(8,128)(2,1)S(1)} copy-done((bf16[48,30,1152]{2,0,1:T(8,128)(2,1)S(1)}, bf16[48,30,1152]{2,0,1:T(8,128)(2,1)}, u32[]{:S(2)}) %copy-start) | copy-done | bytes 3317784
  66.3 2.0 %shard_map.99 = (bf16[8,32,1152]{2,1,0:T(8,128)(2,1)S(1)}, bf16[8,32,1152]{2,1,0:T(8,128)(2,1)S(1)}) custom-call(s32[2]{0:T(128)S(1)} %pad_add_fusion.ids, bf16[8,32,1152]{2,1,0:T(8,128)(2,1)S(1)} %shard_map.98.mine, bf16[8,32,1152]{2,1,0:T(8,128)(2,1)S(1)} %collective-permute-done.5.theirs, bf16[30,48,1152]{2,1,0:T(8,128)(2,1)S(1)} %bitcast.23), custom_call_target="tpu_custom_call" | custom-call | flops 1073741824 | bytes 1048576 | tf_op jit(solution)/shard_map/pallas_call | solution.py:379
  68.9 1.5 %shard_map.103.coupling = f32[48,16]{1,0:T(8,128)S(1)} custom-call(bf16[8,32,1152]{2,1,0:T(8,128)(2,1)S(1)} %shard_map.98.mine, bf16[8,32,1152]{2,1,0:T(8,128)(2,1)S(1)} %collective-permute-done.5.theirs, bf16[30,48,1152]{2,1,0:T(8,128)(2,1)S(1)} %bitcast.24), custom_call_target="tpu_custom_call" | custom-call | flops 1073741824 | bytes 1048576 | tf_op jit(solution)/shard_map/pallas_call | solution.py:385
  71.3 2.3 %shard_map.104 = (f32[16,128]{1,0:T(8,128)S(1)}, f32[16,128]{1,0:T(8,128)S(1)}) custom-call(s32[2]{0:T(128)S(1)} %pad_add_fusion.ids, bf16[8,32,1152]{2,1,0:T(8,128)(2,1)S(1)} %shard_map.98.mine, bf16[8,32,1152]{2,1,0:T(8,128)(2,1)S(1)} %collective-permute-done.5.theirs, bf16[4,2,32,1152]{3,2,1,0:T(8,128)(2,1)S(1)} %shard_map.100.ov, ...), custom_call_target="tpu_custom_call" | custom-call | flops 16777216 | bytes 1048576 | tf_op jit(solution)/shard_map/pallas_call | solution.py:402
  74.2 9.6 %all-to-all-done.2.x = bf16[8,32,1152]{2,1,0:T(8,128)(2,1)S(1)} async-done(((bf16[8,32,1152]{2,1,0:T(8,128)(2,1)}), bf16[8,32,1152]{2,1,0:T(8,128)(2,1)S(1)}, u32[]{:S(2)}, u32[]{:S(2)}) %all-to-all-start.2) | async-done | bytes 589856 | tf_op jit(solution)/shard_map/all_to_all | solution.py:61
  83.8 2.5 %shard_map.105 = f32[8,2,1,256]{3,2,1,0:T(1,128)} custom-call(s32[2]{0:T(128)S(1)} %pad_add_fusion.ids, bf16[8,32,1152]{2,1,0:T(8,128)(2,1)S(1)} %shard_map.98.mine, bf16[8,32,1152]{2,1,0:T(8,128)(2,1)S(1)} %collective-permute-done.5.theirs, bf16[8,32,1152]{2,1,0:T(8,128)(2,1)S(1)} %all-to-all-done.2.x, f32[16,128]{1,0:T(8,128)S(1)} %get-tuple-element.21.rows), custom_call_target="tpu_custom_call" | custom-call | flops 16777216 | bytes 1048576 | tf_op jit(solution)/shard_map/pallas_call | solution.py:408
  86.3 3.9 %all-to-all-start.3 = ((f32[16,1,256]{2,1,0:T(1,128)}), f32[16,1,256]{2,1,0:T(1,128)S(1)}, u32[]{:S(2)}, u32[]{:S(2)}) async-start(f32[16,1,256]{2,1,0:T(1,128)} %bitcast.13), calls=%async_computation.3 | async-start | bytes 32768 | tf_op jit(solution)/shard_map/all_to_all | solution.py:61
  90.2 7.5 %collective-permute-start.7 = (bf16[2,32,1152]{2,1,0:T(8,128)(2,1)S(1)}, bf16[2,32,1152]{2,1,0:T(8,128)(2,1)S(1)}, u32[]{:S(2)}, u32[]{:S(2)}) collective-permute-start(bf16[2,32,1152]{2,1,0:T(8,128)(2,1)S(1)} %get-tuple-element.31), channel_id=1, source_target_pairs={{0,0},{128,1},{32,32},{160,33},{64,64},{192,65},{96,96},{224,97},{... | collective-permute-start | bytes 442376 | tf_op jit(solution)/shard_map/ppermute | solution.py:82
  98.1 3.6 %collective-permute-start.9 = (bf16[2,32,1152]{2,1,0:T(8,128)(2,1)S(1)}, bf16[2,32,1152]{2,1,0:T(8,128)(2,1)S(1)}, u32[]{:S(2)}, u32[]{:S(2)}) collective-permute-start(bf16[2,32,1152]{2,1,0:T(8,128)(2,1)S(1)} %get-tuple-element.29), channel_id=1, source_target_pairs={{64,0},{192,1},{96,32},{224,33},{0,64},{128,65},{32,96},{160,97},{... | collective-permute-start | bytes 442376 | tf_op jit(solution)/shard_map/ppermute | solution.py:82
  101.7 1.1 collective-permute-start.10
  103.4 6.9 %all-to-all-start.4 = ((f32[16,1,256]{2,1,0:T(1,128)}), f32[16,1,256]{2,1,0:T(1,128)S(1)}, u32[]{:S(2)}, u32[]{:S(2)}) async-start(f32[16,1,256]{2,1,0:T(1,128)} %shard_map.106), calls=%async_computation.4 | async-start | bytes 32768 | tf_op jit(solution)/shard_map/all_to_all | solution.py:61
  110.4 2.5 %collective-permute-done.10.refs_3_ = bf16[2,32,1152]{2,1,0:T(8,128)(2,1)S(1)} collective-permute-done((bf16[2,32,1152]{2,1,0:T(8,128)(2,1)S(1)}, bf16[2,32,1152]{2,1,0:T(8,128)(2,1)S(1)}, u32[]{:S(2)}, u32[]{:S(2)}) %collective-permute-start.10) | collective-permute-done | bytes 147488 | tf_op jit(solution)/shard_map/ppermute | solution.py:82
  113.6 1.4 %copy.11 = bf16[2,30,4608]{2,0,1:T(2,128)(2,1)} copy(bf16[2,30,4608]{2,1,0:T(8,128)(2,1)S(1)} %shard_map.101) | data formatting | bytes 1105920
  114.9 1.8 %all-to-all-done.4.x = f32[16,1,256]{2,1,0:T(1,128)S(1)} async-done(((f32[16,1,256]{2,1,0:T(1,128)}), f32[16,1,256]{2,1,0:T(1,128)S(1)}, u32[]{:S(2)}, u32[]{:S(2)}) %all-to-all-start.4) | async-done | bytes 16416 | tf_op jit(solution)/shard_map/all_to_all | solution.py:61
  116.8 1.5 %shard_map.107 = (f32[2,96]{1,0:T(2,128)}, f32[2,16]{1,0:T(2,128)}) custom-call(s32[2]{0:T(128)S(1)} %pad_add_fusion.ids, s32[16]{0:T(128)S(1)} %copy-done.3, f32[1,16]{1,0:T(1,128)S(1)} %convert_bitcast_fusion.active, f32[16,1,256]{2,1,0:T(1,128)S(1)} %all-to-all-done.4.x, f32[16,128]{1,0:T(8,128)S(1)} %copy-done.8, bf16[96,96]{1,0:T(8,128)(2,1)S(1)} %copy-done.6), custom_call_target="tpu_custom_call" | custom-call | flops 16777216 | bytes 1048576 | tf_op jit(solution)/shard_map/pallas_call | solution.py:414
  (40 shorter events, 5.6 us)
Async XLA Ops:
  0.6 45.5 %copy-start.5 = (bf16[96,96]{1,0:T(8,128)(2,1)S(1)}, bf16[96,96]{1,0:T(8,128)(2,1)}, u32[]{:S(2)}) copy-start(bf16[96,96]{1,0:T(8,128)(2,1)} %fock.5) | copy-start | bytes 55300
  1.8 0.7 copy-start.2
  4.0 19.2 %all-to-all-start = ((bf16[16,32,640]{2,1,0:T(8,128)(2,1)}), bf16[16,32,640]{2,1,0:T(8,128)(2,1)S(1)}, u32[]{:S(2)}, u32[]{:S(2)}) async-start(bf16[16,32,640]{2,1,0:T(8,128)(2,1)} %get-tuple-element.14), calls=%async_computation | async-start | bytes 1310720 | tf_op jit(solution)/shard_map/all_to_all | solution.py:61
  11.6 34.5 %collective-permute-start = (bf16[4,2,32,1152]{3,2,1,0:T(8,128)(2,1)S(1)}, bf16[4,2,32,1152]{3,2,1,0:T(8,128)(2,1)S(1)}, u32[]{:S(2)}, u32[]{:S(2)}) collective-permute-start(bf16[4,2,32,1152]{3,2,1,0:T(8,128)(2,1)S(1)} %get-tuple-element.15.zb), channel_id=1, source_target_pairs={{0,1},{1,0},{2,3},{3,2},{4,5},{5,4},{6,7},{7,6},{8,9},{9,8},{10,11... | collective-permute-start | bytes 1769480 | tf_op jit(solution)/shard_map/ppermute | solution.py:69
  23.2 1.0 copy-start.4
  26.3 23.0 %all-to-all-start.1 = ((bf16[16,32,640]{2,1,0:T(8,128)(2,1)}), bf16[16,32,640]{2,1,0:T(8,128)(2,1)S(1)}, u32[]{:S(2)}, u32[]{:S(2)}) async-start(bf16[16,32,640]{2,1,0:T(8,128)(2,1)} %shard_map.95.after), calls=%async_computation.1 | async-start | bytes 1310720 | tf_op jit(solution)/shard_map/all_to_all | solution.py:61
  30.8 19.3 %collective-permute-start.1 = (bf16[2,32,1152]{2,1,0:T(8,128)(2,1)}, bf16[2,32,1152]{2,1,0:T(8,128)(2,1)S(1)}, u32[]{:S(2)}, u32[]{:S(2)}) collective-permute-start(bf16[2,32,1152]{2,1,0:T(8,128)(2,1)} %get-tuple-element.35), channel_id=1, source_target_pairs={{0,0},{1,128},{32,32},{33,160},{64,64},{65,192},{96,96},{97,224},{... | collective-permute-start | bytes 442376 | tf_op jit(solution)/shard_map/ppermute | solution.py:82
  41.7 8.4 %collective-permute-start.2 = (bf16[2,32,1152]{2,1,0:T(8,128)(2,1)}, bf16[2,32,1152]{2,1,0:T(8,128)(2,1)}, u32[]{:S(2)}, u32[]{:S(2)}) collective-permute-start(bf16[2,32,1152]{2,1,0:T(8,128)(2,1)} %get-tuple-element.34), channel_id=1, source_target_pairs={{0,32},{1,160},{32,64},{33,192},{64,96},{65,224},{96,0},{97,128},{... | collective-permute-start | bytes 442376 | tf_op jit(solution)/shard_map/ppermute | solution.py:82
  41.8 12.2 %collective-permute-start.3 = (bf16[2,32,1152]{2,1,0:T(8,128)(2,1)}, bf16[2,32,1152]{2,1,0:T(8,128)(2,1)}, u32[]{:S(2)}, u32[]{:S(2)}) collective-permute-start(bf16[2,32,1152]{2,1,0:T(8,128)(2,1)} %get-tuple-element.33), channel_id=1, source_target_pairs={{0,64},{1,192},{32,96},{33,224},{64,0},{65,128},{96,32},{97,160},{... | collective-permute-start | bytes 442376 | tf_op jit(solution)/shard_map/ppermute | solution.py:82
  46.1 9.4 %collective-permute-start.4 = (bf16[2,32,1152]{2,1,0:T(8,128)(2,1)}, bf16[2,32,1152]{2,1,0:T(8,128)(2,1)}, u32[]{:S(2)}, u32[]{:S(2)}) collective-permute-start(bf16[2,32,1152]{2,1,0:T(8,128)(2,1)} %get-tuple-element.32), channel_id=1, source_target_pairs={{0,96},{1,224},{32,0},{33,128},{64,32},{65,160},{96,64},{97,192},{... | collective-permute-start | bytes 442376 | tf_op jit(solution)/shard_map/ppermute | solution.py:82
  50.0 6.7 %collective-permute-start.11 = (bf16[4,32,1152]{2,1,0:T(8,128)(2,1)S(1)}, bf16[4,32,1152]{2,1,0:T(8,128)(2,1)S(1)}, u32[]{:S(2)}, u32[]{:S(2)}) collective-permute-start(bf16[4,32,1152]{2,1,0:T(8,128)(2,1)S(1)} %get-tuple-element.20), channel_id=1, source_target_pairs={{0,1},{1,0},{2,3},{3,2},{4,5},{5,4},{6,7},{7,6},{8,9},{9,8},{10,11... | collective-permute-start | bytes 884744 | tf_op jit(solution)/shard_map/ppermute | solution.py:69
  56.6 7.7 %collective-permute-start.5 = (bf16[8,32,1152]{2,1,0:T(8,128)(2,1)S(1)}, bf16[8,32,1152]{2,1,0:T(8,128)(2,1)S(1)}, u32[]{:S(2)}, u32[]{:S(2)}) collective-permute-start(bf16[8,32,1152]{2,1,0:T(8,128)(2,1)S(1)} %shard_map.98.mine), channel_id=1, source_target_pairs={{0,1},{1,0},{2,3},{3,2},{4,5},{5,4},{6,7},{7,6},{8,9},{9,8},{10,11... | collective-permute-start | bytes 1769480 | tf_op jit(solution)/shard_map/ppermute | solution.py:69
  58.1 25.7 %all-to-all-start.2 = ((bf16[8,32,1152]{2,1,0:T(8,128)(2,1)}), bf16[8,32,1152]{2,1,0:T(8,128)(2,1)S(1)}, u32[]{:S(2)}, u32[]{:S(2)}) async-start(bf16[8,32,1152]{2,1,0:T(8,128)(2,1)} %shard_map.102), calls=%async_computation.2 | async-start | bytes 1179648 | tf_op jit(solution)/shard_map/all_to_all | solution.py:61
  64.4 1.9 %copy-start = (bf16[48,30,1152]{2,0,1:T(8,128)(2,1)S(1)}, bf16[48,30,1152]{2,0,1:T(8,128)(2,1)}, u32[]{:S(2)}) copy-start(bf16[48,30,1152]{2,0,1:T(8,128)(2,1)} %param.11) | copy-start | bytes 9953284
  66.3 2.6 %copy-start.1 = (bf16[48,30,1152]{2,0,1:T(8,128)(2,1)S(1)}, bf16[48,30,1152]{2,0,1:T(8,128)(2,1)}, u32[]{:S(2)}) copy-start(bf16[48,30,1152]{2,0,1:T(8,128)(2,1)} %param.12) | copy-start | bytes 9953284
  68.3 2.3 %collective-permute-start.6 = (bf16[8,32,1152]{2,1,0:T(8,128)(2,1)S(1)}, bf16[8,32,1152]{2,1,0:T(8,128)(2,1)S(1)}, u32[]{:S(2)}, u32[]{:S(2)}) collective-permute-start(bf16[8,32,1152]{2,1,0:T(8,128)(2,1)S(1)} %get-tuple-element.18), channel_id=1, source_target_pairs={{0,1},{1,0},{2,3},{3,2},{4,5},{5,4},{6,7},{7,6},{8,9},{9,8},{10,11... | collective-permute-start | bytes 1769480 | tf_op jit(solution)/shard_map/ppermute | solution.py:69
  70.6 39.7 %copy-start.3 = (s32[16]{0:T(128)S(1)}, s32[16]{0:T(128)}, u32[]{:S(2)}) copy-start(s32[16]{0:T(128)} %conv.3) | copy-start | bytes 196
  73.6 0.6 copy-start.7
  86.3 30.5 %copy-start.6 = (bf16[96,96]{1,0:T(8,128)(2,1)S(1)}, bf16[96,96]{1,0:T(8,128)(2,1)}, u32[]{:S(2)}) copy-start(bf16[96,96]{1,0:T(8,128)(2,1)} %fock.5) | copy-start | bytes 55300
  86.3 30.5 %copy-start.8 = (f32[16,128]{1,0:T(8,128)S(1)}, f32[16,128]{1,0:T(8,128)}, u32[]{:S(2)}) copy-start(f32[16,128]{1,0:T(8,128)} %copy-done.7) | copy-start | bytes 24580
  86.3 16.5 %all-to-all-start.3 = ((f32[16,1,256]{2,1,0:T(1,128)}), f32[16,1,256]{2,1,0:T(1,128)S(1)}, u32[]{:S(2)}, u32[]{:S(2)}) async-start(f32[16,1,256]{2,1,0:T(1,128)} %bitcast.13), calls=%async_computation.3 | async-start | bytes 32768 | tf_op jit(solution)/shard_map/all_to_all | solution.py:61
  90.2 20.1 %collective-permute-start.7 = (bf16[2,32,1152]{2,1,0:T(8,128)(2,1)S(1)}, bf16[2,32,1152]{2,1,0:T(8,128)(2,1)S(1)}, u32[]{:S(2)}, u32[]{:S(2)}) collective-permute-start(bf16[2,32,1152]{2,1,0:T(8,128)(2,1)S(1)} %get-tuple-element.31), channel_id=1, source_target_pairs={{0,0},{128,1},{32,32},{160,33},{64,64},{192,65},{96,96},{224,97},{... | collective-permute-start | bytes 442376 | tf_op jit(solution)/shard_map/ppermute | solution.py:82
  97.7 12.6 %collective-permute-start.8 = (bf16[2,32,1152]{2,1,0:T(8,128)(2,1)S(1)}, bf16[2,32,1152]{2,1,0:T(8,128)(2,1)S(1)}, u32[]{:S(2)}, u32[]{:S(2)}) collective-permute-start(bf16[2,32,1152]{2,1,0:T(8,128)(2,1)S(1)} %get-tuple-element.30), channel_id=1, source_target_pairs={{32,0},{160,1},{64,32},{192,33},{96,64},{224,65},{0,96},{128,97},{... | collective-permute-start | bytes 442376 | tf_op jit(solution)/shard_map/ppermute | solution.py:82
  98.1 12.3 %collective-permute-start.9 = (bf16[2,32,1152]{2,1,0:T(8,128)(2,1)S(1)}, bf16[2,32,1152]{2,1,0:T(8,128)(2,1)S(1)}, u32[]{:S(2)}, u32[]{:S(2)}) collective-permute-start(bf16[2,32,1152]{2,1,0:T(8,128)(2,1)S(1)} %get-tuple-element.29), channel_id=1, source_target_pairs={{64,0},{192,1},{96,32},{224,33},{0,64},{128,65},{32,96},{160,97},{... | collective-permute-start | bytes 442376 | tf_op jit(solution)/shard_map/ppermute | solution.py:82
  101.7 11.2 %collective-permute-start.10 = (bf16[2,32,1152]{2,1,0:T(8,128)(2,1)S(1)}, bf16[2,32,1152]{2,1,0:T(8,128)(2,1)S(1)}, u32[]{:S(2)}, u32[]{:S(2)}) collective-permute-start(bf16[2,32,1152]{2,1,0:T(8,128)(2,1)S(1)} %get-tuple-element.28), channel_id=1, source_target_pairs={{96,0},{224,1},{0,32},{128,33},{32,64},{160,65},{64,96},{192,97},{... | collective-permute-start | bytes 442376 | tf_op jit(solution)/shard_map/ppermute | solution.py:82
  103.4 13.3 %all-to-all-start.4 = ((f32[16,1,256]{2,1,0:T(1,128)}), f32[16,1,256]{2,1,0:T(1,128)S(1)}, u32[]{:S(2)}, u32[]{:S(2)}) async-start(f32[16,1,256]{2,1,0:T(1,128)} %shard_map.106), calls=%async_computation.4 | async-start | bytes 32768 | tf_op jit(solution)/shard_map/all_to_all | solution.py:61
